TPU v7x, 32 devices: a whole 2x2x4 slice. The times are simulated.
32 devices in a mesh: lon: 4 (over y, x), lat: 8 (over z, core).
Axes of the slice: x: 2, y: 2, z: 4, core: 2. Of those that a mesh axis runs over, the one named last changes fastest.
Arguments:
- tracers: float32 [4, 32, 64, 512], P(None, None, 'lat', 'lon'), may hold values from -6 to 6
- winds: float32 [2, 32, 64, 512], P(None, None, 'lat', 'lon'), may hold values from -0.45 to 0.45
- gases: bfloat16 [12, 32, 64, 512], P(None, None, 'lat', 'lon'), may hold values from -6 to 6
- sun_index: int32 [64, 512], P('lat', 'lon'), may hold values from 0 to 63, as said below
- block_slot: int32 [64, 4], P('lat', 'lon'), may hold values from -1 to 7, as said below
- albedo: bfloat16 [64, 512], P('lat', 'lon'), may hold values from 0.049804688 to 0.59765625
- sun_table: float32 [64], replicated, may hold values from 0.05 to 1
- solar: float32 [224], replicated, may hold values from 0.002 to 0.02
- w_first: bfloat16 [16, 64], replicated, may hold values from -1.5 to 1.5
- b_first: float32 [64], replicated, may hold values from -3 to 3
- w_second: bfloat16 [64, 64], replicated, may hold values from -0.75 to 0.75
- b_second: float32 [64], replicated, may hold values from -3 to 3
- w_third: bfloat16 [64, 224], replicated, may hold values from -0.75 to 0.75
- b_third: float32 [224], replicated, may hold values from -2 to 1
Outputs:
- tracers_out: float32 [4, 32, 64, 512], P(None, None, 'lat', 'lon')
- heating: float32 [32, 64, 512], P(None, 'lat', 'lon')
Inputs may be any that keep to these rules, and one draw needn't show every extreme that they name: `block_slot`: each latitude row of one device's slab is a block of 128 columns. For the two devices at equal lat whose lon indices differ by 2, exactly 8 of their 16 blocks have a slot number of 0 or more, and these carry 0 to 7 once each; in every draw some device has all its blocks numbered. `sun_index`: 0 on every column of a block whose block_slot is -1, and 1 or more on every column of the other blocks.
All inputs are finite; a program needn't handle non-finite values.
Results may differ from a plain program's by a relative error of at most 0.0003.
Values may be sent and summed in bfloat16 or wider, within the bound.
No kernel may reach another device: no remote copies, remote signals or barrier semaphores. Data moves between devices by JAX's collectives and lax.ppermute only.
A program may use at most 64 MiB of HBM per device.

v0:
```python
import jax
import jax.numpy as jnp
from jax import lax
from jax.sharding import PartitionSpec as P

PRE_STEPS = 2
POST_STEPS = 2


tau_scale = 0.05
mu_floor = 0.05
heat_scale = 30.0
diffuse_factor = 1.66


def with_halo(cells, sides, width):
    for axis, dim in sides:
        count = lax.axis_size(axis)
        head = lax.slice_in_dim(cells, 0, width, axis=dim)
        tail = lax.slice_in_dim(cells, cells.shape[dim] - width, cells.shape[dim], axis=dim)
        cells = jnp.concatenate(
            [
                lax.ppermute(tail, axis, [(i, (i + 1) % count) for i in range(count)]),
                cells,
                lax.ppermute(head, axis, [((i + 1) % count, i) for i in range(count)]),
            ],
            axis=dim,
        )
    return cells


def from_behind(x, axis, by):
    length = lax.axis_size(axis)
    return lax.ppermute(x, axis, [(i, (i + by) % length) for i in range(length)])


def advance(padded, courant):
    along = courant[0]
    across = courant[1]
    rows_mid = padded[:, :, 1:-1, :]
    along_mid = along[:, 1:-1, :]
    face_east = 0.5 * (along_mid[..., :-1] + along_mid[..., 1:])
    east_flux = (
        jnp.maximum(face_east, 0.0) * rows_mid[..., :-1]
        + jnp.minimum(face_east, 0.0) * rows_mid[..., 1:]
    )
    cols_mid = padded[:, :, :, 1:-1]
    across_mid = across[:, :, 1:-1]
    face_north = 0.5 * (across_mid[:, :-1, :] + across_mid[:, 1:, :])
    north_flux = (
        jnp.maximum(face_north, 0.0) * cols_mid[:, :, :-1, :]
        + jnp.minimum(face_north, 0.0) * cols_mid[:, :, 1:, :]
    )
    return (
        padded[:, :, 1:-1, 1:-1]
        - (east_flux[..., 1:] - east_flux[..., :-1])
        - (north_flux[:, :, 1:, :] - north_flux[:, :, :-1, :])
    )


def radiate(feat_rows, index_row, ground, sun_table, solar, weights):
    w_first, b_first, w_second, b_second, w_third, b_third = weights
    featn = w_first.shape[0]
    levels = feat_rows.shape[0] // featn
    width = feat_rows.shape[1]
    inputs = feat_rows.reshape(featn, levels * width)
    hidden = jnp.dot(w_first.T, inputs, preferred_element_type=jnp.float32) + b_first[:, None]
    hidden = jax.nn.silu(hidden).astype(jnp.bfloat16)
    hidden = jnp.dot(w_second.T, hidden, preferred_element_type=jnp.float32) + b_second[:, None]
    hidden = jax.nn.silu(hidden).astype(jnp.bfloat16)
    logits = jnp.dot(w_third.T, hidden, preferred_element_type=jnp.float32) + b_third[:, None]
    optical = (tau_scale * jax.nn.softplus(logits)).reshape(-1, levels, width)
    entries = jnp.arange(sun_table.shape[0]).astype(jnp.float32)
    hits = (index_row[None, :] == entries[:, None]) & (entries[:, None] > 0.0)
    cosine = jnp.sum(jnp.where(hits, sun_table[:, None], 0.0), 0)
    safe = jnp.maximum(cosine, mu_floor)
    depth = jnp.cumsum(optical, axis=1)
    above = depth - optical
    total = depth[:, -1:, :]
    below = total - depth
    top_flux = solar[:, None, None] * cosine[None, None, :]
    direct = top_flux * jnp.exp(-above / safe) * (1.0 - jnp.exp(-optical / safe))
    upward = (
        ground[None, None, :]
        * top_flux
        * jnp.exp(-total / safe)
        * jnp.exp(-diffuse_factor * below)
        * (1.0 - jnp.exp(-diffuse_factor * optical))
    )
    return heat_scale * jnp.sum(direct + upward, 0)


def body(
    tracers,
    winds,
    gases,
    sun_index,
    block_slot,
    albedo,
    sun_table,
    solar,
    w_first,
    b_first,
    w_second,
    b_second,
    w_third,
    b_third,
):
    weights = (w_first, b_first, w_second, b_second, w_third, b_third)
    clat = tracers.shape[2]
    width = tracers.shape[3]
    total_rows = lax.axis_size("lat") * clat
    lat_start = lax.axis_index("lat") * clat

    def keep_rows(padded, rim):
        rows = lat_start - rim + jnp.arange(padded.shape[2])
        inside = ((rows >= 0) & (rows < total_rows)).astype(jnp.float32)
        return padded * inside[:, None]

    wind_pad = keep_rows(with_halo(winds, (("lon", 3), ("lat", 2)), 2), 2)
    wind_inner = wind_pad[:, :, 1:-1, 1:-1]

    def transport(state, count):
        for section in range(count):
            padded = keep_rows(with_halo(state, (("lon", 3), ("lat", 2)), 1), 1)
            state = advance(padded, wind_inner)
        return state

    state = transport(tracers, PRE_STEPS)
    features = jnp.concatenate([gases, state.astype(jnp.bfloat16)], 0).reshape(-1, clat, width)
    extras = jnp.stack([sun_index.astype(jnp.bfloat16), albedo], 0)
    payload = jnp.concatenate([features, extras], 0)

    def radiate_block(block):
        return radiate(
            block[:-2],
            block[-2].astype(jnp.float32),
            block[-1].astype(jnp.float32),
            sun_table,
            solar,
            weights,
        )

    half = clat // 2
    slot_ids = jnp.arange(clat)
    select = (block_slot[:, 0][None, :] == slot_ids[:, None]).astype(jnp.bfloat16)
    by_slot = jnp.einsum("sr,crl->csl", select, payload, preferred_element_type=jnp.float32).astype(
        jnp.bfloat16
    )
    upper = lax.axis_index("lon") >= lax.axis_size("lon") // 2
    mine = jnp.where(upper, by_slot[:, half:], by_slot[:, :half])
    theirs = jnp.where(upper, by_slot[:, :half], by_slot[:, half:])
    arrived = from_behind(theirs, "lon", lax.axis_size("lon") // 2)
    owned = mine + arrived
    heat_owned = lax.map(radiate_block, jnp.moveaxis(owned, 1, 0))
    heat_back = from_behind(heat_owned, "lon", lax.axis_size("lon") // 2)
    heat_slots = jnp.where(
        upper,
        jnp.concatenate([heat_back, heat_owned], 0),
        jnp.concatenate([heat_owned, heat_back], 0),
    )
    heat_rows = jnp.einsum(
        "sr,slc->rlc", select.astype(jnp.float32), heat_slots, precision=lax.Precision.HIGHEST
    )
    heating = jnp.moveaxis(heat_rows, 0, 1)
    state = state.at[0].add(heating)
    final = transport(state, POST_STEPS)
    return (final, heating)


def solution(mesh):
    in_specs = (
        P(None, None, "lat", "lon"),
        P(None, None, "lat", "lon"),
        P(None, None, "lat", "lon"),
        P("lat", "lon"),
        P("lat", "lon"),
        P("lat", "lon"),
        P(),
        P(),
        P(),
        P(),
        P(),
        P(),
        P(),
        P(),
    )
    out_specs = (P(None, None, "lat", "lon"), P(None, "lat", "lon"))
    return jax.shard_map(body, mesh=mesh, in_specs=in_specs, out_specs=out_specs, check_vma=False)
```

profile of v0, /device:TPU:1, one launch (start us, length us, event | category | flops | bytes accessed | tf_op | source)
XLA Modules:
  0.0 274.1 jit_solution(15585888885357052852)
XLA Ops:
  0.6 1.9 fusion.62
  2.6 2.0 collective-permute-start.4
  9.5 19.2 %collective-permute-done = f32[4,32,8,1]{3,2,1,0:T(8,128)S(1)} collective-permute-done((f32[4,32,8,1]{3,2,1,0:T(8,128)S(1)}, f32[4,32,8,1]{3,2,1,0:T(8,128)S(1)}, u32[]{:S(2)}, u32[]{:S(2)}) %collective-permute-start) | collective-permute-done | bytes 4128 | tf_op jit(solution)/shard_map/ppermute | solution.py:23
  28.6 11.2 %collective-permute-done.1 = f32[4,32,8,1]{3,2,1,0:T(8,128)S(1)} collective-permute-done((f32[4,32,8,1]{3,2,1,0:T(8,128)S(1)}, f32[4,32,8,1]{3,2,1,0:T(8,128)S(1)}, u32[]{:S(2)}, u32[]{:S(2)}) %collective-permute-start.1) | collective-permute-done | bytes 4128 | tf_op jit(solution)/shard_map/ppermute | solution.py:25
  40.7 2.8 %collective-permute-start.2 = (f32[4,32,1,130]{3,2,1,0:T(1,128)S(1)}, f32[4,32,1,130]{3,2,1,0:T(1,128)S(1)}, u32[]{:S(2)}, u32[]{:S(2)}) collective-permute-start(f32[4,32,1,130]{3,2,1,0:T(1,128)S(1)} %get-tuple-element.208), channel_id=1, source_target_pairs={{0,1},{1,2},{2,3},{3,4},{4,5},{5,6},{6,7},{7,0},{8,9},{9,10},{10,1... | collective-permute-start | bytes 199688 | tf_op jit(solution)/shard_map/ppermute | solution.py:23
  46.5 2.8 %collective-permute-done.3 = f32[4,32,1,130]{3,2,1,0:T(1,128)S(1)} collective-permute-done((f32[4,32,1,130]{3,2,1,0:T(1,128)S(1)}, f32[4,32,1,130]{3,2,1,0:T(1,128)S(1)}, u32[]{:S(2)}, u32[]{:S(2)}) %collective-permute-start.3) | collective-permute-done | bytes 66592 | tf_op jit(solution)/shard_map/ppermute | solution.py:25
  56.6 9.7 %collective-permute-done.8 = f32[4,32,8,1]{3,2,1,0:T(8,128)S(1)} collective-permute-done((f32[4,32,8,1]{3,2,1,0:T(8,128)S(1)}, f32[4,32,8,1]{3,2,1,0:T(8,128)S(1)}, u32[]{:S(2)}, u32[]{:S(2)}) %collective-permute-start.8) | collective-permute-done | bytes 4128 | tf_op jit(solution)/shard_map/ppermute | solution.py:23
  66.3 10.7 %collective-permute-done.9 = f32[4,32,8,1]{3,2,1,0:T(8,128)S(1)} collective-permute-done((f32[4,32,8,1]{3,2,1,0:T(8,128)S(1)}, f32[4,32,8,1]{3,2,1,0:T(8,128)S(1)}, u32[]{:S(2)}, u32[]{:S(2)}) %collective-permute-start.9) | collective-permute-done | bytes 4128 | tf_op jit(solution)/shard_map/ppermute | solution.py:25
  77.8 2.8 %collective-permute-start.10 = (f32[4,32,1,130]{3,2,1,0:T(1,128)S(1)}, f32[4,32,1,130]{3,2,1,0:T(1,128)S(1)}, u32[]{:S(2)}, u32[]{:S(2)}) collective-permute-start(f32[4,32,1,130]{3,2,1,0:T(1,128)S(1)} %get-tuple-element.206), channel_id=1, source_target_pairs={{0,1},{1,2},{2,3},{3,4},{4,5},{5,6},{6,7},{7,0},{8,9},{9,10},{10,1... | collective-permute-start | bytes 199688 | tf_op jit(solution)/shard_map/ppermute | solution.py:23
  82.6 3.0 %collective-permute-done.11 = f32[4,32,1,130]{3,2,1,0:T(1,128)S(1)} collective-permute-done((f32[4,32,1,130]{3,2,1,0:T(1,128)S(1)}, f32[4,32,1,130]{3,2,1,0:T(1,128)S(1)}, u32[]{:S(2)}, u32[]{:S(2)}) %collective-permute-start.11) | collective-permute-done | bytes 66592 | tf_op jit(solution)/shard_map/ppermute | solution.py:25
  92.0 9.9 %collective-permute-done.12 = bf16[514,4,128]{2,1,0:T(4,128)(2,1)S(1)} collective-permute-done((bf16[514,4,128]{2,1,0:T(4,128)(2,1)}, bf16[514,4,128]{2,1,0:T(4,128)(2,1)S(1)}, u32[]{:S(2)}, u32[]{:S(2)}) %collective-permute-start.12) | collective-permute-done | bytes 526368 | tf_op jit(solution)/shard_map/ppermute | solution.py:34
  102.6 94.9 %while.13 = (s32[]{:T(128)}, f32[4,32,128]{2,1,0:T(8,128)S(1)}, f32[224]{0:T(256)S(1)}, bf16[4,514,128]{2,1,0:T(8,128)(2,1)S(1)}, f32[64]{0:T(128)S(1)}, /*index...) while((s32[]{:T(128)}, f32[4,32,128]{2,1,0:T(8,128)S(1)}, ...), condition=%wide.region_4.5_spmd, body=%wide.region_0.4_spmd.sunk | while | flops 214114752 | bytes 87048464 | solution.py:155
  103.7 2.3 compare_select_fusion.2
  107.9 2.1 fusion.86
  114.6 11.8 %fusion.88 = f32[4096]{0:T(1024)S(1)} fusion(f32[28,8,32,128]{3,2,1,0:T(8,128)S(1)} %bitcast.151, f32[28,8,32,128]{3,2,1,0:T(8,128)S(1)} %bitcast.152, f32[28,8,32,128]{3,2,1,0:T(8,128)S(1)} %bitcast.153, f32[224,4096]{1,0:T(8,128)S(1)} %copy-done.2, f32[4096]{0:T(1024)S(1)} %broadcast_bitcast_fusion.2, f32[224,32,128]{2,0,1:T(8,128)S(1)} %copy-done), kind=kLoop, calls=%fused_computation.13.clone.1 | loop fusion | flops 15593472 | bytes 18382848 | tf_op jit(solution)/shard_map/while/body/eval_jaxpr/reduce_sum | solution.py:90
  127.4 2.3 compare_select_fusion.2
  131.5 2.1 fusion.86
  138.3 11.8 %fusion.88 = f32[4096]{0:T(1024)S(1)} fusion(f32[28,8,32,128]{3,2,1,0:T(8,128)S(1)} %bitcast.151, f32[28,8,32,128]{3,2,1,0:T(8,128)S(1)} %bitcast.152, f32[28,8,32,128]{3,2,1,0:T(8,128)S(1)} %bitcast.153, f32[224,4096]{1,0:T(8,128)S(1)} %copy-done.2, f32[4096]{0:T(1024)S(1)} %broadcast_bitcast_fusion.2, f32[224,32,128]{2,0,1:T(8,128)S(1)} %copy-done), kind=kLoop, calls=%fused_computation.13.clone.1 | loop fusion | flops 15593472 | bytes 18382848 | tf_op jit(solution)/shard_map/while/body/eval_jaxpr/reduce_sum | solution.py:90
  151.1 2.3 compare_select_fusion.2
  155.2 2.1 fusion.86
  162.0 11.8 %fusion.88 = f32[4096]{0:T(1024)S(1)} fusion(f32[28,8,32,128]{3,2,1,0:T(8,128)S(1)} %bitcast.151, f32[28,8,32,128]{3,2,1,0:T(8,128)S(1)} %bitcast.152, f32[28,8,32,128]{3,2,1,0:T(8,128)S(1)} %bitcast.153, f32[224,4096]{1,0:T(8,128)S(1)} %copy-done.2, f32[4096]{0:T(1024)S(1)} %broadcast_bitcast_fusion.2, f32[224,32,128]{2,0,1:T(8,128)S(1)} %copy-done), kind=kLoop, calls=%fused_computation.13.clone.1 | loop fusion | flops 15593472 | bytes 18382848 | tf_op jit(solution)/shard_map/while/body/eval_jaxpr/reduce_sum | solution.py:90
  174.7 2.3 compare_select_fusion.2
  178.9 2.1 fusion.86
  185.6 11.8 %fusion.88 = f32[4096]{0:T(1024)S(1)} fusion(f32[28,8,32,128]{3,2,1,0:T(8,128)S(1)} %bitcast.151, f32[28,8,32,128]{3,2,1,0:T(8,128)S(1)} %bitcast.152, f32[28,8,32,128]{3,2,1,0:T(8,128)S(1)} %bitcast.153, f32[224,4096]{1,0:T(8,128)S(1)} %copy-done.2, f32[4096]{0:T(1024)S(1)} %broadcast_bitcast_fusion.2, f32[224,32,128]{2,0,1:T(8,128)S(1)} %copy-done), kind=kLoop, calls=%fused_computation.13.clone.1 | loop fusion | flops 15593472 | bytes 18382848 | tf_op jit(solution)/shard_map/while/body/eval_jaxpr/reduce_sum | solution.py:90
  198.6 2.0 collective-permute-done.13
  204.2 7.4 %collective-permute-done.14 = f32[4,32,8,1]{3,2,1,0:T(8,128)S(1)} collective-permute-done((f32[4,32,8,1]{3,2,1,0:T(8,128)S(1)}, f32[4,32,8,1]{3,2,1,0:T(8,128)S(1)}, u32[]{:S(2)}, u32[]{:S(2)}) %collective-permute-start.14) | collective-permute-done | bytes 4128 | tf_op jit(solution)/shard_map/ppermute | solution.py:23
  211.6 11.0 %collective-permute-done.15 = f32[4,32,8,1]{3,2,1,0:T(8,128)S(1)} collective-permute-done((f32[4,32,8,1]{3,2,1,0:T(8,128)S(1)}, f32[4,32,8,1]{3,2,1,0:T(8,128)S(1)}, u32[]{:S(2)}, u32[]{:S(2)}) %collective-permute-start.15) | collective-permute-done | bytes 4128 | tf_op jit(solution)/shard_map/ppermute | solution.py:25
  223.5 8.5 %collective-permute-start.16 = (f32[4,32,1,130]{3,2,1,0:T(1,128)S(1)}, f32[4,32,1,130]{3,2,1,0:T(1,128)S(1)}, u32[]{:S(2)}, u32[]{:S(2)}) collective-permute-start(f32[4,32,1,130]{3,2,1,0:T(1,128)S(1)} %get-tuple-element.204), channel_id=1, source_target_pairs={{0,1},{1,2},{2,3},{3,4},{4,5},{5,6},{6,7},{7,0},{8,9},{9,10},{10,1... | collective-permute-start | bytes 199688 | tf_op jit(solution)/shard_map/ppermute | solution.py:23
  234.0 3.8 %collective-permute-done.17 = f32[4,32,1,130]{3,2,1,0:T(1,128)S(1)} collective-permute-done((f32[4,32,1,130]{3,2,1,0:T(1,128)S(1)}, f32[4,32,1,130]{3,2,1,0:T(1,128)S(1)}, u32[]{:S(2)}, u32[]{:S(2)}) %collective-permute-start.17) | collective-permute-done | bytes 66592 | tf_op jit(solution)/shard_map/ppermute | solution.py:25
  242.9 12.4 %collective-permute-done.18 = f32[4,32,8,1]{3,2,1,0:T(8,128)S(1)} collective-permute-done((f32[4,32,8,1]{3,2,1,0:T(8,128)S(1)}, f32[4,32,8,1]{3,2,1,0:T(8,128)S(1)}, u32[]{:S(2)}, u32[]{:S(2)}) %collective-permute-start.18) | collective-permute-done | bytes 4128 | tf_op jit(solution)/shard_map/ppermute | solution.py:23
  255.3 10.2 %collective-permute-done.19 = f32[4,32,8,1]{3,2,1,0:T(8,128)S(1)} collective-permute-done((f32[4,32,8,1]{3,2,1,0:T(8,128)S(1)}, f32[4,32,8,1]{3,2,1,0:T(8,128)S(1)}, u32[]{:S(2)}, u32[]{:S(2)}) %collective-permute-start.19) | collective-permute-done | bytes 4128 | tf_op jit(solution)/shard_map/ppermute | solution.py:25
  268.4 2.5 collective-permute-done.21
  (178 shorter events, 73.5 us)
Async XLA Ops:
  0.6 39.2 %copy-start.3 = (f32[4,32,8,128]{3,2,1,0:T(8,128)S(1)}, f32[4,32,8,128]{3,2,1,0:T(8,128)}, u32[]{:S(2)}) copy-start(f32[4,32,8,128]{3,2,1,0:T(8,128)} %param.18) | copy-start | bytes 1572868
  2.6 40.9 %copy-start.4 = (f32[2,32,8,128]{3,2,1,0:T(8,128)S(1)}, f32[2,32,8,128]{3,2,1,0:T(8,128)}, u32[]{:S(2)}) copy-start(f32[2,32,8,128]{3,2,1,0:T(8,128)} %param.19) | copy-start | bytes 786436
  2.6 40.9 %collective-permute-start.4 = (f32[2,32,8,2]{3,2,1,0:T(8,128)}, f32[2,32,8,2]{3,2,1,0:T(8,128)S(1)}, u32[]{:S(2)}, u32[]{:S(2)}) collective-permute-start(f32[2,32,8,2]{3,2,1,0:T(8,128)} %get-tuple-element.226), channel_id=1, source_target_pairs={{0,8},{8,16},{16,24},{24,0},{1,9},{9,17},{17,25},{25,1},{2,10},{10... | collective-permute-start | bytes 12296 | tf_op jit(solution)/shard_map/ppermute | solution.py:23
  4.6 38.9 %collective-permute-start.5 = (f32[2,32,8,2]{3,2,1,0:T(8,128)}, f32[2,32,8,2]{3,2,1,0:T(8,128)S(1)}, u32[]{:S(2)}, u32[]{:S(2)}) collective-permute-start(f32[2,32,8,2]{3,2,1,0:T(8,128)} %get-tuple-element.227), channel_id=1, source_target_pairs={{8,0},{16,8},{24,16},{0,24},{9,1},{17,9},{25,17},{1,25},{10,2},{18... | collective-permute-start | bytes 12296 | tf_op jit(solution)/shard_map/ppermute | solution.py:25
  7.0 21.6 %collective-permute-start = (f32[4,32,8,1]{3,2,1,0:T(8,128)S(1)}, f32[4,32,8,1]{3,2,1,0:T(8,128)S(1)}, u32[]{:S(2)}, u32[]{:S(2)}) collective-permute-start(f32[4,32,8,1]{3,2,1,0:T(8,128)S(1)} %get-tuple-element.224), channel_id=1, source_target_pairs={{0,8},{8,16},{16,24},{24,0},{1,9},{9,17},{17,25},{25,1},{2,10},{10... | collective-permute-start | bytes 12296 | tf_op jit(solution)/shard_map/ppermute | solution.py:23
  7.6 32.3 %collective-permute-start.1 = (f32[4,32,8,1]{3,2,1,0:T(8,128)S(1)}, f32[4,32,8,1]{3,2,1,0:T(8,128)S(1)}, u32[]{:S(2)}, u32[]{:S(2)}) collective-permute-start(f32[4,32,8,1]{3,2,1,0:T(8,128)S(1)} %get-tuple-element.225), channel_id=1, source_target_pairs={{8,0},{16,8},{24,16},{0,24},{9,1},{17,9},{25,17},{1,25},{10,2},{18... | collective-permute-start | bytes 12296 | tf_op jit(solution)/shard_map/ppermute | solution.py:25
  40.7 5.7 %collective-permute-start.2 = (f32[4,32,1,130]{3,2,1,0:T(1,128)S(1)}, f32[4,32,1,130]{3,2,1,0:T(1,128)S(1)}, u32[]{:S(2)}, u32[]{:S(2)}) collective-permute-start(f32[4,32,1,130]{3,2,1,0:T(1,128)S(1)} %get-tuple-element.208), channel_id=1, source_target_pairs={{0,1},{1,2},{2,3},{3,4},{4,5},{5,6},{6,7},{7,0},{8,9},{9,10},{10,1... | collective-permute-start | bytes 199688 | tf_op jit(solution)/shard_map/ppermute | solution.py:23
  43.5 5.7 %collective-permute-start.3 = (f32[4,32,1,130]{3,2,1,0:T(1,128)S(1)}, f32[4,32,1,130]{3,2,1,0:T(1,128)S(1)}, u32[]{:S(2)}, u32[]{:S(2)}) collective-permute-start(f32[4,32,1,130]{3,2,1,0:T(1,128)S(1)} %get-tuple-element.209), channel_id=1, source_target_pairs={{1,0},{2,1},{3,2},{4,3},{5,4},{6,5},{7,6},{0,7},{9,8},{10,9},{11,1... | collective-permute-start | bytes 199688 | tf_op jit(solution)/shard_map/ppermute | solution.py:25
  44.0 6.3 %collective-permute-start.6 = (f32[2,32,2,132]{3,2,1,0:T(2,128)S(1)}, f32[2,32,2,132]{3,2,1,0:T(2,128)S(1)}, u32[]{:S(2)}, u32[]{:S(2)}) collective-permute-start(f32[2,32,2,132]{3,2,1,0:T(2,128)S(1)} %get-tuple-element.212), channel_id=1, source_target_pairs={{0,1},{1,2},{2,3},{3,4},{4,5},{5,6},{6,7},{7,0},{8,9},{9,10},{10,1... | collective-permute-start | bytes 202760 | tf_op jit(solution)/shard_map/ppermute | solution.py:23
  45.8 5.6 %collective-permute-start.7 = (f32[2,32,2,132]{3,2,1,0:T(2,128)S(1)}, f32[2,32,2,132]{3,2,1,0:T(2,128)S(1)}, u32[]{:S(2)}, u32[]{:S(2)}) collective-permute-start(f32[2,32,2,132]{3,2,1,0:T(2,128)S(1)} %get-tuple-element.213), channel_id=1, source_target_pairs={{1,0},{2,1},{3,2},{4,3},{5,4},{6,5},{7,6},{0,7},{9,8},{10,9},{11,1... | collective-permute-start | bytes 202760 | tf_op jit(solution)/shard_map/ppermute | solution.py:25
  54.0 26.8 %copy-start.8 = (s32[8,128]{1,0:T(8,128)S(1)}, s32[8,128]{1,0:T(8,128)}, u32[]{:S(2)}) copy-start(s32[8,128]{1,0:T(8,128)} %param.21) | copy-start | bytes 12292
  54.2 12.1 %collective-permute-start.8 = (f32[4,32,8,1]{3,2,1,0:T(8,128)S(1)}, f32[4,32,8,1]{3,2,1,0:T(8,128)S(1)}, u32[]{:S(2)}, u32[]{:S(2)}) collective-permute-start(f32[4,32,8,1]{3,2,1,0:T(8,128)S(1)} %get-tuple-element.218), channel_id=1, source_target_pairs={{0,8},{8,16},{16,24},{24,0},{1,9},{9,17},{17,25},{25,1},{2,10},{10... | collective-permute-start | bytes 12296 | tf_op jit(solution)/shard_map/ppermute | solution.py:23
  55.5 21.5 %collective-permute-start.9 = (f32[4,32,8,1]{3,2,1,0:T(8,128)S(1)}, f32[4,32,8,1]{3,2,1,0:T(8,128)S(1)}, u32[]{:S(2)}, u32[]{:S(2)}) collective-permute-start(f32[4,32,8,1]{3,2,1,0:T(8,128)S(1)} %get-tuple-element.219), channel_id=1, source_target_pairs={{8,0},{16,8},{24,16},{0,24},{9,1},{17,9},{25,17},{1,25},{10,2},{18... | collective-permute-start | bytes 12296 | tf_op jit(solution)/shard_map/ppermute | solution.py:25
  77.8 4.7 %collective-permute-start.10 = (f32[4,32,1,130]{3,2,1,0:T(1,128)S(1)}, f32[4,32,1,130]{3,2,1,0:T(1,128)S(1)}, u32[]{:S(2)}, u32[]{:S(2)}) collective-permute-start(f32[4,32,1,130]{3,2,1,0:T(1,128)S(1)} %get-tuple-element.206), channel_id=1, source_target_pairs={{0,1},{1,2},{2,3},{3,4},{4,5},{5,6},{6,7},{7,0},{8,9},{9,10},{10,1... | collective-permute-start | bytes 199688 | tf_op jit(solution)/shard_map/ppermute | solution.py:23
  80.6 5.0 %collective-permute-start.11 = (f32[4,32,1,130]{3,2,1,0:T(1,128)S(1)}, f32[4,32,1,130]{3,2,1,0:T(1,128)S(1)}, u32[]{:S(2)}, u32[]{:S(2)}) collective-permute-start(f32[4,32,1,130]{3,2,1,0:T(1,128)S(1)} %get-tuple-element.207), channel_id=1, source_target_pairs={{1,0},{2,1},{3,2},{4,3},{5,4},{6,5},{7,6},{0,7},{9,8},{10,9},{11,1... | collective-permute-start | bytes 199688 | tf_op jit(solution)/shard_map/ppermute | solution.py:25
  89.5 13.0 %copy-start.6 = (f32[224]{0:T(256)S(1)}, f32[224]{0:T(256)}, u32[]{:S(2)}) copy-start(f32[224]{0:T(256)} %param.25) | copy-start | bytes 2692
  89.5 13.0 %copy-start.7 = (f32[64]{0:T(128)S(1)}, f32[64]{0:T(128)}, u32[]{:S(2)}) copy-start(f32[64]{0:T(128)} %param.24) | copy-start | bytes 772
  89.5 13.0 %copy-start.10 = (bf16[64,224]{1,0:T(8,128)(2,1)S(1)}, bf16[64,224]{1,0:T(8,128)(2,1)}, u32[]{:S(2)}) copy-start(bf16[64,224]{1,0:T(8,128)(2,1)} %param.30) | copy-start | bytes 86020
  89.5 13.0 %copy-start.11 = (bf16[64,64]{1,0:T(8,128)(2,1)S(1)}, bf16[64,64]{1,0:T(8,128)(2,1)}, u32[]{:S(2)}) copy-start(bf16[64,64]{1,0:T(8,128)(2,1)} %param.28) | copy-start | bytes 24580
  89.5 13.0 %copy-start.12 = (bf16[16,64]{1,0:T(8,128)(2,1)S(1)}, bf16[16,64]{1,0:T(8,128)(2,1)}, u32[]{:S(2)}) copy-start(bf16[16,64]{1,0:T(8,128)(2,1)} %param.26) | copy-start | bytes 6148
  89.5 13.0 %copy-start.14 = (f32[224]{0:T(256)S(1)}, f32[224]{0:T(256)}, u32[]{:S(2)}) copy-start(f32[224]{0:T(256)} %param.31) | copy-start | bytes 2692
  89.5 13.0 %copy-start.15 = (f32[64]{0:T(128)S(1)}, f32[64]{0:T(128)}, u32[]{:S(2)}) copy-start(f32[64]{0:T(128)} %param.27) | copy-start | bytes 772
  90.8 11.1 %collective-permute-start.12 = (bf16[514,4,128]{2,1,0:T(4,128)(2,1)}, bf16[514,4,128]{2,1,0:T(4,128)(2,1)S(1)}, u32[]{:S(2)}, u32[]{:S(2)}) collective-permute-start(bf16[514,4,128]{2,1,0:T(4,128)(2,1)} %broadcast_select_fusion), channel_id=1, source_target_pairs={{0,16},{8,24},{16,0},{24,8},{1,17},{9,25},{17,1},{25,9},{2,18},{10... | collective-permute-start | bytes 1579016 | tf_op jit(solution)/shard_map/ppermute | solution.py:34
  197.5 3.2 %collective-permute-start.13 = (f32[4,32,128]{2,1,0:T(8,128)S(1)}, f32[4,32,128]{2,1,0:T(8,128)S(1)}, u32[]{:S(2)}, u32[]{:S(2)}) collective-permute-start(f32[4,32,128]{2,1,0:T(8,128)S(1)} %get-tuple-element.151), channel_id=1, source_target_pairs={{0,16},{8,24},{16,0},{24,8},{1,17},{9,25},{17,1},{25,9},{2,18},{10... | collective-permute-start | bytes 196616 | tf_op jit(solution)/shard_map/ppermute | solution.py:34
  201.8 9.8 %collective-permute-start.14 = (f32[4,32,8,1]{3,2,1,0:T(8,128)S(1)}, f32[4,32,8,1]{3,2,1,0:T(8,128)S(1)}, u32[]{:S(2)}, u32[]{:S(2)}) collective-permute-start(f32[4,32,8,1]{3,2,1,0:T(8,128)S(1)} %get-tuple-element.216), channel_id=1, source_target_pairs={{0,8},{8,16},{16,24},{24,0},{1,9},{9,17},{17,25},{25,1},{2,10},{10... | collective-permute-start | bytes 12296 | tf_op jit(solution)/shard_map/ppermute | solution.py:23
  202.9 19.7 %collective-permute-start.15 = (f32[4,32,8,1]{3,2,1,0:T(8,128)S(1)}, f32[4,32,8,1]{3,2,1,0:T(8,128)S(1)}, u32[]{:S(2)}, u32[]{:S(2)}) collective-permute-start(f32[4,32,8,1]{3,2,1,0:T(8,128)S(1)} %get-tuple-element.217), channel_id=1, source_target_pairs={{8,0},{16,8},{24,16},{0,24},{9,1},{17,9},{25,17},{1,25},{10,2},{18... | collective-permute-start | bytes 12296 | tf_op jit(solution)/shard_map/ppermute | solution.py:25
  223.5 10.5 %collective-permute-start.16 = (f32[4,32,1,130]{3,2,1,0:T(1,128)S(1)}, f32[4,32,1,130]{3,2,1,0:T(1,128)S(1)}, u32[]{:S(2)}, u32[]{:S(2)}) collective-permute-start(f32[4,32,1,130]{3,2,1,0:T(1,128)S(1)} %get-tuple-element.204), channel_id=1, source_target_pairs={{0,1},{1,2},{2,3},{3,4},{4,5},{5,6},{6,7},{7,0},{8,9},{9,10},{10,1... | collective-permute-start | bytes 199688 | tf_op jit(solution)/shard_map/ppermute | solution.py:23
  232.0 5.8 %collective-permute-start.17 = (f32[4,32,1,130]{3,2,1,0:T(1,128)S(1)}, f32[4,32,1,130]{3,2,1,0:T(1,128)S(1)}, u32[]{:S(2)}, u32[]{:S(2)}) collective-permute-start(f32[4,32,1,130]{3,2,1,0:T(1,128)S(1)} %get-tuple-element.205), channel_id=1, source_target_pairs={{1,0},{2,1},{3,2},{4,3},{5,4},{6,5},{7,6},{0,7},{9,8},{10,9},{11,1... | collective-permute-start | bytes 199688 | tf_op jit(solution)/shard_map/ppermute | solution.py:25
  240.5 14.8 %collective-permute-start.18 = (f32[4,32,8,1]{3,2,1,0:T(8,128)S(1)}, f32[4,32,8,1]{3,2,1,0:T(8,128)S(1)}, u32[]{:S(2)}, u32[]{:S(2)}) collective-permute-start(f32[4,32,8,1]{3,2,1,0:T(8,128)S(1)} %get-tuple-element.214), channel_id=1, source_target_pairs={{0,8},{8,16},{16,24},{24,0},{1,9},{9,17},{17,25},{25,1},{2,10},{10... | collective-permute-start | bytes 12296 | tf_op jit(solution)/shard_map/ppermute | solution.py:23
  241.7 23.8 %collective-permute-start.19 = (f32[4,32,8,1]{3,2,1,0:T(8,128)S(1)}, f32[4,32,8,1]{3,2,1,0:T(8,128)S(1)}, u32[]{:S(2)}, u32[]{:S(2)}) collective-permute-start(f32[4,32,8,1]{3,2,1,0:T(8,128)S(1)} %get-tuple-element.215), channel_id=1, source_target_pairs={{8,0},{16,8},{24,16},{0,24},{9,1},{17,9},{25,17},{1,25},{10,2},{18... | collective-permute-start | bytes 12296 | tf_op jit(solution)/shard_map/ppermute | solution.py:25
  266.4 2.0 collective-permute-start.20
  266.4 4.4 %collective-permute-start.21 = (f32[4,32,1,130]{3,2,1,0:T(1,128)S(1)}, f32[4,32,1,130]{3,2,1,0:T(1,128)S(1)}, u32[]{:S(2)}, u32[]{:S(2)}) collective-permute-start(f32[4,32,1,130]{3,2,1,0:T(1,128)S(1)} %get-tuple-element.203), channel_id=1, source_target_pairs={{1,0},{2,1},{3,2},{4,3},{5,4},{6,5},{7,6},{0,7},{9,8},{10,9},{11,1... | collective-permute-start | bytes 199688 | tf_op jit(solution)/shard_map/ppermute | solution.py:25
  (16 other events, 43.7 us)
where the time goes:
time: 278 us; the launch traced here: 274 us
  waiting for transfers between devices  122 us (44%)
  other arithmetic  77.9 us (28%)
  starting transfers between devices  32.3 us (12%)
  local copies, waits for them, and re-layouts  25.9 us (9%)
  matrix products  14.3 us (5%)
    ppermute x10, waiting for transfers between devices, with_halo(): lax.ppermute(head, axis, [((i + 1) % count, i) for i in range(count)])  56.3 us
    ppermute x10, waiting for transfers between devices, with_halo(): lax.ppermute(tail, axis, [(i, (i + 1) % count) for i in range(count)])  53.7 us
    reduce_sum x4, other arithmetic, radiate(): return heat_scale * jnp.sum(direct + upward, 0)  47.2 us
    ppermute x10, starting transfers between devices, with_halo(): lax.ppermute(tail, axis, [(i, (i + 1) % count) for i in range(count)])  22.1 us
    while x24, local copies, waits for them, and re-layouts  17.5 us
    ppermute x2, waiting for transfers between devices, from_behind(): lax.ppermute(x, axis, [(i, (i + by) % length) for i in range(length)])  12 us
    dot_general x4, matrix products, radiate(): jnp.dot(w_third.T, hidden, preferred_element_type=jnp.float32)  9.38 us
    another operation x4, other arithmetic, radiate(): depth = jnp.cumsum(optical, axis=1)  8.56 us
  transfers between devices with their start and end apart: 22, of which 18 were waited for; matrix products, arithmetic and copies ran while one was open for 1% of the time, Pallas kernels for 0%

commit v1 on v0

v1 whole, which is shorter than its diff:
```python
import functools
import math

import jax
import jax.numpy as jnp
from jax import lax
from jax.experimental import pallas as pl
from jax.experimental.pallas import tpu as pltpu
from jax.sharding import PartitionSpec as P

tau_scale = 0.05
mu_floor = 0.05
heat_scale = 30.0
diffuse_factor = 1.66
log2e = 1.4426950408889634

ROWS = 8
COLS = 128
RIM = 2
SLOTS = COLS // RIM


def lane_id():
    return lax.broadcasted_iota(jnp.int32, (ROWS, COLS), 1)


def row_id():
    return lax.broadcasted_iota(jnp.int32, (ROWS, COLS), 0)


def ahead_col(tile, beside):
    return pltpu.roll(jnp.where(lane_id() == 0, beside, tile), COLS - 1, 1)


def behind_col(tile, beside):
    return pltpu.roll(jnp.where(lane_id() == COLS - 1, beside, tile), 1, 1)


def ahead_row(tile, beside):
    return pltpu.roll(jnp.where(row_id() == 0, beside, tile), ROWS - 1, 0)


def behind_row(tile, beside):
    return pltpu.roll(jnp.where(row_id() == ROWS - 1, beside, tile), 1, 0)


def flux(face, here, there):
    return jnp.maximum(face, 0.0) * here + jnp.minimum(face, 0.0) * there


def faces(along, across):
    am, ah, av, ac = along
    bm, bh, bv, bc = across
    east = tuple(
        0.5 * (t + ahead_col(t, o)) for t, o in ((am, ah), (ah, am), (av, ac), (ac, av))
    )
    north = tuple(
        0.5 * (t + ahead_row(t, o)) for t, o in ((bm, bv), (bh, bc), (bv, bm), (bc, bh))
    )
    return east, north


def two_steps(q, east, north, inside):
    m, h, v, c = q
    em = flux(east[0], m, ahead_col(m, h))
    eh = flux(east[1], h, ahead_col(h, m))
    ev = flux(east[2], v, ahead_col(v, c))
    ec = flux(east[3], c, ahead_col(c, v))
    nm = flux(north[0], m, ahead_row(m, v))
    nh = flux(north[1], h, ahead_row(h, c))
    nv = flux(north[2], v, ahead_row(v, m))
    nc = flux(north[3], c, ahead_row(c, h))
    m1 = m - (em - behind_col(em, eh)) - (nm - behind_row(nm, nv))
    h1 = h - (eh - behind_col(eh, em)) - (nh - behind_row(nh, nc))
    v1 = v - (ev - behind_col(ev, ec)) - (nv - behind_row(nv, nm))
    v1 = jnp.where(inside > 0.0, v1, 0.0)
    em = flux(east[0], m1, ahead_col(m1, h1))
    eh = flux(east[1], h1, ahead_col(h1, m1))
    nm = flux(north[0], m1, ahead_row(m1, v1))
    nv = flux(north[2], v1, ahead_row(v1, m1))
    return m1 - (em - behind_col(em, eh)) - (nm - behind_row(nm, nv))


def pack_sides(tile, slot, packs):
    head, tail = packs
    lane = lane_id()
    here = (lane >= RIM * slot) & (lane < RIM * slot + RIM)
    head = jnp.where(here, pltpu.roll(tile, RIM * slot, 1), head)
    tail = jnp.where(here, pltpu.roll(tile, lax.rem(RIM * slot + RIM, COLS), 1), tail)
    return head, tail


def unpack_sides(from_right, from_left, slot):
    right = pltpu.roll(from_right, lax.rem(COLS - RIM * slot, COLS), 1)
    left = pltpu.roll(from_left, lax.rem(2 * COLS - RIM - RIM * slot, COLS), 1)
    return jnp.where(lane_id() < COLS // 2, right, left)


def place(field, level, levels):
    per = SLOTS // levels
    return field // per, (field % per) * levels + level


def packed_tiles(fields, levels):
    return pl.cdiv(fields * levels, SLOTS)


def pack_fields(sources, levels, head_ref, tail_ref):
    count = packed_tiles(len(sources), levels)
    zero = jnp.zeros((ROWS, COLS), jnp.float32)

    def step(level, packs):
        packs = list(packs)
        for field, source in enumerate(sources):
            tile, slot = place(field, level, levels)
            packs[tile] = pack_sides(source(level), slot, packs[tile])
        return tuple(packs)

    packs = lax.fori_loop(0, levels, step, ((zero, zero),) * count)
    for tile, (head, tail) in enumerate(packs):
        head_ref[tile] = head
        tail_ref[tile] = tail


def pack_cols_kernel(tracers, winds, head, tail):
    levels = tracers.shape[1]
    fields = [(tracers, f) for f in range(tracers.shape[0])]
    fields += [(winds, f) for f in range(winds.shape[0])]
    pack_fields(
        [lambda level, ref=ref, f=f: ref[f, level] for ref, f in fields], levels, head, tail
    )


def row_payload(fields, levels):
    rows = RIM * fields * levels + 2 * RIM * packed_tiles(fields, levels)
    return -(-rows // 16) * 16


def pack_rows_kernel(*refs):
    *fields, from_right, from_left, head, tail = refs
    at = 0
    total = sum(ref.shape[0] for ref in fields) // ROWS
    for ref in fields:
        tiles = ref.shape[0] // ROWS
        for row in range(RIM):
            head[pl.ds(row * total + at, tiles), :] = ref[pl.ds(row, tiles, stride=ROWS), :]
            tail[pl.ds(row * total + at, tiles), :] = ref[
                pl.ds(ROWS - RIM + row, tiles, stride=ROWS), :
            ]
        at += tiles
    base = RIM * total
    head[base:, :] = jnp.zeros((head.shape[0] - base, COLS), jnp.float32)
    tail[base:, :] = jnp.zeros((head.shape[0] - base, COLS), jnp.float32)
    at = base
    for ref in (from_right, from_left):
        for tile in range(ref.shape[0]):
            head[at : at + RIM, :] = ref[tile, 0:RIM, :]
            tail[at : at + RIM, :] = ref[tile, ROWS - RIM : ROWS, :]
            at += RIM


def unpack_rows(from_north, from_south, rim_ref, corner_ref, tiles, packed):
    for row in range(RIM):
        rim_ref[pl.ds(row, tiles, stride=ROWS), :] = from_north[pl.ds(row * tiles, tiles), :]
        rim_ref[pl.ds(ROWS - RIM + row, tiles, stride=ROWS), :] = from_south[
            pl.ds(row * tiles, tiles), :
        ]
    at = RIM * tiles
    for tile in range(2 * packed):
        corner_ref[tile, 0:RIM, :] = from_north[at : at + RIM, :]
        corner_ref[tile, ROWS - RIM : ROWS, :] = from_south[at : at + RIM, :]
        at += RIM


def rim_tiles(field, level, levels, packed, right, left, rim_ref, corner_ref):
    tile, slot = place(field, level, levels)
    side = unpack_sides(right[tile], left[tile], slot)
    row = pl.multiple_of((field * levels + level) * ROWS, ROWS)
    rows = rim_ref[pl.ds(row, ROWS), :]
    corner = unpack_sides(corner_ref[tile], corner_ref[packed + tile], slot)
    return side, rows, corner


def first_kernel(
    tracers,
    winds,
    right,
    left,
    north,
    south,
    inside,
    gases,
    index,
    ground,
    table,
    lsolar,
    w1,
    b1,
    w2,
    b2,
    w3,
    state,
    heating,
    head,
    tail,
    rim_ref,
    corner_ref,
    xs,
    depth,
    weight,
    sums,
    kappa,
    lground,
):
    ntr, levels = tracers.shape[0], tracers.shape[1]
    fields = ntr + winds.shape[0]
    packed = packed_tiles(fields, levels)
    groups = lsolar.shape[0]
    hid = b1.shape[0]
    unpack_rows(north, south, rim_ref, corner_ref, fields * levels, packed)
    keep = inside[...]

    def transport(level, carry):
        rim = functools.partial(
            rim_tiles,
            level=level,
            levels=levels,
            packed=packed,
            right=right,
            left=left,
            rim_ref=rim_ref,
            corner_ref=corner_ref,
        )
        east, north_face = faces(
            (winds[0, level], *rim(ntr)), (winds[1, level], *rim(ntr + 1))
        )
        out = []
        for f in range(ntr):
            q = two_steps((tracers[f, level], *rim(f)), east, north_face, keep)
            state[f, level] = q
            out.append(q)
        xs[level] = jnp.concatenate(out, 0).astype(jnp.bfloat16)
        return carry

    lax.fori_loop(0, levels, transport, 0)

    ids = index[...]
    cosine = jnp.zeros((ROWS, COLS), jnp.float32)
    for entry in range(1, table.shape[0]):
        cosine = jnp.where(ids == entry, table[entry], cosine)
    slant = tau_scale / jnp.maximum(cosine, mu_floor)
    lg = jnp.log2(ground[...])
    for row in range(ROWS):
        kappa[row] = jnp.broadcast_to(slant[row : row + 1], (ROWS, COLS))
        lground[row] = jnp.broadcast_to(lg[row : row + 1], (ROWS, COLS))

    diffuse = diffuse_factor * tau_scale
    zero = jnp.zeros((groups, ROWS, COLS), jnp.float32)
    depth[0, 0] = zero
    depth[1, 0] = zero
    ones = jnp.ones((w3.shape[1] - hid, 2 * COLS), jnp.bfloat16)

    def optical(row, pair):
        buf = lax.rem(row, 2)
        l0 = 2 * pair
        x = jnp.concatenate(
            [jnp.concatenate([gases[l0 + k], xs[l0 + k]], 0) for k in range(2)], 1
        )
        wide1 = jnp.concatenate([b1[...]] * 2, 1)
        wide2 = jnp.concatenate([b2[...]] * 2, 1)
        mine = w1[pl.ds(pl.multiple_of(row * hid, hid), hid), :]
        y = jnp.dot(mine, x, preferred_element_type=jnp.float32) + wide1
        y = (y + y * jnp.tanh(y)).astype(jnp.bfloat16)
        y = jnp.dot(w2[...], y, preferred_element_type=jnp.float32) + wide2
        y = (y + y * jnp.tanh(y)).astype(jnp.bfloat16)
        y = jnp.concatenate([y, ones], 0)
        t = jnp.dot(w3[...], y, preferred_element_type=jnp.float32) * log2e
        soft = jnp.maximum(t, jnp.log2(1.0 + jnp.exp2(jnp.minimum(t, 126.0))))
        soft = soft.reshape(groups, ROWS, 2 * COLS)
        d = depth[buf, l0] + soft[:, :, :COLS]
        depth[buf, l0 + 1] = d
        depth[buf, l0 + 2] = d + soft[:, :, COLS:]

    def light(row, level):
        buf = lax.rem(row, 2)
        d = depth[buf, level]
        direct = jnp.exp2(lsolar[...] - d * kappa[row][None])
        upward = jnp.exp2(weight[...] + d * diffuse)
        sums[row, level] = jnp.sum(direct - upward, 0)

    def close(row):
        buf = lax.rem(row, 2)
        total = depth[buf, levels]
        weight[...] = (
            lsolar[...] + lground[row][None] - total * (kappa[row] + diffuse)[None]
        )
        light(row, levels)

    def lights(row, pair):
        light(row, 2 * pair)
        light(row, 2 * pair + 1)

    pairs = levels // 2

    def only_optical(pair, carry):
        optical(0, pair)
        return carry

    lax.fori_loop(0, pairs, only_optical, 0)

    def one_row(row, carry):
        close(row - 1)

        def both(pair, inner):
            optical(row, pair)
            lights(row - 1, pair)
            return inner

        return lax.fori_loop(0, pairs, both, carry)

    lax.fori_loop(1, ROWS, one_row, 0)
    close(ROWS - 1)

    def only_light(pair, carry):
        lights(ROWS - 1, pair)
        return carry

    lax.fori_loop(0, pairs, only_light, 0)

    scaled = heat_scale * cosine
    for row in range(ROWS):
        change = sums[row, 0:levels] - sums[row, 1 : levels + 1]
        heating[:, row, :] = jnp.sum(change, 1) * scaled[row : row + 1]

    def add(level, carry):
        state[0, level] = state[0, level] + heating[level]
        return carry

    lax.fori_loop(0, levels, add, 0)
    pack_fields(
        [lambda level, f=f: state[f, level] for f in range(ntr)], levels, head, tail
    )


def last_kernel(
    tracers,
    winds,
    right,
    left,
    north,
    south,
    wind_right,
    wind_left,
    wind_north,
    wind_south,
    inside,
    out,
    rim_ref,
    corner_ref,
    wind_rim_ref,
    wind_corner_ref,
):
    ntr, levels = tracers.shape[0], tracers.shape[1]
    fields = ntr + winds.shape[0]
    packed = packed_tiles(ntr, levels)
    wind_packed = packed_tiles(fields, levels)
    unpack_rows(north, south, rim_ref, corner_ref, ntr * levels, packed)
    unpack_rows(
        wind_north, wind_south, wind_rim_ref, wind_corner_ref, fields * levels, wind_packed
    )
    keep = inside[...]

    def transport(level, carry):
        rim = functools.partial(
            rim_tiles,
            level=level,
            levels=levels,
            packed=packed,
            right=right,
            left=left,
            rim_ref=rim_ref,
            corner_ref=corner_ref,
        )
        wind_rim = functools.partial(
            rim_tiles,
            level=level,
            levels=levels,
            packed=wind_packed,
            right=wind_right,
            left=wind_left,
            rim_ref=wind_rim_ref,
            corner_ref=wind_corner_ref,
        )
        east, north_face = faces(
            (winds[0, level], *wind_rim(ntr)), (winds[1, level], *wind_rim(ntr + 1))
        )
        for f in range(ntr):
            out[f, level] = two_steps((tracers[f, level], *rim(f)), east, north_face, keep)
        return carry

    lax.fori_loop(0, levels, transport, 0)


vmem = pl.BlockSpec(memory_space=pltpu.VMEM)
smem = pl.BlockSpec(memory_space=pltpu.SMEM)
f32 = jnp.float32


def tiles_like(*shape):
    return jax.ShapeDtypeStruct(shape, f32)


def shift(x, axis, by, wrap):
    count = lax.axis_size(axis)
    return lax.ppermute(
        x, axis, [(i, (i + by) % count) for i in range(count) if wrap or 0 <= i + by < count]
    )


def exchange_cols(head, tail):
    return shift(head, "lon", -1, True), shift(tail, "lon", 1, True)


def exchange_rows(fields, right, left, levels):
    count = sum(f.shape[0] for f in fields)
    rows = row_payload(count, levels)
    head, tail = pl.pallas_call(
        pack_rows_kernel,
        in_specs=[vmem] * (len(fields) + 2),
        out_specs=[vmem] * 2,
        out_shape=[tiles_like(rows, COLS)] * 2,
        name="pack_rows",
    )(*[f.reshape(-1, COLS) for f in fields], right, left)
    return shift(head, "lat", -1, False), shift(tail, "lat", 1, False)


def split3(x):
    hi = lax.reduce_precision(x, 8, 7)
    mid = lax.reduce_precision(x - hi, 8, 7)
    return [hi, mid, x - hi - mid]


def body(
    tracers,
    winds,
    gases,
    sun_index,
    block_slot,
    albedo,
    sun_table,
    solar,
    w_first,
    b_first,
    w_second,
    b_second,
    w_third,
    b_third,
):
    ntr, levels, clat, width = tracers.shape
    fields = ntr + winds.shape[0]
    gas = gases.shape[0]
    hid = w_first.shape[1]
    bands = solar.shape[0]
    if (clat, width) != (ROWS, COLS) or levels % 2 or SLOTS % levels or bands % ROWS:
        raise ValueError("unsupported sizes")

    head, tail = pl.pallas_call(
        pack_cols_kernel,
        in_specs=[vmem] * 2,
        out_specs=[vmem] * 2,
        out_shape=[tiles_like(packed_tiles(fields, levels), ROWS, COLS)] * 2,
        name="pack_cols",
    )(tracers, winds)
    right, left = exchange_cols(head, tail)
    north, south = exchange_rows((tracers, winds), right, left, levels)

    lat = lax.axis_index("lat")
    row = jnp.arange(ROWS)[:, None]
    inside = jnp.where(row == 0, lat < lax.axis_size("lat") - 1, (row == ROWS - 1) & (lat > 0))
    inside = jnp.broadcast_to(inside.astype(f32), (ROWS, COLS))
    gas_rows = gases.transpose(1, 0, 2, 3).reshape(levels, gas * ROWS, COLS)
    index = jnp.where(block_slot >= 0, sun_index, 0)
    ground = albedo.astype(f32)
    lsolar = jnp.broadcast_to(jnp.log2(solar)[:, None], (bands, COLS))
    lsolar = lsolar.reshape(bands // ROWS, ROWS, COLS)
    eye = jnp.eye(ROWS, dtype=jnp.bfloat16)
    w1 = (0.5 * w_first.T)[None, :, :, None] * eye[:, None, None, :]
    w1 = w1.reshape(ROWS * hid, -1).astype(jnp.bfloat16)
    b1 = jnp.broadcast_to(0.5 * b_first[:, None], (hid, COLS))
    w2 = (0.5 * w_second.T).astype(jnp.bfloat16)
    b2 = jnp.broadcast_to(0.5 * b_second[:, None], (hid, COLS))
    extra = [b[:, None].astype(jnp.bfloat16) for b in split3(b_third)]
    w3 = jnp.concatenate(
        [w_third.T, *extra, jnp.zeros((bands, 16 - len(extra)), jnp.bfloat16)], 1
    )

    packed = packed_tiles(fields, levels)
    state, heating, head, tail = pl.pallas_call(
        first_kernel,
        in_specs=[vmem] * 10 + [smem] + [vmem] * 6,
        out_specs=[vmem] * 4,
        out_shape=[
            tiles_like(ntr, levels, ROWS, COLS),
            tiles_like(levels, ROWS, COLS),
        ]
        + [tiles_like(packed_tiles(ntr, levels), ROWS, COLS)] * 2,
        scratch_shapes=[
            pltpu.VMEM((fields * levels * ROWS, COLS), f32),
            pltpu.VMEM((2 * packed, ROWS, COLS), f32),
            pltpu.VMEM((levels, ntr * ROWS, COLS), jnp.bfloat16),
            pltpu.VMEM((2, levels + 1, bands // ROWS, ROWS, COLS), f32),
            pltpu.VMEM((bands // ROWS, ROWS, COLS), f32),
            pltpu.VMEM((ROWS, levels + 1, ROWS, COLS), f32),
            pltpu.VMEM((ROWS, ROWS, COLS), f32),
            pltpu.VMEM((ROWS, ROWS, COLS), f32),
        ],
        name="transport_radiation",
    )(
        tracers,
        winds,
        right,
        left,
        north,
        south,
        inside,
        gas_rows,
        index,
        ground,
        sun_table,
        lsolar,
        w1,
        b1,
        w2,
        b2,
        w3,
    )

    right2, left2 = exchange_cols(head, tail)
    north2, south2 = exchange_rows((state,), right2, left2, levels)
    packed2 = packed_tiles(ntr, levels)
    final = pl.pallas_call(
        last_kernel,
        in_specs=[vmem] * 11,
        out_specs=vmem,
        out_shape=tiles_like(ntr, levels, ROWS, COLS),
        scratch_shapes=[
            pltpu.VMEM((ntr * levels * ROWS, COLS), f32),
            pltpu.VMEM((2 * packed2, ROWS, COLS), f32),
            pltpu.VMEM((fields * levels * ROWS, COLS), f32),
            pltpu.VMEM((2 * packed, ROWS, COLS), f32),
        ],
        name="last_transport",
    )(state, winds, right2, left2, north2, south2, right, left, north, south, inside)
    return final, heating


def solution(mesh):
    grid = P(None, None, "lat", "lon")
    in_specs = (grid, grid, grid) + (P("lat", "lon"),) * 3 + (P(),) * 8
    out_specs = (grid, P(None, "lat", "lon"))
    return jax.shard_map(body, mesh=mesh, in_specs=in_specs, out_specs=out_specs, check_vma=False)
```

time: 278 us -> 157 us (0.56); the launches traced: 274 us -> 157 us
  Pallas kernels: 0 us -> 116 us
  waiting for transfers between devices: 122 us -> 8.9 us
  other arithmetic: 77.9 us -> 1.99 us
  local copies, waits for them, and re-layouts: 25.9 us -> 9.88 us
  matrix products: 14.3 us -> 0 us
  starting transfers between devices: 32.3 us -> 19.4 us
    pallas_call x0 -> x5, Pallas kernels: none -> 116 us  [the longest x1 93.7 us: body(): pl.pallas_call(first_kernel, in_specs=[vmem] * 10 + [smem] + [vmem] * 6,...]
    ppermute x22 -> x8, waiting for transfers between devices: 122 us -> 8.9 us  [shift(): lax.ppermute(x, axis, [(i, (i + by) % count) for i in range(count) if wra...]
    reduce_sum x8 -> x0, other arithmetic: 47.6 us -> none  [the longest x4 47.2 us: radiate(): return heat_scale * jnp.sum(direct + upward, 0)]
    while x25 -> x0, local copies, waits for them, and re-layouts: 17.6 us -> none
    dot_general x10 -> x0, matrix products: 14.3 us -> none  [the longest x4 9.38 us: radiate(): jnp.dot(w_third.T, hidden, preferred_element_type=jnp.float32)]
    ppermute x22 -> x8, starting transfers between devices: 32.3 us -> 19.4 us  [shift(): lax.ppermute(x, axis, [(i, (i + by) % count) for i in range(count) if wra...]
    another operation x5 -> x1, other arithmetic: 8.56 us -> 0.01 us  [body(): lsolar = jnp.broadcast_to(jnp.log2(solar)[:, None], (bands, COLS))]
    mul x17 -> x5, other arithmetic: 9.11 us -> 0.71 us  [the longest x1 0.61 us: body(): w2 = (0.5 * w_second.T).astype(jnp.bfloat16)]
  transfers between devices with their start and end apart: 22 -> 8, of which waited for: 18 -> 6; matrix products, arithmetic and copies ran while one was open for 1% -> 3% of each run, Pallas kernels for 0% -> 0%
where the time goes in v1:
time: 157 us
  Pallas kernels  116 us (74%)
  starting transfers between devices  19.4 us (12%)
  local copies, waits for them, and re-layouts  9.88 us (6%)
  waiting for transfers between devices  8.9 us (6%)
  other arithmetic  1.99 us (1%)
    pallas_call x1, Pallas kernels, body(): pl.pallas_call(first_kernel, in_specs=[vmem] * 10 + [smem] + [vmem] * 6,...  93.7 us
    ppermute x8, starting transfers between devices, shift(): lax.ppermute(x, axis, [(i, (i + by) % count) for i in range(count) if wra...  19.4 us
    pallas_call x1, Pallas kernels, body(): pl.pallas_call(last_kernel, in_specs=[vmem] * 11, out_specs=vmem, out_sha...  14.1 us
    ppermute x8, waiting for transfers between devices, shift(): lax.ppermute(x, axis, [(i, (i + by) % count) for i in range(count) if wra...  8.9 us
    pallas_call x1, Pallas kernels, body(): pl.pallas_call(pack_cols_kernel, in_specs=[vmem] * 2, out_specs=[vmem] *...  4.4 us
    unnamed x40, local copies, waits for them, and re-layouts  3.96 us
    pallas_call x2, Pallas kernels, exchange_rows(): pl.pallas_call(pack_rows_kernel, in_specs=[vmem] * (len(fields) + 2), out...  3.77 us
  transfers between devices with their start and end apart: 8, of which 6 were waited for; matrix products, arithmetic and copies ran while one was open for 3% of the time, Pallas kernels for 0%

profile of v1, /device:TPU:1, one launch (start us, length us, event | category | flops | bytes accessed | tf_op | source)
XLA Modules:
  0.0 157.0 jit_solution(1684792830230052429)
XLA Ops:
  0.7 4.4 %pack_cols.1 = (f32[3,8,128]{2,1,0:T(8,128)}, f32[3,8,128]{2,1,0:T(8,128)}) custom-call(f32[4,32,8,128]{3,2,1,0:T(8,128)} %tracers.3, f32[2,32,8,128]{3,2,1,0:T(8,128)} %winds.5), custom_call_target="tpu_custom_call" | custom-call | tf_op jit(solution)/shard_map/pack_cols/pallas_call | solution.py:467
  5.1 3.0 %collective-permute-start = (f32[3,8,128]{2,1,0:T(8,128)}, f32[3,8,128]{2,1,0:T(8,128)S(1)}, u32[]{:S(2)}, u32[]{:S(2)}) collective-permute-start(f32[3,8,128]{2,1,0:T(8,128)} %get-tuple-element.12), channel_id=1, source_target_pairs={{0,24},{8,0},{16,8},{24,16},{1,25},{9,1},{17,9},{25,17},{2,26},{10... | collective-permute-start | bytes 36872 | tf_op jit(solution)/shard_map/ppermute | solution.py:415
  8.1 0.6 copy-done.17
  8.9 0.6 multiply_bitcast_fusion.w2
  9.5 1.0 copy_bitcast_fusion.gases
  10.5 0.7 broadcast_select_fusion.index
  11.9 0.6 convert_element_type.37.ground
  12.9 0.6 copy-done.9
  13.9 0.8 copy.26.w1
  14.6 0.8 concatenate.3.w3
  15.4 0.6 copy-done.5
  16.0 2.0 %pack_rows.2 = (f32[400,128]{1,0:T(8,128)}, f32[400,128]{1,0:T(8,128)}) custom-call(f32[1024,128]{1,0:T(8,128)} %bitcast.19, f32[512,128]{1,0:T(8,128)} %bitcast.20, f32[3,8,128]{2,1,0:T(8,128)} %copy-done.5, f32[3,8,128]{2,1,0:T(8,128)} %copy-done.6), custom_call_target="tpu_custom_call" | custom-call | tf_op jit(solution)/shard_map/pack_rows/pallas_call | solution.py:427
  18.0 3.0 %collective-permute-start.2 = (f32[400,128]{1,0:T(8,128)}, f32[400,128]{1,0:T(8,128)S(1)}, u32[]{:S(2)}, u32[]{:S(2)}) collective-permute-start(f32[400,128]{1,0:T(8,128)} %get-tuple-element.14), channel_id=1, source_target_pairs={{1,0},{2,1},{3,2},{4,3},{5,4},{6,5},{7,6},{9,8},{10,9},{11,10},{12... | collective-permute-start | bytes 614408 | tf_op jit(solution)/shard_map/ppermute | solution.py:415
  21.0 3.1 %collective-permute-start.3 = (f32[400,128]{1,0:T(8,128)}, f32[400,128]{1,0:T(8,128)S(1)}, u32[]{:S(2)}, u32[]{:S(2)}) collective-permute-start(f32[400,128]{1,0:T(8,128)} %get-tuple-element.15), channel_id=1, source_target_pairs={{0,1},{1,2},{2,3},{3,4},{4,5},{5,6},{6,7},{8,9},{9,10},{10,11},{11... | collective-permute-start | bytes 614408 | tf_op jit(solution)/shard_map/ppermute | solution.py:415
  24.1 1.7 %collective-permute-done.2.north.wind_north = f32[400,128]{1,0:T(8,128)S(1)} collective-permute-done((f32[400,128]{1,0:T(8,128)}, f32[400,128]{1,0:T(8,128)S(1)}, u32[]{:S(2)}, u32[]{:S(2)}) %collective-permute-start.2) | collective-permute-done | bytes 204832 | tf_op jit(solution)/shard_map/ppermute | solution.py:415
  25.8 1.3 collective-permute-done.3.south.wind_south
  27.1 0.7 broadcast_in_dim.31.inside
  27.8 0.7 broadcast_in_dim.60.b2
  28.4 0.7 broadcast_in_dim.59.b1
  29.1 0.7 broadcast_in_dim.58.lsolar
  29.9 93.7 %transport_radiation.1 = (f32[4,32,8,128]{3,2,1,0:T(8,128)}, f32[32,8,128]{2,1,0:T(8,128)}, f32[2,8,128]{2,1,0:T(8,128)}, f32[2,8,128]{2,1,0:T(8,128)}) custom-call(f32[4,32,8,128]{3,2,1,0:T(8,128)} %tracers.3, f32[2,32,8,128]{3,2,1,0:T(8,128)} %winds.5, f32[3,8,128]{2,1,0:T(8,128)} %copy-done.5, f32[3,8,128]{2,1,0:T(8,128)} %copy-done.6, ...), custom_call_target="tpu_custom_call" | custom-call | tf_op jit(solution)/shard_map/transport_radiation/pallas_call | solution.py:498
  123.5 2.7 %collective-permute-start.4 = (f32[2,8,128]{2,1,0:T(8,128)}, f32[2,8,128]{2,1,0:T(8,128)S(1)}, u32[]{:S(2)}, u32[]{:S(2)}) collective-permute-start(f32[2,8,128]{2,1,0:T(8,128)} %get-tuple-element.17), channel_id=1, source_target_pairs={{0,24},{8,0},{16,8},{24,16},{1,25},{9,1},{17,9},{25,17},{2,26},{10... | collective-permute-start | bytes 24584 | tf_op jit(solution)/shard_map/ppermute | solution.py:415
  126.2 1.0 collective-permute-done.4.refs_1_.right
  127.2 2.6 %collective-permute-done.5.refs_2_.left = f32[2,8,128]{2,1,0:T(8,128)S(1)} collective-permute-done((f32[2,8,128]{2,1,0:T(8,128)}, f32[2,8,128]{2,1,0:T(8,128)S(1)}, u32[]{:S(2)}, u32[]{:S(2)}) %collective-permute-start.5) | collective-permute-done | bytes 8224 | tf_op jit(solution)/shard_map/ppermute | solution.py:415
  129.8 0.6 copy-done.8
  130.4 1.8 %pack_rows.3 = (f32[272,128]{1,0:T(8,128)}, f32[272,128]{1,0:T(8,128)}) custom-call(f32[1024,128]{1,0:T(8,128)} %bitcast.21, f32[2,8,128]{2,1,0:T(8,128)} %copy-done.7, f32[2,8,128]{2,1,0:T(8,128)} %copy-done.8), custom_call_target="tpu_custom_call" | custom-call | tf_op jit(solution)/shard_map/pack_rows/pallas_call | solution.py:427
  132.2 1.9 %collective-permute-start.6 = (f32[272,128]{1,0:T(8,128)}, f32[272,128]{1,0:T(8,128)S(1)}, u32[]{:S(2)}, u32[]{:S(2)}) collective-permute-start(f32[272,128]{1,0:T(8,128)} %get-tuple-element.19), channel_id=1, source_target_pairs={{1,0},{2,1},{3,2},{4,3},{5,4},{6,5},{7,6},{9,8},{10,9},{11,10},{12... | collective-permute-start | bytes 417800 | tf_op jit(solution)/shard_map/ppermute | solution.py:415
  134.1 5.7 %collective-permute-start.7 = (f32[272,128]{1,0:T(8,128)}, f32[272,128]{1,0:T(8,128)S(1)}, u32[]{:S(2)}, u32[]{:S(2)}) collective-permute-start(f32[272,128]{1,0:T(8,128)} %get-tuple-element.20), channel_id=1, source_target_pairs={{0,1},{1,2},{2,3},{3,4},{4,5},{5,6},{6,7},{8,9},{9,10},{10,11},{11... | collective-permute-start | bytes 417800 | tf_op jit(solution)/shard_map/ppermute | solution.py:415
  139.8 1.0 collective-permute-done.6.north
  140.9 1.3 collective-permute-done.7.south
  142.2 0.7 copy-done.4
  142.8 14.1 %last_transport.1 = f32[4,32,8,128]{3,2,1,0:T(8,128)} custom-call(f32[4,32,8,128]{3,2,1,0:T(8,128)} %get-tuple-element.16.tracers, f32[2,32,8,128]{3,2,1,0:T(8,128)} %winds.5, f32[2,8,128]{2,1,0:T(8,128)} %copy-done.7, f32[2,8,128]{2,1,0:T(8,128)} %copy-done.8, f32[272,128]{1,0:T(8,128)} %copy-done.3, f32[272,128]{1,0:T(8,128)} %copy-done.4, ...), custom_call_target="tpu_custom_call" | custom-call | tf_op jit(solution)/shard_map/last_transport/pallas_call | solution.py:541
  (54 shorter events, 1.6 us)
Async XLA Ops:
  0.6 8.9 %copy-start = (bf16[12,32,8,128]{3,2,1,0:T(8,128)(2,1)S(1)}, bf16[12,32,8,128]{3,2,1,0:T(8,128)(2,1)}, u32[]{:S(2)}) copy-start(bf16[12,32,8,128]{3,2,1,0:T(8,128)(2,1)} %param.16) | copy-start | bytes 2359300
  0.6 7.4 %copy-start.16 = (s32[8,1]{0,1:T(1,128)S(1)}, s32[8,1]{0,1:T(1,128)}, u32[]{:S(2)}) copy-start(s32[8,1]{0,1:T(1,128)} %param.18) | copy-start | bytes 100
  5.1 3.7 %copy-start.10 = (bf16[64,64]{1,0:T(8,128)(2,1)S(1)}, bf16[64,64]{1,0:T(8,128)(2,1)}, u32[]{:S(2)}) copy-start(bf16[64,64]{1,0:T(8,128)(2,1)} %param.24) | copy-start | bytes 24580
  5.1 10.4 %collective-permute-start = (f32[3,8,128]{2,1,0:T(8,128)}, f32[3,8,128]{2,1,0:T(8,128)S(1)}, u32[]{:S(2)}, u32[]{:S(2)}) collective-permute-start(f32[3,8,128]{2,1,0:T(8,128)} %get-tuple-element.12), channel_id=1, source_target_pairs={{0,24},{8,0},{16,8},{24,16},{1,25},{9,1},{17,9},{25,17},{2,26},{10... | collective-permute-start | bytes 36872 | tf_op jit(solution)/shard_map/ppermute | solution.py:415
  8.0 7.4 %collective-permute-start.1 = (f32[3,8,128]{2,1,0:T(8,128)}, f32[3,8,128]{2,1,0:T(8,128)S(1)}, u32[]{:S(2)}, u32[]{:S(2)}) collective-permute-start(f32[3,8,128]{2,1,0:T(8,128)} %get-tuple-element.13), channel_id=1, source_target_pairs={{0,8},{8,16},{16,24},{24,0},{1,9},{9,17},{17,25},{25,1},{2,10},{10... | collective-permute-start | bytes 36872 | tf_op jit(solution)/shard_map/ppermute | solution.py:415
  8.0 0.7 copy-start.17
  8.1 0.7 copy-start.14
  8.1 0.7 copy-start.15
  8.1 0.7 copy-start.11
  9.5 1.0 copy-start.12
  11.2 0.7 copy-start.13
  12.8 0.8 copy-start.9
  15.4 0.6 copy-start.5
  15.4 0.6 copy-start.6
  18.0 6.1 %copy-start.18 = (f32[64]{0:T(128)S(1)}, f32[64]{0:T(128)}, u32[]{:S(2)}) copy-start(f32[64]{0:T(128)} %param.25) | copy-start | bytes 772
  18.0 7.8 %collective-permute-start.2 = (f32[400,128]{1,0:T(8,128)}, f32[400,128]{1,0:T(8,128)S(1)}, u32[]{:S(2)}, u32[]{:S(2)}) collective-permute-start(f32[400,128]{1,0:T(8,128)} %get-tuple-element.14), channel_id=1, source_target_pairs={{1,0},{2,1},{3,2},{4,3},{5,4},{6,5},{7,6},{9,8},{10,9},{11,10},{12... | collective-permute-start | bytes 614408 | tf_op jit(solution)/shard_map/ppermute | solution.py:415
  21.0 6.1 %collective-permute-start.3 = (f32[400,128]{1,0:T(8,128)}, f32[400,128]{1,0:T(8,128)S(1)}, u32[]{:S(2)}, u32[]{:S(2)}) collective-permute-start(f32[400,128]{1,0:T(8,128)} %get-tuple-element.15), channel_id=1, source_target_pairs={{0,1},{1,2},{2,3},{3,4},{4,5},{5,6},{6,7},{8,9},{9,10},{10,11},{11... | collective-permute-start | bytes 614408 | tf_op jit(solution)/shard_map/ppermute | solution.py:415
  25.8 4.1 %copy-start.1 = (f32[400,128]{1,0:T(8,128)}, f32[400,128]{1,0:T(8,128)S(1)}, u32[]{:S(2)}) copy-start(f32[400,128]{1,0:T(8,128)S(1)} %collective-permute-done.2.north.wind_north) | copy-start | bytes 614404
  27.1 2.8 %copy-start.2 = (f32[400,128]{1,0:T(8,128)}, f32[400,128]{1,0:T(8,128)S(1)}, u32[]{:S(2)}) copy-start(f32[400,128]{1,0:T(8,128)S(1)} %collective-permute-done.3.south.wind_south) | copy-start | bytes 614404
  123.5 3.7 %collective-permute-start.4 = (f32[2,8,128]{2,1,0:T(8,128)}, f32[2,8,128]{2,1,0:T(8,128)S(1)}, u32[]{:S(2)}, u32[]{:S(2)}) collective-permute-start(f32[2,8,128]{2,1,0:T(8,128)} %get-tuple-element.17), channel_id=1, source_target_pairs={{0,24},{8,0},{16,8},{24,16},{1,25},{9,1},{17,9},{25,17},{2,26},{10... | collective-permute-start | bytes 24584 | tf_op jit(solution)/shard_map/ppermute | solution.py:415
  126.2 3.6 %collective-permute-start.5 = (f32[2,8,128]{2,1,0:T(8,128)}, f32[2,8,128]{2,1,0:T(8,128)S(1)}, u32[]{:S(2)}, u32[]{:S(2)}) collective-permute-start(f32[2,8,128]{2,1,0:T(8,128)} %get-tuple-element.18), channel_id=1, source_target_pairs={{0,8},{8,16},{16,24},{24,0},{1,9},{9,17},{17,25},{25,1},{2,10},{10... | collective-permute-start | bytes 24584 | tf_op jit(solution)/shard_map/ppermute | solution.py:415
  127.2 2.6 %copy-start.7 = (f32[2,8,128]{2,1,0:T(8,128)}, f32[2,8,128]{2,1,0:T(8,128)S(1)}, u32[]{:S(2)}) copy-start(f32[2,8,128]{2,1,0:T(8,128)S(1)} %collective-permute-done.4.refs_1_.right) | copy-start | bytes 24580
  129.8 0.6 copy-start.8
  132.2 8.6 %collective-permute-start.6 = (f32[272,128]{1,0:T(8,128)}, f32[272,128]{1,0:T(8,128)S(1)}, u32[]{:S(2)}, u32[]{:S(2)}) collective-permute-start(f32[272,128]{1,0:T(8,128)} %get-tuple-element.19), channel_id=1, source_target_pairs={{1,0},{2,1},{3,2},{4,3},{5,4},{6,5},{7,6},{9,8},{10,9},{11,10},{12... | collective-permute-start | bytes 417800 | tf_op jit(solution)/shard_map/ppermute | solution.py:415
  134.1 8.0 %collective-permute-start.7 = (f32[272,128]{1,0:T(8,128)}, f32[272,128]{1,0:T(8,128)S(1)}, u32[]{:S(2)}, u32[]{:S(2)}) collective-permute-start(f32[272,128]{1,0:T(8,128)} %get-tuple-element.20), channel_id=1, source_target_pairs={{0,1},{1,2},{2,3},{3,4},{4,5},{5,6},{6,7},{8,9},{9,10},{10,11},{11... | collective-permute-start | bytes 417800 | tf_op jit(solution)/shard_map/ppermute | solution.py:415
  140.8 1.3 copy-start.3
  142.2 0.7 copy-start.4

commit v2 on v1

v2 whole, which is shorter than its diff:
```python
import functools
import math

import jax
import jax.numpy as jnp
from jax import lax
from jax.experimental import pallas as pl
from jax.experimental.pallas import tpu as pltpu
from jax.sharding import PartitionSpec as P

tau_scale = 0.05
mu_floor = 0.05
heat_scale = 30.0
diffuse_factor = 1.66
log2e = 1.4426950408889634

ROWS = 8
COLS = 128
RIM = 2
SLOTS = COLS // RIM


def lane_id():
    return lax.broadcasted_iota(jnp.int32, (ROWS, COLS), 1)


def row_id():
    return lax.broadcasted_iota(jnp.int32, (ROWS, COLS), 0)


def ahead_col(tile, beside):
    return pltpu.roll(jnp.where(lane_id() == 0, beside, tile), COLS - 1, 1)


def behind_col(tile, beside):
    return pltpu.roll(jnp.where(lane_id() == COLS - 1, beside, tile), 1, 1)


def ahead_row(tile, beside):
    return pltpu.roll(jnp.where(row_id() == 0, beside, tile), ROWS - 1, 0)


def behind_row(tile, beside):
    return pltpu.roll(jnp.where(row_id() == ROWS - 1, beside, tile), 1, 0)


def flux(face, here, there):
    return jnp.maximum(face, 0.0) * here + jnp.minimum(face, 0.0) * there


def faces(along, across):
    am, ah, av, ac = along
    bm, bh, bv, bc = across
    east = tuple(
        0.5 * (t + ahead_col(t, o)) for t, o in ((am, ah), (ah, am), (av, ac), (ac, av))
    )
    north = tuple(
        0.5 * (t + ahead_row(t, o)) for t, o in ((bm, bv), (bh, bc), (bv, bm), (bc, bh))
    )
    return east, north


def two_steps(q, east, north, inside):
    m, h, v, c = q
    em = flux(east[0], m, ahead_col(m, h))
    eh = flux(east[1], h, ahead_col(h, m))
    ev = flux(east[2], v, ahead_col(v, c))
    ec = flux(east[3], c, ahead_col(c, v))
    nm = flux(north[0], m, ahead_row(m, v))
    nh = flux(north[1], h, ahead_row(h, c))
    nv = flux(north[2], v, ahead_row(v, m))
    nc = flux(north[3], c, ahead_row(c, h))
    m1 = m - (em - behind_col(em, eh)) - (nm - behind_row(nm, nv))
    h1 = h - (eh - behind_col(eh, em)) - (nh - behind_row(nh, nc))
    v1 = v - (ev - behind_col(ev, ec)) - (nv - behind_row(nv, nm))
    v1 = jnp.where(inside > 0.0, v1, 0.0)
    em = flux(east[0], m1, ahead_col(m1, h1))
    eh = flux(east[1], h1, ahead_col(h1, m1))
    nm = flux(north[0], m1, ahead_row(m1, v1))
    nv = flux(north[2], v1, ahead_row(v1, m1))
    return m1 - (em - behind_col(em, eh)) - (nm - behind_row(nm, nv))


def pack_sides(tile, slot, packs):
    head, tail = packs
    lane = lane_id()
    here = (lane >= RIM * slot) & (lane < RIM * slot + RIM)
    head = jnp.where(here, pltpu.roll(tile, RIM * slot, 1), head)
    tail = jnp.where(here, pltpu.roll(tile, lax.rem(RIM * slot + RIM, COLS), 1), tail)
    return head, tail


def unpack_sides(from_right, from_left, slot):
    right = pltpu.roll(from_right, lax.rem(COLS - RIM * slot, COLS), 1)
    left = pltpu.roll(from_left, lax.rem(2 * COLS - RIM - RIM * slot, COLS), 1)
    return jnp.where(lane_id() < COLS // 2, right, left)


def tile_at(tile):
    return pl.ds(pl.multiple_of(tile * ROWS, ROWS), ROWS)


def kept_rows(edges):
    after = (row_id() == 0) & (edges[0] > 0)
    before = (row_id() == ROWS - 1) & (edges[1] > 0)
    return jnp.where(after | before, 1.0, 0.0)


def each_level(levels, step, carry, block):
    def trip(at, carry):
        for k in range(block):
            carry = step(block * at + k, carry)
        return carry

    return lax.fori_loop(0, levels // block, trip, carry)


def place(field, level, levels):
    per = SLOTS // levels
    return field // per, (field % per) * levels + level


def packed_tiles(fields, levels):
    return pl.cdiv(fields * levels, SLOTS)


def pack_fields(sources, levels, head_ref, tail_ref):
    count = packed_tiles(len(sources), levels)
    zero = jnp.zeros((ROWS, COLS), jnp.float32)

    def step(level, packs):
        packs = list(packs)
        for field, source in enumerate(sources):
            tile, slot = place(field, level, levels)
            packs[tile] = pack_sides(source(level), slot, packs[tile])
        return tuple(packs)

    packs = each_level(levels, step, ((zero, zero),) * count, 8)
    for tile, (head, tail) in enumerate(packs):
        head_ref[tile] = head
        tail_ref[tile] = tail


def pack_rows(sources, head, tail):
    at = 0
    total = sum(ref.shape[0] for ref in sources) // ROWS
    for ref in sources:
        tiles = ref.shape[0] // ROWS
        for row in range(RIM):
            head[pl.ds(row * total + at, tiles), :] = ref[pl.ds(row, tiles, stride=ROWS), :]
            tail[pl.ds(row * total + at, tiles), :] = ref[
                pl.ds(ROWS - RIM + row, tiles, stride=ROWS), :
            ]
        at += tiles


def row_payload(fields, levels):
    rows = RIM * fields * levels + 2 * RIM * packed_tiles(fields, levels)
    return -(-rows // 16) * 16


def pack_kernel(levels, tracers, winds, head, tail, head_rows, tail_rows):
    sources = []
    for ref in (tracers, winds):
        for f in range(ref.shape[0] // (levels * ROWS)):
            base = f * levels * ROWS
            sources.append(
                lambda level, ref=ref, base=base: ref[
                    pl.ds(pl.multiple_of(base + level * ROWS, ROWS), ROWS), :
                ]
            )
    pack_rows((tracers, winds), head_rows, tail_rows)
    pack_fields(sources, levels, head, tail)


def corner_kernel(head_in, tail_in, from_right, from_left, head, tail, near, far, sems):
    del head_in, tail_in
    near[...] = jnp.zeros(near.shape, jnp.float32)
    far[...] = jnp.zeros(far.shape, jnp.float32)
    at = 0
    for ref in (from_right, from_left):
        for tile in range(ref.shape[0]):
            near[at : at + RIM, :] = ref[tile, 0:RIM, :]
            far[at : at + RIM, :] = ref[tile, ROWS - RIM : ROWS, :]
            at += RIM
    base = head.shape[0] - near.shape[0]
    copies = [
        pltpu.make_async_copy(block, whole.at[pl.ds(base, near.shape[0])], sems.at[k])
        for k, (block, whole) in enumerate(((near, head), (far, tail)))
    ]
    for copy in copies:
        copy.start()
    for copy in copies:
        copy.wait()


def unpack_rows(from_north, from_south, rim_ref, corner_ref, tiles, packed):
    for row in range(RIM):
        rim_ref[pl.ds(row, tiles, stride=ROWS), :] = from_north[pl.ds(row * tiles, tiles), :]
        rim_ref[pl.ds(ROWS - RIM + row, tiles, stride=ROWS), :] = from_south[
            pl.ds(row * tiles, tiles), :
        ]
    at = RIM * tiles
    for tile in range(2 * packed):
        corner_ref[tile, 0:RIM, :] = from_north[at : at + RIM, :]
        corner_ref[tile, ROWS - RIM : ROWS, :] = from_south[at : at + RIM, :]
        at += RIM


def rim_tiles(field, level, levels, packed, right, left, rim_ref, corner_ref):
    tile, slot = place(field, level, levels)
    side = unpack_sides(right[tile], left[tile], slot)
    row = pl.multiple_of((field * levels + level) * ROWS, ROWS)
    rows = rim_ref[pl.ds(row, ROWS), :]
    corner = unpack_sides(corner_ref[tile], corner_ref[packed + tile], slot)
    return side, rows, corner


def first_kernel(
    tracers,
    winds,
    right,
    left,
    north,
    south,
    edges,
    gases,
    w1,
    b1,
    w2,
    b2,
    w3,
    lsolar,
    kappa,
    lground,
    scaled,
    state,
    heating,
    head,
    tail,
    head_rows,
    tail_rows,
    face,
    rim_ref,
    corner_ref,
    xs,
    hid_a,
    hid_b,
    hidden,
    logits,
    depth_a,
    depth_b,
    weight,
    sums,
):
    depths = (depth_a, depth_b)
    ntr, levels = tracers.shape[0], tracers.shape[1]
    fields = ntr + winds.shape[0]
    packed = packed_tiles(fields, levels)
    groups = lsolar.shape[0]
    hid = b1.shape[0]
    unpack_rows(north, south, rim_ref, corner_ref, fields * levels, packed)
    keep = kept_rows(edges)

    def transport(level, carry):
        rim = functools.partial(
            rim_tiles,
            level=level,
            levels=levels,
            packed=packed,
            right=right,
            left=left,
            rim_ref=rim_ref,
            corner_ref=corner_ref,
        )
        east, north_face = faces(
            (winds[0, level], *rim(ntr)), (winds[1, level], *rim(ntr + 1))
        )
        face[level] = jnp.stack([*east, *north_face])
        out = []
        for f in range(ntr):
            q = two_steps((tracers[f, level], *rim(f)), east, north_face, keep)
            state[tile_at(f * levels + level), :] = q
            out.append(q)
        xs[level] = jnp.concatenate(out, 0).astype(jnp.bfloat16)
        return carry

    each_level(levels, transport, 0, 4)

    diffuse = diffuse_factor * tau_scale
    pairs = levels // 2
    depths[0][0] = jnp.zeros((groups, ROWS, COLS), jnp.float32)
    depths[1][0] = jnp.zeros((groups, ROWS, COLS), jnp.float32)
    ones = jnp.ones((w3.shape[1] - hid, 2 * COLS), jnp.bfloat16)

    def silu(half):
        return (half + half * jnp.tanh(half)).astype(jnp.bfloat16)

    def layer_one(pair, out):
        x = jnp.concatenate(
            [jnp.concatenate([gases[2 * pair + k], xs[2 * pair + k]], 0) for k in range(2)], 1
        )
        wide = jnp.concatenate([b1[...]] * 2, 1)
        part = ROWS // 2
        for at in range(0, ROWS, part):
            mine = w1[at * hid : (at + part) * hid, :]
            y = jnp.dot(mine, x, preferred_element_type=jnp.float32)
            for k in range(part):
                out[(at + k) * hid : (at + k + 1) * hid, :] = silu(
                    y[k * hid : (k + 1) * hid] + wide
                )

    def layer_two(pair, source, at=lambda row, pair: row * pairs + pair):
        wide = jnp.concatenate([b2[...]] * 2, 1)
        for row in range(ROWS):
            y = source[row * hid : (row + 1) * hid, :]
            y = silu(jnp.dot(w2[...], y, preferred_element_type=jnp.float32) + wide)
            hidden[at(row, pair)] = jnp.concatenate([y, ones], 0)

    def layers(step, carry):
        layer_one(2 * step, hid_a)

        layer_two(
            2 * step - 1,
            hid_b,
            lambda row, pair: jnp.where(step == 0, ROWS * pairs, row * pairs + pair),
        )

        layer_one(2 * step + 1, hid_b)
        layer_two(2 * step, hid_a)
        return carry

    lax.fori_loop(0, pairs // 2, layers, 0)
    layer_two(pairs - 1, hid_b)

    def third(at):
        logits[...] = jnp.dot(w3[...], hidden[at], preferred_element_type=jnp.float32).reshape(
            groups, ROWS, 2 * COLS
        )

    def optical(pair, depth):
        t = logits[...] * log2e
        soft = jnp.maximum(t, jnp.log2(1.0 + jnp.exp2(jnp.minimum(t, 126.0))))
        d = depth[2 * pair] + soft[:, :, :COLS]
        depth[2 * pair + 1] = d
        depth[2 * pair + 2] = d + soft[:, :, COLS:]

    def light(row, level, depth):
        d = depth[level]
        direct = jnp.exp2(lsolar[...] - d * kappa[row][None])
        upward = jnp.exp2(weight[...] + d * diffuse)
        sums[row, level] = jnp.sum(direct - upward, 0)

    def close(row, depth):
        total = depth[levels]
        weight[...] = (
            lsolar[...] + lground[row][None] - total * (kappa[row] + diffuse)[None]
        )
        light(row, levels, depth)

    def both(row, depth, before):
        close(row - 1, before)

        def step(pair, carry):
            optical(pair, depth)
            light(row - 1, 2 * pair, before)
            light(row - 1, 2 * pair + 1, before)
            third(row * pairs + pair + 1)
            return carry

        lax.fori_loop(0, pairs, step, 0)

    def only_optical(pair, carry):
        optical(pair, depths[0])
        third(pair + 1)
        return carry

    third(0)
    lax.fori_loop(0, pairs, only_optical, 0)

    def two_rows(step, carry):
        both(2 * step + 1, depths[1], depths[0])
        both(2 * step + 2, depths[0], depths[1])
        return carry

    lax.fori_loop(0, ROWS // 2 - 1, two_rows, 0)
    both(ROWS - 1, depths[1], depths[0])
    close(ROWS - 1, depths[1])

    def only_light(pair, carry):
        light(ROWS - 1, 2 * pair, depths[1])
        light(ROWS - 1, 2 * pair + 1, depths[1])
        return carry

    lax.fori_loop(0, pairs, only_light, 0)

    for row in range(ROWS):
        change = sums[row, 0:levels] - sums[row, 1 : levels + 1]
        heating[:, row, :] = jnp.sum(change, 1) * scaled[row : row + 1, :]

    def add(level, carry):
        tile = tile_at(level)
        state[tile, :] = state[tile, :] + heating[level]
        return carry

    each_level(levels, add, 0, 8)
    pack_rows((state,), head_rows, tail_rows)
    pack_fields(
        [lambda level, f=f: state[tile_at(f * levels + level), :] for f in range(ntr)],
        levels,
        head,
        tail,
    )


def last_kernel(tracers, face, right, left, north, south, edges, out, rim_ref, corner_ref):
    ntr, levels = out.shape[0], out.shape[1]
    packed = packed_tiles(ntr, levels)
    unpack_rows(north, south, rim_ref, corner_ref, ntr * levels, packed)
    keep = kept_rows(edges)

    def transport(level, carry):
        rim = functools.partial(
            rim_tiles,
            level=level,
            levels=levels,
            packed=packed,
            right=right,
            left=left,
            rim_ref=rim_ref,
            corner_ref=corner_ref,
        )
        tiles = [face[level, k] for k in range(8)]
        for f in range(ntr):
            q = tracers[tile_at(f * levels + level), :]
            out[f, level] = two_steps((q, *rim(f)), tiles[:4], tiles[4:], keep)
        return carry

    each_level(levels, transport, 0, 4)


def prepare_kernel(
    index,
    slot,
    ground,
    table,
    solar,
    w_first,
    b_first,
    w_second,
    b_second,
    w_third,
    b_third,
    w1,
    b1,
    w2,
    b2,
    w3,
    lsolar,
    kappa,
    lground,
    scaled,
    square,
    wide,
):
    feat, hid = w_first.shape
    bands = solar.shape[1]

    def column(ref, factor):
        square[:, 0 : ref.shape[1]] = jnp.broadcast_to(ref[...], (COLS, ref.shape[1])) * factor
        return jnp.transpose(square[...])[0 : ref.shape[1]]

    square[...] = jnp.zeros(square.shape, jnp.float32)
    b1[...] = column(b_first, 0.5)
    b2[...] = column(b_second, 0.5)

    square[...] = jnp.zeros(square.shape, jnp.float32)
    square[0:hid, 0:hid] = w_second[...].astype(jnp.float32) * 0.5
    w2[...] = jnp.transpose(square[...])[0:hid, 0:hid].astype(jnp.bfloat16)

    square[...] = jnp.zeros(square.shape, jnp.float32)
    square[0:feat, 0:hid] = w_first[...].astype(jnp.float32) * 0.5
    by_unit = jnp.transpose(square[...])[0:hid].astype(jnp.bfloat16)
    source = lax.broadcasted_iota(jnp.int32, (COLS, COLS), 0)
    lane = lax.broadcasted_iota(jnp.int32, (COLS, COLS), 1)
    spread = jnp.where(lane // ROWS == source, 1.0, 0.0).astype(jnp.bfloat16)
    by_lane = jnp.dot(by_unit, spread, preferred_element_type=jnp.float32)
    of_row = lax.broadcasted_iota(jnp.int32, (hid, COLS), 1) % ROWS
    for row in range(ROWS):
        w1[row * hid : (row + 1) * hid, :] = jnp.where(of_row == row, by_lane, 0.0).astype(
            jnp.bfloat16
        )

    wide[...] = jnp.zeros(wide.shape, jnp.float32)
    wide[0:hid, 0:bands] = w_third[...].astype(jnp.float32)
    rest = b_third[...]
    for k in range(3):
        part = rest.astype(jnp.bfloat16).astype(jnp.float32)
        wide[hid + k : hid + k + 1, 0:bands] = part
        rest = rest - part
    w3[...] = jnp.transpose(wide[...])[0:bands, 0 : w3.shape[1]].astype(jnp.bfloat16)

    wide[:, 0:bands] = jnp.broadcast_to(jnp.log2(solar[...]), (COLS, bands))
    lsolar[...] = jnp.transpose(wide[...])[0:bands].reshape(lsolar.shape)

    ids = index[...]
    cosine = jnp.zeros((ROWS, COLS), jnp.float32)
    for entry in range(1, table.shape[0]):
        cosine = jnp.where(ids == entry, table[entry], cosine)
    slant = tau_scale / jnp.maximum(cosine, mu_floor)
    lg = jnp.log2(ground[...].astype(jnp.float32))
    for row in range(ROWS):
        kappa[row] = jnp.broadcast_to(slant[row : row + 1], (ROWS, COLS))
        lground[row] = jnp.broadcast_to(lg[row : row + 1], (ROWS, COLS))
        lit = jnp.where(slot[0, row] >= 0, heat_scale, 0.0)
        scaled[row : row + 1, :] = lit * cosine[row : row + 1]


vmem = pl.BlockSpec(memory_space=pltpu.VMEM)
smem = pl.BlockSpec(memory_space=pltpu.SMEM)
f32 = jnp.float32


def tiles_like(*shape):
    return jax.ShapeDtypeStruct(shape, f32)


def shift(x, axis, by, wrap):
    count = lax.axis_size(axis)
    return lax.ppermute(
        x, axis, [(i, (i + by) % count) for i in range(count) if wrap or 0 <= i + by < count]
    )


def exchange_cols(head, tail):
    return shift(head, "lon", -1, True), shift(tail, "lon", 1, True)


def exchange_rows(head, tail, right, left):
    any_space = pl.BlockSpec(memory_space=pl.ANY)
    spare = -(-2 * RIM * right.shape[0] // 16) * 16
    head, tail = pl.pallas_call(
        corner_kernel,
        in_specs=[any_space] * 2 + [vmem] * 2,
        out_specs=[any_space] * 2,
        out_shape=[tiles_like(*head.shape)] * 2,
        input_output_aliases={0: 0, 1: 1},
        scratch_shapes=[pltpu.VMEM((spare, COLS), f32)] * 2 + [pltpu.SemaphoreType.DMA((2,))],
        name="add_corners",
    )(head, tail, right, left)
    return shift(head, "lat", -1, False), shift(tail, "lat", 1, False)


def body(
    tracers,
    winds,
    gases,
    sun_index,
    block_slot,
    albedo,
    sun_table,
    solar,
    w_first,
    b_first,
    w_second,
    b_second,
    w_third,
    b_third,
):
    ntr, levels, clat, width = tracers.shape
    fields = ntr + winds.shape[0]
    gas = gases.shape[0]
    hid = w_first.shape[1]
    bands = solar.shape[0]
    if (clat, width) != (ROWS, COLS) or w_first.shape[0] * ROWS != COLS or levels % 8 or SLOTS % levels or bands % ROWS:
        raise ValueError("unsupported sizes")

    flat = (tracers.reshape(-1, COLS), winds.reshape(-1, COLS))
    columns = tiles_like(packed_tiles(fields, levels), ROWS, COLS)
    head, tail, head_rows, tail_rows = pl.pallas_call(
        functools.partial(pack_kernel, levels),
        in_specs=[vmem] * 2,
        out_specs=[vmem] * 4,
        out_shape=[columns] * 2 + [tiles_like(row_payload(fields, levels), COLS)] * 2,
        name="pack",
    )(*flat)
    right, left = exchange_cols(head, tail)

    groups = bands // ROWS
    bf16 = jnp.bfloat16
    prepared = pl.pallas_call(
        prepare_kernel,
        in_specs=[vmem, smem, vmem, smem] + [vmem] * 7,
        out_specs=[vmem] * 9,
        out_shape=[
            jax.ShapeDtypeStruct((ROWS * hid, w_first.shape[0] * ROWS), bf16),
            tiles_like(hid, COLS),
            jax.ShapeDtypeStruct((hid, hid), bf16),
            tiles_like(hid, COLS),
            jax.ShapeDtypeStruct((bands, hid + 16), bf16),
            tiles_like(groups, ROWS, COLS),
            tiles_like(ROWS, ROWS, COLS),
            tiles_like(ROWS, ROWS, COLS),
            tiles_like(ROWS, COLS),
        ],
        scratch_shapes=[
            pltpu.VMEM((COLS, COLS), f32),
            pltpu.VMEM((COLS, pl.cdiv(bands, COLS) * COLS), f32),
        ],
        name="prepare",
    )(
        sun_index,
        block_slot.reshape(1, -1),
        albedo,
        sun_table,
        solar.reshape(1, -1),
        w_first,
        b_first.reshape(1, -1),
        w_second,
        b_second.reshape(1, -1),
        w_third,
        b_third.reshape(1, -1),
    )
    gas_rows = gases.transpose(1, 0, 2, 3).reshape(levels, gas * ROWS, COLS)
    lat = lax.axis_index("lat")
    edges = jnp.stack([lat < lax.axis_size("lat") - 1, lat > 0]).astype(jnp.int32)
    right, left, prepared, gas_rows = lax.optimization_barrier((right, left, prepared, gas_rows))
    north, south = exchange_rows(head_rows, tail_rows, right, left)

    packed = packed_tiles(fields, levels)
    state, heating, head, tail, head_rows, tail_rows, face = pl.pallas_call(
        first_kernel,
        in_specs=[vmem] * 6 + [smem] + [vmem] * 10,
        out_specs=[vmem] * 7,
        out_shape=[
            tiles_like(ntr * levels * ROWS, COLS),
            tiles_like(levels, ROWS, COLS),
        ]
        + [tiles_like(packed_tiles(ntr, levels), ROWS, COLS)] * 2
        + [tiles_like(row_payload(ntr, levels), COLS)] * 2
        + [tiles_like(levels, 8, ROWS, COLS)],
        scratch_shapes=[
            pltpu.VMEM((fields * levels * ROWS, COLS), f32),
            pltpu.VMEM((2 * packed, ROWS, COLS), f32),
            pltpu.VMEM((levels, ntr * ROWS, COLS), bf16),
            pltpu.VMEM((ROWS * hid, 2 * COLS), bf16),
            pltpu.VMEM((ROWS * hid, 2 * COLS), bf16),
            pltpu.VMEM((ROWS * levels // 2 + 1, hid + 16, 2 * COLS), bf16),
            pltpu.VMEM((groups, ROWS, 2 * COLS), f32),
            pltpu.VMEM((levels + 1, groups, ROWS, COLS), f32),
            pltpu.VMEM((levels + 1, groups, ROWS, COLS), f32),
            pltpu.VMEM((groups, ROWS, COLS), f32),
            pltpu.VMEM((ROWS, levels + 1, ROWS, COLS), f32),
        ],
        name="transport_radiation",
    )(tracers, winds, right, left, north, south, edges, gas_rows, *prepared)

    right, left = exchange_cols(head, tail)
    north, south = exchange_rows(head_rows, tail_rows, right, left)
    final = pl.pallas_call(
        last_kernel,
        in_specs=[vmem] * 6 + [smem],
        out_specs=vmem,
        out_shape=tiles_like(ntr, levels, ROWS, COLS),
        scratch_shapes=[
            pltpu.VMEM((ntr * levels * ROWS, COLS), f32),
            pltpu.VMEM((2 * packed_tiles(ntr, levels), ROWS, COLS), f32),
        ],
        name="last_transport",
    )(state, face, right, left, north, south, edges)
    return final, heating


def solution(mesh):
    grid = P(None, None, "lat", "lon")
    in_specs = (grid, grid, grid) + (P("lat", "lon"),) * 3 + (P(),) * 8
    out_specs = (grid, P(None, "lat", "lon"))
    return jax.shard_map(body, mesh=mesh, in_specs=in_specs, out_specs=out_specs, check_vma=False)
```

time: 157 us -> 82.6 us (0.53)
  Pallas kernels: 116 us -> 49.6 us
  local copies, waits for them, and re-layouts: 9.88 us -> 3.59 us
    pallas_call x5 -> x6, Pallas kernels: 116 us -> 49.6 us  [the longest x1 36.8 us: body(): pl.pallas_call(first_kernel, in_specs=[vmem] * 6 + [smem] + [vmem] * 10,...]
    broadcast_in_dim x6 -> x0, local copies, waits for them, and re-layouts: 2.85 us -> none  [the longest x2 0.82 us: body(): lsolar = jnp.broadcast_to(jnp.log2(solar)[:, None], (bands, COLS))]
    unnamed x40 -> x18, local copies, waits for them, and re-layouts: 3.96 us -> 2.55 us
  transfers between devices with their start and end apart: 8 -> 8, of which waited for: 6 -> 7; matrix products, arithmetic and copies ran while one was open for 3% -> 2% of each run, Pallas kernels for 0% -> 2%
where the time goes in v2:
time: 82.6 us; the launch traced here: 82.1 us
  Pallas kernels  49.6 us (60%)
  starting transfers between devices  19.3 us (23%)
  waiting for transfers between devices  8.4 us (10%)
  local copies, waits for them, and re-layouts  3.59 us (4%)
    pallas_call x1, Pallas kernels, body(): pl.pallas_call(first_kernel, in_specs=[vmem] * 6 + [smem] + [vmem] * 10,...  36.8 us
    ppermute x8, starting transfers between devices, shift(): lax.ppermute(x, axis, [(i, (i + by) % count) for i in range(count) if wra...  19.3 us
    ppermute x8, waiting for transfers between devices, shift(): lax.ppermute(x, axis, [(i, (i + by) % count) for i in range(count) if wra...  8.4 us
    pallas_call x1, Pallas kernels, body(): pl.pallas_call(last_kernel, in_specs=[vmem] * 6 + [smem], out_specs=vmem,...  5.74 us
    pallas_call x2, Pallas kernels, exchange_rows(): pl.pallas_call(corner_kernel, in_specs=[any_space] * 2 + [vmem] * 2, out_...  2.69 us
    pallas_call x1, Pallas kernels, body(): pl.pallas_call(functools.partial(pack_kernel, levels), in_specs=[vmem] *...  2.63 us
    unnamed x18, local copies, waits for them, and re-layouts  2.55 us
    pallas_call x1, Pallas kernels, body(): pl.pallas_call(prepare_kernel, in_specs=[vmem, smem, vmem, smem] + [vmem]...  1.78 us
  transfers between devices with their start and end apart: 8, of which 7 were waited for; matrix products, arithmetic and copies ran while one was open for 2% of the time, Pallas kernels for 2%

profile of v2, /device:TPU:1, one launch (start us, length us, event | category | flops | bytes accessed | tf_op | source)
XLA Modules:
  0.0 82.1 jit_solution(12899439827077181162)
XLA Ops:
  0.6 0.0 copy-start
  0.6 2.6 %pack.1 = (f32[3,8,128]{2,1,0:T(8,128)}, f32[3,8,128]{2,1,0:T(8,128)}, f32[400,128]{1,0:T(8,128)}, f32[400,128]{1,0:T(8,128)}) custom-call(f32[1024,128]{1,0:T(8,128)} %bitcast.14, f32[512,128]{1,0:T(8,128)} %bitcast.15), custom_call_target="tpu_custom_call" | custom-call | tf_op jit(solution)/shard_map/pack/pallas_call | solution.py:580
  3.3 3.0 %collective-permute-start = (f32[3,8,128]{2,1,0:T(8,128)}, f32[3,8,128]{2,1,0:T(8,128)S(1)}, u32[]{:S(2)}, u32[]{:S(2)}) collective-permute-start(f32[3,8,128]{2,1,0:T(8,128)} %get-tuple-element.38), channel_id=1, source_target_pairs={{0,24},{8,0},{16,8},{24,16},{1,25},{9,1},{17,9},{25,17},{2,26},{10... | collective-permute-start | bytes 36872 | tf_op jit(solution)/shard_map/ppermute | solution.py:530
  6.3 0.0 collective-permute-start.1
  6.3 0.0 copy-done
  6.3 1.0 %copy_bitcast_fusion.gases = bf16[32,96,128]{2,1,0:T(8,128)(2,1)} fusion(bf16[12,32,8,128]{3,2,1,0:T(8,128)(2,1)S(1)} %copy-done), kind=kLoop, calls=%fused_computation | loop fusion | bytes 1572864 | tf_op jit(solution)/shard_map/reshape | solution.py:624
  7.3 1.8 %prepare.1 = (bf16[512,128]{1,0:T(8,128)(2,1)}, f32[64,128]{1,0:T(8,128)}, bf16[64,64]{1,0:T(8,128)(2,1)}, f32[64,128]{1,0:T(8,128)}, bf16[224,80]{1,0:T(8,128)(...) custom-call(s32[8,128]{1,0:T(8,128)} %index.1, ...), custom_call_target="tpu_custom_call" | custom-call | tf_op jit(solution)/shard_map/prepare/pallas_call | solution.py:591
  9.1 0.0 collective-permute-done.from_right.right
  9.1 0.0 copy-start.5
  9.1 0.8 collective-permute-done.1.from_left.left
  9.9 0.6 copy-done.6
  10.5 1.3 %add_corners.2 = (f32[400,128]{1,0:T(8,128)}, f32[400,128]{1,0:T(8,128)}) custom-call(f32[400,128]{1,0:T(8,128)} %get-tuple-element.51.head_in, f32[400,128]{1,0:T(8,128)} %get-tuple-element.52.tail_in, f32[3,8,128]{2,1,0:T(8,128)} %copy-done.5, f32[3,8,128]{2,1,0:T(8,128)} %copy-done.6), custom_call_target="tpu_custom_call", output_to_operand_aliasing={{0}: (0, {}), {1}: (1, {})} | custom-call | tf_op jit(solution)/shard_map/add_corners/pallas_call | solution.py:542
  11.9 4.0 %collective-permute-start.2 = (f32[400,128]{1,0:T(8,128)}, f32[400,128]{1,0:T(8,128)S(1)}, u32[]{:S(2)}, u32[]{:S(2)}) collective-permute-start(f32[400,128]{1,0:T(8,128)} %get-tuple-element.53), channel_id=1, source_target_pairs={{1,0},{2,1},{3,2},{4,3},{5,4},{6,5},{7,6},{9,8},{10,9},{11,10},{12... | collective-permute-start | bytes 614408 | tf_op jit(solution)/shard_map/ppermute | solution.py:530
  15.9 3.1 %collective-permute-start.3 = (f32[400,128]{1,0:T(8,128)}, f32[400,128]{1,0:T(8,128)S(1)}, u32[]{:S(2)}, u32[]{:S(2)}) collective-permute-start(f32[400,128]{1,0:T(8,128)} %get-tuple-element.54), channel_id=1, source_target_pairs={{0,1},{1,2},{2,3},{3,4},{4,5},{5,6},{6,7},{8,9},{9,10},{10,11},{11... | collective-permute-start | bytes 614408 | tf_op jit(solution)/shard_map/ppermute | solution.py:530
  19.0 0.6 add_convert_fusion.edges
  19.6 1.1 %collective-permute-done.2.north = f32[400,128]{1,0:T(8,128)S(1)} collective-permute-done((f32[400,128]{1,0:T(8,128)}, f32[400,128]{1,0:T(8,128)S(1)}, u32[]{:S(2)}, u32[]{:S(2)}) %collective-permute-start.2) | collective-permute-done | bytes 204832 | tf_op jit(solution)/shard_map/ppermute | solution.py:530
  20.7 1.3 %collective-permute-done.3.south = f32[400,128]{1,0:T(8,128)S(1)} collective-permute-done((f32[400,128]{1,0:T(8,128)}, f32[400,128]{1,0:T(8,128)S(1)}, u32[]{:S(2)}, u32[]{:S(2)}) %collective-permute-start.3) | collective-permute-done | bytes 204832 | tf_op jit(solution)/shard_map/ppermute | solution.py:530
  22.0 0.7 copy-done.2
  22.7 36.8 %transport_radiation.1 = (f32[1024,128]{1,0:T(8,128)}, f32[32,8,128]{2,1,0:T(8,128)}, f32[2,8,128]{2,1,0:T(8,128)}, f32[2,8,128]{2,1,0:T(8,128)}, f32[272,128]{1...) custom-call(f32[4,32,8,128]{3,2,1,0:T(8,128)} %tracers.1, f32[2,32,8,128]{3,2,1,0:T(8,128)} %winds.1, ...), custom_call_target="tpu_custom_call" | custom-call | tf_op jit(solution)/shard_map/transport_radiation/pallas_call | solution.py:631
  59.4 0.7 collective-permute-start.4
  60.2 0.8 collective-permute-start.5
  61.0 1.5 %collective-permute-done.4.from_right.right = f32[2,8,128]{2,1,0:T(8,128)S(1)} collective-permute-done((f32[2,8,128]{2,1,0:T(8,128)}, f32[2,8,128]{2,1,0:T(8,128)S(1)}, u32[]{:S(2)}, u32[]{:S(2)}) %collective-permute-start.4) | collective-permute-done | bytes 8224 | tf_op jit(solution)/shard_map/ppermute | solution.py:530
  62.5 1.3 %collective-permute-done.5.from_left.left = f32[2,8,128]{2,1,0:T(8,128)S(1)} collective-permute-done((f32[2,8,128]{2,1,0:T(8,128)}, f32[2,8,128]{2,1,0:T(8,128)S(1)}, u32[]{:S(2)}, u32[]{:S(2)}) %collective-permute-start.5) | collective-permute-done | bytes 8224 | tf_op jit(solution)/shard_map/ppermute | solution.py:530
  63.8 0.6 copy-done.8
  64.4 1.3 %add_corners.3 = (f32[272,128]{1,0:T(8,128)}, f32[272,128]{1,0:T(8,128)}) custom-call(f32[272,128]{1,0:T(8,128)} %get-tuple-element.69.head_in, f32[272,128]{1,0:T(8,128)} %get-tuple-element.70.tail_in, f32[2,8,128]{2,1,0:T(8,128)} %copy-done.7, f32[2,8,128]{2,1,0:T(8,128)} %copy-done.8), custom_call_target="tpu_custom_call", output_to_operand_aliasing={{0}: (0, {}), {1}: (1, {})} | custom-call | tf_op jit(solution)/shard_map/add_corners/pallas_call | solution.py:542
  65.8 1.9 %collective-permute-start.6 = (f32[272,128]{1,0:T(8,128)}, f32[272,128]{1,0:T(8,128)S(1)}, u32[]{:S(2)}, u32[]{:S(2)}) collective-permute-start(f32[272,128]{1,0:T(8,128)} %get-tuple-element.71), channel_id=1, source_target_pairs={{1,0},{2,1},{3,2},{4,3},{5,4},{6,5},{7,6},{9,8},{10,9},{11,10},{12... | collective-permute-start | bytes 417800 | tf_op jit(solution)/shard_map/ppermute | solution.py:530
  67.7 5.7 %collective-permute-start.7 = (f32[272,128]{1,0:T(8,128)}, f32[272,128]{1,0:T(8,128)S(1)}, u32[]{:S(2)}, u32[]{:S(2)}) collective-permute-start(f32[272,128]{1,0:T(8,128)} %get-tuple-element.72), channel_id=1, source_target_pairs={{0,1},{1,2},{2,3},{3,4},{4,5},{5,6},{6,7},{8,9},{9,10},{10,11},{11... | collective-permute-start | bytes 417800 | tf_op jit(solution)/shard_map/ppermute | solution.py:530
  73.4 1.0 %collective-permute-done.6.north = f32[272,128]{1,0:T(8,128)S(1)} collective-permute-done((f32[272,128]{1,0:T(8,128)}, f32[272,128]{1,0:T(8,128)S(1)}, u32[]{:S(2)}, u32[]{:S(2)}) %collective-permute-start.6) | collective-permute-done | bytes 139296 | tf_op jit(solution)/shard_map/ppermute | solution.py:530
  74.4 1.3 %collective-permute-done.7.south = f32[272,128]{1,0:T(8,128)S(1)} collective-permute-done((f32[272,128]{1,0:T(8,128)}, f32[272,128]{1,0:T(8,128)S(1)}, u32[]{:S(2)}, u32[]{:S(2)}) %collective-permute-start.7) | collective-permute-done | bytes 139296 | tf_op jit(solution)/shard_map/ppermute | solution.py:530
  75.7 0.0 copy-done.3
  75.7 0.6 copy-done.4
  76.4 5.7 %last_transport.1 = f32[4,32,8,128]{3,2,1,0:T(8,128)} custom-call(f32[1024,128]{1,0:T(8,128)} %get-tuple-element.65.tracers, f32[32,8,8,128]{3,2,1,0:T(8,128)} %get-tuple-element.66.face, f32[2,8,128]{2,1,0:T(8,128)} %copy-done.7, f32[2,8,128]{2,1,0:T(8,128)} %copy-done.8, f32[272,128]{1,0:T(8,128)} %copy-done.3, f32[272,128]{1,0:T(8,128)} %copy-done.4, ...), custom_call_target="tpu_custom_call" | custom-call | tf_op jit(solution)/shard_map/last_transport/pallas_call | solution.py:660
  (10 shorter events, 0.0 us)
Async XLA Ops:
  0.6 5.6 %copy-start = (bf16[12,32,8,128]{3,2,1,0:T(8,128)(2,1)S(1)}, bf16[12,32,8,128]{3,2,1,0:T(8,128)(2,1)}, u32[]{:S(2)}) copy-start(bf16[12,32,8,128]{3,2,1,0:T(8,128)(2,1)} %param.16) | copy-start | bytes 2359300
  3.3 5.8 %collective-permute-start = (f32[3,8,128]{2,1,0:T(8,128)}, f32[3,8,128]{2,1,0:T(8,128)S(1)}, u32[]{:S(2)}, u32[]{:S(2)}) collective-permute-start(f32[3,8,128]{2,1,0:T(8,128)} %get-tuple-element.38), channel_id=1, source_target_pairs={{0,24},{8,0},{16,8},{24,16},{1,25},{9,1},{17,9},{25,17},{2,26},{10... | collective-permute-start | bytes 36872 | tf_op jit(solution)/shard_map/ppermute | solution.py:530
  6.3 3.7 %collective-permute-start.1 = (f32[3,8,128]{2,1,0:T(8,128)}, f32[3,8,128]{2,1,0:T(8,128)S(1)}, u32[]{:S(2)}, u32[]{:S(2)}) collective-permute-start(f32[3,8,128]{2,1,0:T(8,128)} %get-tuple-element.39), channel_id=1, source_target_pairs={{0,8},{8,16},{16,24},{24,0},{1,9},{9,17},{17,25},{25,1},{2,10},{10... | collective-permute-start | bytes 36872 | tf_op jit(solution)/shard_map/ppermute | solution.py:530
  9.1 0.8 copy-start.5
  9.9 0.6 copy-start.6
  11.9 8.8 %collective-permute-start.2 = (f32[400,128]{1,0:T(8,128)}, f32[400,128]{1,0:T(8,128)S(1)}, u32[]{:S(2)}, u32[]{:S(2)}) collective-permute-start(f32[400,128]{1,0:T(8,128)} %get-tuple-element.53), channel_id=1, source_target_pairs={{1,0},{2,1},{3,2},{4,3},{5,4},{6,5},{7,6},{9,8},{10,9},{11,10},{12... | collective-permute-start | bytes 614408 | tf_op jit(solution)/shard_map/ppermute | solution.py:530
  15.9 6.1 %collective-permute-start.3 = (f32[400,128]{1,0:T(8,128)}, f32[400,128]{1,0:T(8,128)S(1)}, u32[]{:S(2)}, u32[]{:S(2)}) collective-permute-start(f32[400,128]{1,0:T(8,128)} %get-tuple-element.54), channel_id=1, source_target_pairs={{0,1},{1,2},{2,3},{3,4},{4,5},{5,6},{6,7},{8,9},{9,10},{10,11},{11... | collective-permute-start | bytes 614408 | tf_op jit(solution)/shard_map/ppermute | solution.py:530
  20.7 1.3 %copy-start.1 = (f32[400,128]{1,0:T(8,128)}, f32[400,128]{1,0:T(8,128)S(1)}, u32[]{:S(2)}) copy-start(f32[400,128]{1,0:T(8,128)S(1)} %collective-permute-done.2.north) | copy-start | bytes 614404
  22.0 0.7 copy-start.2
  59.4 3.1 %collective-permute-start.4 = (f32[2,8,128]{2,1,0:T(8,128)}, f32[2,8,128]{2,1,0:T(8,128)S(1)}, u32[]{:S(2)}, u32[]{:S(2)}) collective-permute-start(f32[2,8,128]{2,1,0:T(8,128)} %get-tuple-element.67), channel_id=1, source_target_pairs={{0,24},{8,0},{16,8},{24,16},{1,25},{9,1},{17,9},{25,17},{2,26},{10... | collective-permute-start | bytes 24584 | tf_op jit(solution)/shard_map/ppermute | solution.py:530
  60.2 3.6 %collective-permute-start.5 = (f32[2,8,128]{2,1,0:T(8,128)}, f32[2,8,128]{2,1,0:T(8,128)S(1)}, u32[]{:S(2)}, u32[]{:S(2)}) collective-permute-start(f32[2,8,128]{2,1,0:T(8,128)} %get-tuple-element.68), channel_id=1, source_target_pairs={{0,8},{8,16},{16,24},{24,0},{1,9},{9,17},{17,25},{25,1},{2,10},{10... | collective-permute-start | bytes 24584 | tf_op jit(solution)/shard_map/ppermute | solution.py:530
  62.5 1.3 %copy-start.7 = (f32[2,8,128]{2,1,0:T(8,128)}, f32[2,8,128]{2,1,0:T(8,128)S(1)}, u32[]{:S(2)}) copy-start(f32[2,8,128]{2,1,0:T(8,128)S(1)} %collective-permute-done.4.from_right.right) | copy-start | bytes 24580
  63.8 0.6 copy-start.8
  65.8 8.7 %collective-permute-start.6 = (f32[272,128]{1,0:T(8,128)}, f32[272,128]{1,0:T(8,128)S(1)}, u32[]{:S(2)}, u32[]{:S(2)}) collective-permute-start(f32[272,128]{1,0:T(8,128)} %get-tuple-element.71), channel_id=1, source_target_pairs={{1,0},{2,1},{3,2},{4,3},{5,4},{6,5},{7,6},{9,8},{10,9},{11,10},{12... | collective-permute-start | bytes 417800 | tf_op jit(solution)/shard_map/ppermute | solution.py:530
  67.7 8.1 %collective-permute-start.7 = (f32[272,128]{1,0:T(8,128)}, f32[272,128]{1,0:T(8,128)S(1)}, u32[]{:S(2)}, u32[]{:S(2)}) collective-permute-start(f32[272,128]{1,0:T(8,128)} %get-tuple-element.72), channel_id=1, source_target_pairs={{0,1},{1,2},{2,3},{3,4},{4,5},{5,6},{6,7},{8,9},{9,10},{10,11},{11... | collective-permute-start | bytes 417800 | tf_op jit(solution)/shard_map/ppermute | solution.py:530
  74.4 1.3 %copy-start.3 = (f32[272,128]{1,0:T(8,128)}, f32[272,128]{1,0:T(8,128)S(1)}, u32[]{:S(2)}) copy-start(f32[272,128]{1,0:T(8,128)S(1)} %collective-permute-done.6.north) | copy-start | bytes 417796
  75.7 0.7 copy-start.4

commit v3 on v2

--- a/solution.py
+++ b/solution.py
@@ -18,6 +18,7 @@
 COLS = 128
 RIM = 2
 SLOTS = COLS // RIM
+HAS_AFTER, HAS_BEFORE, LAT_EVEN, LON_EVEN = range(4)
 
 
 def lane_id():
@@ -28,14 +29,6 @@
     return lax.broadcasted_iota(jnp.int32, (ROWS, COLS), 0)
 
 
-def ahead_col(tile, beside):
-    return pltpu.roll(jnp.where(lane_id() == 0, beside, tile), COLS - 1, 1)
-
-
-def behind_col(tile, beside):
-    return pltpu.roll(jnp.where(lane_id() == COLS - 1, beside, tile), 1, 1)
-
-
 def ahead_row(tile, beside):
     return pltpu.roll(jnp.where(row_id() == 0, beside, tile), ROWS - 1, 0)
 
@@ -48,37 +41,36 @@
     return jnp.maximum(face, 0.0) * here + jnp.minimum(face, 0.0) * there
 
 
-def faces(along, across):
-    am, ah, av, ac = along
-    bm, bh, bv, bc = across
-    east = tuple(
-        0.5 * (t + ahead_col(t, o)) for t, o in ((am, ah), (ah, am), (av, ac), (ac, av))
-    )
-    north = tuple(
-        0.5 * (t + ahead_row(t, o)) for t, o in ((bm, bv), (bh, bc), (bv, bm), (bc, bh))
-    )
-    return east, north
-
-
-def two_steps(q, east, north, inside):
-    m, h, v, c = q
-    em = flux(east[0], m, ahead_col(m, h))
-    eh = flux(east[1], h, ahead_col(h, m))
-    ev = flux(east[2], v, ahead_col(v, c))
-    ec = flux(east[3], c, ahead_col(c, v))
-    nm = flux(north[0], m, ahead_row(m, v))
-    nh = flux(north[1], h, ahead_row(h, c))
-    nv = flux(north[2], v, ahead_row(v, m))
-    nc = flux(north[3], c, ahead_row(c, h))
-    m1 = m - (em - behind_col(em, eh)) - (nm - behind_row(nm, nv))
-    h1 = h - (eh - behind_col(eh, em)) - (nh - behind_row(nh, nc))
-    v1 = v - (ev - behind_col(ev, ec)) - (nv - behind_row(nv, nm))
-    v1 = jnp.where(inside > 0.0, v1, 0.0)
-    em = flux(east[0], m1, ahead_col(m1, h1))
-    eh = flux(east[1], h1, ahead_col(h1, m1))
-    nm = flux(north[0], m1, ahead_row(m1, v1))
-    nv = flux(north[2], v1, ahead_row(v1, m1))
-    return m1 - (em - behind_col(em, eh)) - (nm - behind_row(nm, nv))
+def next_col(tile, rim):
+    return jnp.where(lane_id() == COLS - 1, rim, pltpu.roll(tile, COLS - 1, 1))
+
+
+def col_change(face, first, tile, rim):
+    out = flux(face, tile, next_col(tile, rim))
+    return out - jnp.where(lane_id() == 0, flux(first, rim, tile), pltpu.roll(out, 1, 1))
+
+
+def col_faces(wind, rim):
+    return 0.5 * (wind + next_col(wind, rim)), 0.5 * (rim + wind)
+
+
+def row_faces(main, rows):
+    return 0.5 * (main + ahead_row(main, rows)), 0.5 * (rows + ahead_row(rows, main))
+
+
+def row_changes(face, main, rows):
+    out = flux(face[0], main, ahead_row(main, rows))
+    rim = flux(face[1], rows, ahead_row(rows, main))
+    return out - behind_row(out, rim), rim - behind_row(rim, out)
+
+
+def two_steps(main, rows, side, corner, next_side, face, inside):
+    north, south = row_changes(face[4:], main, rows)
+    main1 = main - col_change(face[0], face[1], main, side) - north
+    rows1 = rows - col_change(face[2], face[3], rows, corner) - south
+    rows1 = jnp.where(inside > 0.0, rows1, 0.0)
+    north, _ = row_changes(face[4:], main1, rows1)
+    return main1 - col_change(face[0], face[1], main1, next_side) - north
 
 
 def pack_sides(tile, slot, packs):
@@ -90,19 +82,13 @@
     return head, tail
 
 
-def unpack_sides(from_right, from_left, slot):
-    right = pltpu.roll(from_right, lax.rem(COLS - RIM * slot, COLS), 1)
-    left = pltpu.roll(from_left, lax.rem(2 * COLS - RIM - RIM * slot, COLS), 1)
-    return jnp.where(lane_id() < COLS // 2, right, left)
-
-
 def tile_at(tile):
     return pl.ds(pl.multiple_of(tile * ROWS, ROWS), ROWS)
 
 
-def kept_rows(edges):
-    after = (row_id() == 0) & (edges[0] > 0)
-    before = (row_id() == ROWS - 1) & (edges[1] > 0)
+def kept_rows(flags):
+    after = (row_id() == 0) & (flags[HAS_AFTER] > 0)
+    before = (row_id() == ROWS - 1) & (flags[HAS_BEFORE] > 0)
     return jnp.where(after | before, 1.0, 0.0)
 
 
@@ -124,7 +110,7 @@
     return pl.cdiv(fields * levels, SLOTS)
 
 
-def pack_fields(sources, levels, head_ref, tail_ref):
+def pack_fields(sources, levels, even, one_ref, two_ref):
     count = packed_tiles(len(sources), levels)
     zero = jnp.zeros((ROWS, COLS), jnp.float32)
 
@@ -137,20 +123,20 @@
 
     packs = each_level(levels, step, ((zero, zero),) * count, 8)
     for tile, (head, tail) in enumerate(packs):
-        head_ref[tile] = head
-        tail_ref[tile] = tail
-
-
-def pack_rows(sources, head, tail):
+        one_ref[tile] = jnp.where(even, tail, head)
+        two_ref[tile] = jnp.where(even, head, tail)
+
+
+def pack_rows(sources, even, one, two):
     at = 0
     total = sum(ref.shape[0] for ref in sources) // ROWS
     for ref in sources:
         tiles = ref.shape[0] // ROWS
         for row in range(RIM):
-            head[pl.ds(row * total + at, tiles), :] = ref[pl.ds(row, tiles, stride=ROWS), :]
-            tail[pl.ds(row * total + at, tiles), :] = ref[
-                pl.ds(ROWS - RIM + row, tiles, stride=ROWS), :
-            ]
+            head = ref[pl.ds(row, tiles, stride=ROWS), :]
+            tail = ref[pl.ds(ROWS - RIM + row, tiles, stride=ROWS), :]
+            one[pl.ds(row * total + at, tiles), :] = jnp.where(even, tail, head)
+            two[pl.ds(row * total + at, tiles), :] = jnp.where(even, head, tail)
         at += tiles
 
 
@@ -159,7 +145,7 @@
     return -(-rows // 16) * 16
 
 
-def pack_kernel(levels, tracers, winds, head, tail, head_rows, tail_rows):
+def pack_kernel(levels, flags, tracers, winds, one, two, one_rows, two_rows):
     sources = []
     for ref in (tracers, winds):
         for f in range(ref.shape[0] // (levels * ROWS)):
@@ -169,24 +155,30 @@
                     pl.ds(pl.multiple_of(base + level * ROWS, ROWS), ROWS), :
                 ]
             )
-    pack_rows((tracers, winds), head_rows, tail_rows)
-    pack_fields(sources, levels, head, tail)
-
-
-def corner_kernel(head_in, tail_in, from_right, from_left, head, tail, near, far, sems):
-    del head_in, tail_in
+    pack_rows((tracers, winds), flags[LAT_EVEN] > 0, one_rows, two_rows)
+    pack_fields(sources, levels, flags[LON_EVEN] > 0, one, two)
+
+
+def in_order(even, one, two):
+    return jnp.where(even, one, two), jnp.where(even, two, one)
+
+
+def corner_kernel(one_in, two_in, flags, cols_one, cols_two, one, two, near, far, sems):
+    del one_in, two_in
     near[...] = jnp.zeros(near.shape, jnp.float32)
     far[...] = jnp.zeros(far.shape, jnp.float32)
-    at = 0
-    for ref in (from_right, from_left):
-        for tile in range(ref.shape[0]):
-            near[at : at + RIM, :] = ref[tile, 0:RIM, :]
-            far[at : at + RIM, :] = ref[tile, ROWS - RIM : ROWS, :]
-            at += RIM
-    base = head.shape[0] - near.shape[0]
+    lon_even, lat_even = flags[LON_EVEN] > 0, flags[LAT_EVEN] > 0
+    count = cols_one.shape[0]
+    for tile in range(count):
+        for side, block in enumerate(in_order(lon_even, cols_one[tile], cols_two[tile])):
+            at = RIM * (side * count + tile)
+            head, tail = block[0:RIM], block[ROWS - RIM : ROWS]
+            near[at : at + RIM, :] = jnp.where(lat_even, tail, head)
+            far[at : at + RIM, :] = jnp.where(lat_even, head, tail)
+    base = one.shape[0] - near.shape[0]
     copies = [
         pltpu.make_async_copy(block, whole.at[pl.ds(base, near.shape[0])], sems.at[k])
-        for k, (block, whole) in enumerate(((near, head), (far, tail)))
+        for k, (block, whole) in enumerate(((near, one), (far, two)))
     ]
     for copy in copies:
         copy.start()
@@ -194,36 +186,63 @@
         copy.wait()
 
 
-def unpack_rows(from_north, from_south, rim_ref, corner_ref, tiles, packed):
+def unpack_rows(even, rows_one, rows_two, rim_ref, corner_ref, tiles, packed):
     for row in range(RIM):
-        rim_ref[pl.ds(row, tiles, stride=ROWS), :] = from_north[pl.ds(row * tiles, tiles), :]
-        rim_ref[pl.ds(ROWS - RIM + row, tiles, stride=ROWS), :] = from_south[
-            pl.ds(row * tiles, tiles), :
-        ]
-    at = RIM * tiles
+        here = pl.ds(row * tiles, tiles)
+        after, before = in_order(even, rows_one[here, :], rows_two[here, :])
+        rim_ref[pl.ds(row, tiles, stride=ROWS), :] = after
+        rim_ref[pl.ds(ROWS - RIM + row, tiles, stride=ROWS), :] = before
     for tile in range(2 * packed):
-        corner_ref[tile, 0:RIM, :] = from_north[at : at + RIM, :]
-        corner_ref[tile, ROWS - RIM : ROWS, :] = from_south[at : at + RIM, :]
-        at += RIM
-
-
-def rim_tiles(field, level, levels, packed, right, left, rim_ref, corner_ref):
+        at = RIM * (tiles + tile)
+        after, before = in_order(even, rows_one[at : at + RIM, :], rows_two[at : at + RIM, :])
+        corner_ref[tile, 0:RIM, :] = after
+        corner_ref[tile, ROWS - RIM : ROWS, :] = before
+
+
+def paired(after, before):
+    return jnp.where(lane_id() % 2 == 0, after, before)
+
+
+def side_tiles(even, own_one, own_two, cols_one, cols_two, corner_ref, tile, packed):
+    right, left = in_order(even, cols_one[tile], cols_two[tile])
+    tail, head = in_order(even, own_one[tile], own_two[tile])
+    return (
+        paired(right, left),
+        paired(pltpu.roll(right, COLS - 1, 1), pltpu.roll(head, 1, 1)),
+        paired(pltpu.roll(tail, COLS - 1, 1), pltpu.roll(left, 1, 1)),
+        paired(corner_ref[tile], corner_ref[packed + tile]),
+    )
+
+
+def side_faces(tiles):
+    low = lane_id() < COLS // 2
+    half = [pltpu.roll(t, COLS // 2, 1) for t in tiles]
+    u, after, before, _ = [jnp.where(low, t, h) for t, h in zip(tiles, half)]
+    v, _, _, corner = [jnp.where(low, h, t) for t, h in zip(tiles, half)]
+    return (0.5 * (u + after), 0.5 * (before + u), *row_faces(v, corner))
+
+
+def side_step(tiles, face):
+    here, after, before, corner = tiles
+    east = flux(face[0], here, after) - flux(face[1], before, here)
+    return here - east - row_changes(face[2:], here, corner)[0]
+
+
+def from_side(ref, field, level, levels):
     tile, slot = place(field, level, levels)
-    side = unpack_sides(right[tile], left[tile], slot)
-    row = pl.multiple_of((field * levels + level) * ROWS, ROWS)
-    rows = rim_ref[pl.ds(row, ROWS), :]
-    corner = unpack_sides(corner_ref[tile], corner_ref[packed + tile], slot)
-    return side, rows, corner
+    return pltpu.roll(ref[tile], COLS - 1 - RIM * slot, 1)
 
 
 def first_kernel(
     tracers,
     winds,
-    right,
-    left,
-    north,
-    south,
-    edges,
+    own_one,
+    own_two,
+    cols_one,
+    cols_two,
+    rows_one,
+    rows_two,
+    flags,
     gases,
     w1,
     b1,
@@ -236,18 +255,23 @@
     scaled,
     state,
     heating,
-    head,
-    tail,
-    head_rows,
-    tail_rows,
+    next_one,
+    next_two,
+    next_rows_one,
+    next_rows_two,
     face,
+    side_face,
     rim_ref,
     corner_ref,
+    side_ref,
+    next_side_ref,
+    side_rim_ref,
     xs,
     hid_a,
     hid_b,
     hidden,
-    logits,
+    logits_a,
+    logits_b,
     depth_a,
     depth_b,
     weight,
@@ -259,27 +283,44 @@
     packed = packed_tiles(fields, levels)
     groups = lsolar.shape[0]
     hid = b1.shape[0]
-    unpack_rows(north, south, rim_ref, corner_ref, fields * levels, packed)
-    keep = kept_rows(edges)
+    lon_even, lat_even = flags[LON_EVEN] > 0, flags[LAT_EVEN] > 0
+    unpack_rows(lat_even, rows_one, rows_two, rim_ref, corner_ref, fields * levels, packed)
+    keep = kept_rows(flags)
+    sides = [
+        side_tiles(lon_even, own_one, own_two, cols_one, cols_two, corner_ref, tile, packed)
+        for tile in range(packed)
+    ]
+    of_sides = side_faces(sides[packed - 1])
+    for k, tile in enumerate(of_sides):
+        side_face[k] = tile
+    for tile in range(packed):
+        side_ref[tile] = sides[tile][0]
+        side_rim_ref[tile] = sides[tile][3]
+        if tile < packed - 1:
+            next_side_ref[tile] = side_step(sides[tile], of_sides)
 
     def transport(level, carry):
-        rim = functools.partial(
-            rim_tiles,
-            level=level,
-            levels=levels,
-            packed=packed,
-            right=right,
-            left=left,
-            rim_ref=rim_ref,
-            corner_ref=corner_ref,
+        def rows_of(field):
+            return rim_ref[tile_at(field * levels + level), :]
+
+        tiles = (
+            *col_faces(winds[0, level], from_side(side_ref, ntr, level, levels)),
+            *col_faces(rows_of(ntr), from_side(side_rim_ref, ntr, level, levels)),
+            *row_faces(winds[1, level], rows_of(ntr + 1)),
         )
-        east, north_face = faces(
-            (winds[0, level], *rim(ntr)), (winds[1, level], *rim(ntr + 1))
-        )
-        face[level] = jnp.stack([*east, *north_face])
+        for k, tile in enumerate(tiles):
+            face[level, k] = tile
         out = []
         for f in range(ntr):
-            q = two_steps((tracers[f, level], *rim(f)), east, north_face, keep)
+            q = two_steps(
+                tracers[f, level],
+                rows_of(f),
+                from_side(side_ref, f, level, levels),
+                from_side(side_rim_ref, f, level, levels),
+                from_side(next_side_ref, f, level, levels),
+                tiles,
+                keep,
+            )
             state[tile_at(f * levels + level), :] = q
             out.append(q)
         xs[level] = jnp.concatenate(out, 0).astype(jnp.bfloat16)
@@ -333,13 +374,13 @@
     lax.fori_loop(0, pairs // 2, layers, 0)
     layer_two(pairs - 1, hid_b)
 
-    def third(at):
-        logits[...] = jnp.dot(w3[...], hidden[at], preferred_element_type=jnp.float32).reshape(
+    def third(at, buf):
+        buf[...] = jnp.dot(w3[...], hidden[at], preferred_element_type=jnp.float32).reshape(
             groups, ROWS, 2 * COLS
         )
 
-    def optical(pair, depth):
-        t = logits[...] * log2e
+    def optical(pair, depth, buf):
+        t = buf[...] * log2e
         soft = jnp.maximum(t, jnp.log2(1.0 + jnp.exp2(jnp.minimum(t, 126.0))))
         d = depth[2 * pair] + soft[:, :, :COLS]
         depth[2 * pair + 1] = d
@@ -361,22 +402,27 @@
     def both(row, depth, before):
         close(row - 1, before)
 
-        def step(pair, carry):
-            optical(pair, depth)
-            light(row - 1, 2 * pair, before)
-            light(row - 1, 2 * pair + 1, before)
-            third(row * pairs + pair + 1)
+        def step(trip, carry):
+            for k, buf in enumerate(bufs):
+                pair = 2 * trip + k
+                optical(pair, depth, buf)
+                light(row - 1, 2 * pair, before)
+                light(row - 1, 2 * pair + 1, before)
+                third(row * pairs + pair + 2, buf)
             return carry
 
-        lax.fori_loop(0, pairs, step, 0)
-
-    def only_optical(pair, carry):
-        optical(pair, depths[0])
-        third(pair + 1)
+        lax.fori_loop(0, pairs // 2, step, 0)
+
+    def only_optical(trip, carry):
+        for k, buf in enumerate(bufs):
+            optical(2 * trip + k, depths[0], buf)
+            third(2 * trip + k + 2, buf)
         return carry
 
-    third(0)
-    lax.fori_loop(0, pairs, only_optical, 0)
+    bufs = (logits_a, logits_b)
+    third(0, logits_a)
+    third(1, logits_b)
+    lax.fori_loop(0, pairs // 2, only_optical, 0)
 
     def two_rows(step, carry):
         both(2 * step + 1, depths[1], depths[0])
@@ -404,36 +450,60 @@
         return carry
 
     each_level(levels, add, 0, 8)
-    pack_rows((state,), head_rows, tail_rows)
+    pack_rows((state,), lat_even, next_rows_one, next_rows_two)
     pack_fields(
         [lambda level, f=f: state[tile_at(f * levels + level), :] for f in range(ntr)],
         levels,
-        head,
-        tail,
+        lon_even,
+        next_one,
+        next_two,
     )
 
 
-def last_kernel(tracers, face, right, left, north, south, edges, out, rim_ref, corner_ref):
+def last_kernel(
+    tracers,
+    face,
+    side_face,
+    own_one,
+    own_two,
+    cols_one,
+    cols_two,
+    rows_one,
+    rows_two,
+    flags,
+    out,
+    rim_ref,
+    corner_ref,
+    side_ref,
+    next_side_ref,
+    side_rim_ref,
+):
     ntr, levels = out.shape[0], out.shape[1]
     packed = packed_tiles(ntr, levels)
-    unpack_rows(north, south, rim_ref, corner_ref, ntr * levels, packed)
-    keep = kept_rows(edges)
+    lon_even, lat_even = flags[LON_EVEN] > 0, flags[LAT_EVEN] > 0
+    unpack_rows(lat_even, rows_one, rows_two, rim_ref, corner_ref, ntr * levels, packed)
+    keep = kept_rows(flags)
+    of_sides = [side_face[k] for k in range(4)]
+    for tile in range(packed):
+        sides = side_tiles(
+            lon_even, own_one, own_two, cols_one, cols_two, corner_ref, tile, packed
+        )
+        side_ref[tile] = sides[0]
+        side_rim_ref[tile] = sides[3]
+        next_side_ref[tile] = side_step(sides, of_sides)
 
     def transport(level, carry):
-        rim = functools.partial(
-            rim_tiles,
-            level=level,
-            levels=levels,
-            packed=packed,
-            right=right,
-            left=left,
-            rim_ref=rim_ref,
-            corner_ref=corner_ref,
-        )
-        tiles = [face[level, k] for k in range(8)]
+        tiles = [face[level, k] for k in range(6)]
         for f in range(ntr):
-            q = tracers[tile_at(f * levels + level), :]
-            out[f, level] = two_steps((q, *rim(f)), tiles[:4], tiles[4:], keep)
+            out[f, level] = two_steps(
+                tracers[tile_at(f * levels + level), :],
+                rim_ref[tile_at(f * levels + level), :],
+                from_side(side_ref, f, level, levels),
+                from_side(side_rim_ref, f, level, levels),
+                from_side(next_side_ref, f, level, levels),
+                tiles,
+                keep,
+            )
         return carry
 
     each_level(levels, transport, 0, 4)
@@ -525,30 +595,28 @@
     return jax.ShapeDtypeStruct(shape, f32)
 
 
-def shift(x, axis, by, wrap):
+def swap_pairs(one, two, axis, ring):
     count = lax.axis_size(axis)
-    return lax.ppermute(
-        x, axis, [(i, (i + by) % count) for i in range(count) if wrap or 0 <= i + by < count]
-    )
-
-
-def exchange_cols(head, tail):
-    return shift(head, "lon", -1, True), shift(tail, "lon", 1, True)
-
-
-def exchange_rows(head, tail, right, left):
+    near = [(i, i ^ 1) for i in range(count)]
+    far = [(i, (i - 1 if i % 2 == 0 else i + 1) % count) for i in range(count)]
+    if not ring:
+        far = [(i, j) for i, j in far if abs(i - j) == 1]
+    return lax.ppermute(one, axis, near), lax.ppermute(two, axis, far)
+
+
+def exchange_rows(one, two, flags, cols):
     any_space = pl.BlockSpec(memory_space=pl.ANY)
-    spare = -(-2 * RIM * right.shape[0] // 16) * 16
-    head, tail = pl.pallas_call(
+    spare = -(-2 * RIM * cols[0].shape[0] // 16) * 16
+    one, two = pl.pallas_call(
         corner_kernel,
-        in_specs=[any_space] * 2 + [vmem] * 2,
+        in_specs=[any_space] * 2 + [smem] + [vmem] * 2,
         out_specs=[any_space] * 2,
-        out_shape=[tiles_like(*head.shape)] * 2,
+        out_shape=[tiles_like(*one.shape)] * 2,
         input_output_aliases={0: 0, 1: 1},
         scratch_shapes=[pltpu.VMEM((spare, COLS), f32)] * 2 + [pltpu.SemaphoreType.DMA((2,))],
         name="add_corners",
-    )(head, tail, right, left)
-    return shift(head, "lat", -1, False), shift(tail, "lat", 1, False)
+    )(one, two, flags, *cols)
+    return swap_pairs(one, two, "lat", False)
 
 
 def body(
@@ -572,19 +640,25 @@
     gas = gases.shape[0]
     hid = w_first.shape[1]
     bands = solar.shape[0]
-    if (clat, width) != (ROWS, COLS) or w_first.shape[0] * ROWS != COLS or levels % 8 or SLOTS % levels or bands % ROWS:
+    if lax.axis_size("lat") % 2 or lax.axis_size("lon") % 2:
+        raise ValueError("unsupported mesh")
+    if (clat, width) != (ROWS, COLS) or w_first.shape[0] * ROWS != COLS or levels % 8 or 2 * levels != SLOTS or ntr % 2 or SLOTS % levels or bands % ROWS:
         raise ValueError("unsupported sizes")
 
     flat = (tracers.reshape(-1, COLS), winds.reshape(-1, COLS))
     columns = tiles_like(packed_tiles(fields, levels), ROWS, COLS)
-    head, tail, head_rows, tail_rows = pl.pallas_call(
+    lat, lats = lax.axis_index("lat"), lax.axis_size("lat")
+    flags = [lat < lats - 1, lat > 0, lat % 2 == 0, lax.axis_index("lon") % 2 == 0]
+    flags = jnp.stack(flags).astype(jnp.int32)
+    one, two, rows_one, rows_two = pl.pallas_call(
         functools.partial(pack_kernel, levels),
-        in_specs=[vmem] * 2,
+        in_specs=[smem] + [vmem] * 2,
         out_specs=[vmem] * 4,
         out_shape=[columns] * 2 + [tiles_like(row_payload(fields, levels), COLS)] * 2,
         name="pack",
-    )(*flat)
-    right, left = exchange_cols(head, tail)
+    )(flags, *flat)
+    own = (one, two)
+    cols = swap_pairs(one, two, "lon", True)
 
     groups = bands // ROWS
     bf16 = jnp.bfloat16
@@ -622,30 +696,32 @@
         b_third.reshape(1, -1),
     )
     gas_rows = gases.transpose(1, 0, 2, 3).reshape(levels, gas * ROWS, COLS)
-    lat = lax.axis_index("lat")
-    edges = jnp.stack([lat < lax.axis_size("lat") - 1, lat > 0]).astype(jnp.int32)
-    right, left, prepared, gas_rows = lax.optimization_barrier((right, left, prepared, gas_rows))
-    north, south = exchange_rows(head_rows, tail_rows, right, left)
+    cols, prepared, gas_rows = lax.optimization_barrier((cols, prepared, gas_rows))
+    rows = exchange_rows(rows_one, rows_two, flags, cols)
 
     packed = packed_tiles(fields, levels)
-    state, heating, head, tail, head_rows, tail_rows, face = pl.pallas_call(
+    state, heating, one, two, rows_one, rows_two, face, side_face = pl.pallas_call(
         first_kernel,
-        in_specs=[vmem] * 6 + [smem] + [vmem] * 10,
-        out_specs=[vmem] * 7,
+        in_specs=[vmem] * 8 + [smem] + [vmem] * 10,
+        out_specs=[vmem] * 8,
         out_shape=[
             tiles_like(ntr * levels * ROWS, COLS),
             tiles_like(levels, ROWS, COLS),
         ]
         + [tiles_like(packed_tiles(ntr, levels), ROWS, COLS)] * 2
         + [tiles_like(row_payload(ntr, levels), COLS)] * 2
-        + [tiles_like(levels, 8, ROWS, COLS)],
+        + [tiles_like(levels, 6, ROWS, COLS), tiles_like(4, ROWS, COLS)],
         scratch_shapes=[
             pltpu.VMEM((fields * levels * ROWS, COLS), f32),
             pltpu.VMEM((2 * packed, ROWS, COLS), f32),
+            pltpu.VMEM((packed, ROWS, COLS), f32),
+            pltpu.VMEM((packed, ROWS, COLS), f32),
+            pltpu.VMEM((packed, ROWS, COLS), f32),
             pltpu.VMEM((levels, ntr * ROWS, COLS), bf16),
             pltpu.VMEM((ROWS * hid, 2 * COLS), bf16),
             pltpu.VMEM((ROWS * hid, 2 * COLS), bf16),
-            pltpu.VMEM((ROWS * levels // 2 + 1, hid + 16, 2 * COLS), bf16),
+            pltpu.VMEM((ROWS * levels // 2 + 2, hid + 16, 2 * COLS), bf16),
+            pltpu.VMEM((groups, ROWS, 2 * COLS), f32),
             pltpu.VMEM((groups, ROWS, 2 * COLS), f32),
             pltpu.VMEM((levels + 1, groups, ROWS, COLS), f32),
             pltpu.VMEM((levels + 1, groups, ROWS, COLS), f32),
@@ -653,21 +729,23 @@
             pltpu.VMEM((ROWS, levels + 1, ROWS, COLS), f32),
         ],
         name="transport_radiation",
-    )(tracers, winds, right, left, north, south, edges, gas_rows, *prepared)
-
-    right, left = exchange_cols(head, tail)
-    north, south = exchange_rows(head_rows, tail_rows, right, left)
+    )(tracers, winds, *own, *cols, *rows, flags, gas_rows, *prepared)
+
+    own = (one, two)
+    cols = swap_pairs(one, two, "lon", True)
+    rows = exchange_rows(rows_one, rows_two, flags, cols)
     final = pl.pallas_call(
         last_kernel,
-        in_specs=[vmem] * 6 + [smem],
+        in_specs=[vmem] * 9 + [smem],
         out_specs=vmem,
         out_shape=tiles_like(ntr, levels, ROWS, COLS),
         scratch_shapes=[
             pltpu.VMEM((ntr * levels * ROWS, COLS), f32),
             pltpu.VMEM((2 * packed_tiles(ntr, levels), ROWS, COLS), f32),
-        ],
+        ]
+        + [pltpu.VMEM((packed_tiles(ntr, levels), ROWS, COLS), f32)] * 3,
         name="last_transport",
-    )(state, face, right, left, north, south, edges)
+    )(state, face, side_face, *own, *cols, *rows, flags)
     return final, heating
 
 

time: 82.6 us -> 73.7 us (0.89)
  Pallas kernels: 49.6 us -> 44.2 us
  starting transfers between devices: 19.3 us -> 15.1 us
    pallas_call x5, Pallas kernels: 47.8 us -> 42.4 us  [the longest x1 31.9 us: body(): pl.pallas_call(first_kernel, in_specs=[vmem] * 8 + [smem] + [vmem] * 10,...]
    ppermute x8, starting transfers between devices: 19.3 us -> 15.1 us  [swap_pairs(): return (lax.ppermute(one, axis, near), lax.ppermute(two, axis, far))]
  transfers between devices with their start and end apart: 8 -> 8, of which waited for: 7 -> 4; matrix products, arithmetic and copies ran while one was open for 2% -> 1% of each run, Pallas kernels for 2% -> 2%
where the time goes in v3:
time: 73.7 us; the launch traced here: 73.3 us
  Pallas kernels  44.2 us (60%)
  starting transfers between devices  15.1 us (20%)
  waiting for transfers between devices  9.04 us (12%)
  local copies, waits for them, and re-layouts  3.59 us (5%)
  between operations  0.78 us (1%)
    pallas_call x1, Pallas kernels, body(): pl.pallas_call(first_kernel, in_specs=[vmem] * 8 + [smem] + [vmem] * 10,...  31.9 us
    ppermute x8, starting transfers between devices, swap_pairs(): return (lax.ppermute(one, axis, near), lax.ppermute(two, axis, far))  15.1 us
    ppermute x8, waiting for transfers between devices, swap_pairs(): return (lax.ppermute(one, axis, near), lax.ppermute(two, axis, far))  9.04 us
    pallas_call x1, Pallas kernels, body(): pl.pallas_call(last_kernel, in_specs=[vmem] * 9 + [smem], out_specs=vmem,...  5.23 us
    pallas_call x2, Pallas kernels, exchange_rows(): pl.pallas_call(corner_kernel, in_specs=[any_space] * 2 + [smem] + [vmem]...  2.71 us
    pallas_call x1, Pallas kernels, body(): pl.pallas_call(functools.partial(pack_kernel, levels), in_specs=[smem] +...  2.56 us
    unnamed x18, local copies, waits for them, and re-layouts  2.54 us
    pallas_call x1, Pallas kernels, body(): pl.pallas_call(prepare_kernel, in_specs=[vmem, smem, vmem, smem] + [vmem]...  1.8 us
  transfers between devices with their start and end apart: 8, of which 4 were waited for; matrix products, arithmetic and copies ran while one was open for 1% of the time, Pallas kernels for 2%

profile of v3, /device:TPU:1, one launch (start us, length us, event | category | flops | bytes accessed | tf_op | source)
XLA Modules:
  0.0 73.3 jit_solution(10083572084757358884)
XLA Ops:
  0.6 0.0 copy-start
  0.7 0.6 add_convert_fusion.flags
  1.2 2.6 %pack.1 = (f32[3,8,128]{2,1,0:T(8,128)}, f32[3,8,128]{2,1,0:T(8,128)}, f32[400,128]{1,0:T(8,128)}, f32[400,128]{1,0:T(8,128)}) custom-call(s32[4]{0:T(128)} %add_convert_fusion.flags, f32[1024,128]{1,0:T(8,128)} %bitcast.16, f32[512,128]{1,0:T(8,128)} %bitcast.17), custom_call_target="tpu_custom_call" | custom-call | tf_op jit(solution)/shard_map/pack/pallas_call | solution.py:653
  3.8 2.0 %collective-permute-start = (f32[3,8,128]{2,1,0:T(8,128)}, f32[3,8,128]{2,1,0:T(8,128)S(1)}, u32[]{:S(2)}, u32[]{:S(2)}) collective-permute-start(f32[3,8,128]{2,1,0:T(8,128)} %get-tuple-element.39.own_one), channel_id=1, source_target_pairs={{0,8},{8,0},{16,24},{24,16},{1,9},{9,1},{17,25},{25,17},{2,10},{10... | collective-permute-start | bytes 36872 | tf_op jit(solution)/shard_map/ppermute | solution.py:604
  5.8 1.2 %collective-permute-start.1 = (f32[3,8,128]{2,1,0:T(8,128)}, f32[3,8,128]{2,1,0:T(8,128)S(1)}, u32[]{:S(2)}, u32[]{:S(2)}) collective-permute-start(f32[3,8,128]{2,1,0:T(8,128)} %get-tuple-element.40.own_two), channel_id=1, source_target_pairs={{0,24},{8,16},{16,8},{24,0},{1,25},{9,17},{17,9},{25,1},{2,26},{10... | collective-permute-start | bytes 36872 | tf_op jit(solution)/shard_map/ppermute | solution.py:604
  7.0 1.0 %copy_bitcast_fusion.gases = bf16[32,96,128]{2,1,0:T(8,128)(2,1)} fusion(bf16[12,32,8,128]{3,2,1,0:T(8,128)(2,1)S(1)} %copy-done), kind=kLoop, calls=%fused_computation | loop fusion | bytes 1572864 | tf_op jit(solution)/shard_map/reshape | solution.py:698
  8.1 1.8 %prepare.1 = (bf16[512,128]{1,0:T(8,128)(2,1)}, f32[64,128]{1,0:T(8,128)}, bf16[64,64]{1,0:T(8,128)(2,1)}, f32[64,128]{1,0:T(8,128)}, bf16[224,80]{1,0:T(8,128)(...) custom-call(s32[8,128]{1,0:T(8,128)} %index.1, ...), custom_call_target="tpu_custom_call" | custom-call | tf_op jit(solution)/shard_map/prepare/pallas_call | solution.py:665
  9.9 0.0 collective-permute-done.cols_one
  9.9 0.0 collective-permute-done.1.cols_two
  9.9 0.6 copy-done.5
  10.5 0.0 copy-done.6
  10.5 1.4 %add_corners.2 = (f32[400,128]{1,0:T(8,128)}, f32[400,128]{1,0:T(8,128)}) custom-call(f32[400,128]{1,0:T(8,128)} %get-tuple-element.52.one_in, f32[400,128]{1,0:T(8,128)} %get-tuple-element.53.two_in, s32[4]{0:T(128)} %add_convert_fusion.flags, f32[3,8,128]{2,1,0:T(8,128)} %copy-done.5, ...), custom_call_target="tpu_custom_call", output_to_operand_aliasing={{0}: (0, {}), {1}: (1, {})} | custom-call | tf_op jit(solution)/shard_map/add_corners/pallas_call | solution.py:610
  11.9 1.7 %collective-permute-start.2 = (f32[400,128]{1,0:T(8,128)}, f32[400,128]{1,0:T(8,128)S(1)}, u32[]{:S(2)}, u32[]{:S(2)}) collective-permute-start(f32[400,128]{1,0:T(8,128)} %get-tuple-element.54), channel_id=1, source_target_pairs={{0,1},{1,0},{2,3},{3,2},{4,5},{5,4},{6,7},{7,6},{8,9},{9,8},{10,11... | collective-permute-start | bytes 614408 | tf_op jit(solution)/shard_map/ppermute | solution.py:604
  13.6 3.1 %collective-permute-start.3 = (f32[400,128]{1,0:T(8,128)}, f32[400,128]{1,0:T(8,128)S(1)}, u32[]{:S(2)}, u32[]{:S(2)}) collective-permute-start(f32[400,128]{1,0:T(8,128)} %get-tuple-element.55), channel_id=1, source_target_pairs={{1,2},{2,1},{3,4},{4,3},{5,6},{6,5},{9,10},{10,9},{11,12},{12,11},... | collective-permute-start | bytes 614408 | tf_op jit(solution)/shard_map/ppermute | solution.py:604
  16.7 0.0 collective-permute-done.2.rows_one
  16.7 0.0 copy-start.1
  16.7 4.1 %collective-permute-done.3.rows_two = f32[400,128]{1,0:T(8,128)S(1)} collective-permute-done((f32[400,128]{1,0:T(8,128)}, f32[400,128]{1,0:T(8,128)S(1)}, u32[]{:S(2)}, u32[]{:S(2)}) %collective-permute-start.3) | collective-permute-done | bytes 204832 | tf_op jit(solution)/shard_map/ppermute | solution.py:604
  20.9 0.7 copy-done.2
  21.6 31.9 %transport_radiation.1 = (f32[1024,128]{1,0:T(8,128)}, f32[32,8,128]{2,1,0:T(8,128)}, f32[2,8,128]{2,1,0:T(8,128)}, f32[2,8,128]{2,1,0:T(8,128)}, f32[272,128]{1...) custom-call(f32[4,32,8,128]{3,2,1,0:T(8,128)} %tracers.1, ...), custom_call_target="tpu_custom_call" | custom-call | tf_op jit(solution)/shard_map/transport_radiation/pallas_call | solution.py:703
  53.5 0.8 %collective-permute-start.4 = (f32[2,8,128]{2,1,0:T(8,128)}, f32[2,8,128]{2,1,0:T(8,128)S(1)}, u32[]{:S(2)}, u32[]{:S(2)}) collective-permute-start(f32[2,8,128]{2,1,0:T(8,128)} %get-tuple-element.69.own_one), channel_id=1, source_target_pairs={{0,8},{8,0},{16,24},{24,16},{1,9},{9,1},{17,25},{25,17},{2,10},{10... | collective-permute-start | bytes 24584 | tf_op jit(solution)/shard_map/ppermute | solution.py:604
  54.3 1.6 %collective-permute-start.5 = (f32[2,8,128]{2,1,0:T(8,128)}, f32[2,8,128]{2,1,0:T(8,128)S(1)}, u32[]{:S(2)}, u32[]{:S(2)}) collective-permute-start(f32[2,8,128]{2,1,0:T(8,128)} %get-tuple-element.70.own_two), channel_id=1, source_target_pairs={{0,24},{8,16},{16,8},{24,0},{1,25},{9,17},{17,9},{25,1},{2,26},{10... | collective-permute-start | bytes 24584 | tf_op jit(solution)/shard_map/ppermute | solution.py:604
  56.0 0.3 collective-permute-done.4.cols_one
  56.3 1.7 %collective-permute-done.5.cols_two = f32[2,8,128]{2,1,0:T(8,128)S(1)} collective-permute-done((f32[2,8,128]{2,1,0:T(8,128)}, f32[2,8,128]{2,1,0:T(8,128)S(1)}, u32[]{:S(2)}, u32[]{:S(2)}) %collective-permute-start.5) | collective-permute-done | bytes 8224 | tf_op jit(solution)/shard_map/ppermute | solution.py:604
  57.9 0.0 copy-done.7
  57.9 0.6 copy-done.8
  58.5 1.4 %add_corners.3 = (f32[272,128]{1,0:T(8,128)}, f32[272,128]{1,0:T(8,128)}) custom-call(f32[272,128]{1,0:T(8,128)} %get-tuple-element.71.one_in, f32[272,128]{1,0:T(8,128)} %get-tuple-element.72.two_in, s32[4]{0:T(128)} %add_convert_fusion.flags, f32[2,8,128]{2,1,0:T(8,128)} %copy-done.7, ...), custom_call_target="tpu_custom_call", output_to_operand_aliasing={{0}: (0, {}), {1}: (1, {})} | custom-call | tf_op jit(solution)/shard_map/add_corners/pallas_call | solution.py:610
  59.9 0.1 collective-permute-start.6
  60.0 4.5 %collective-permute-start.7 = (f32[272,128]{1,0:T(8,128)}, f32[272,128]{1,0:T(8,128)S(1)}, u32[]{:S(2)}, u32[]{:S(2)}) collective-permute-start(f32[272,128]{1,0:T(8,128)} %get-tuple-element.74), channel_id=1, source_target_pairs={{1,2},{2,1},{3,4},{4,3},{5,6},{6,5},{9,10},{10,9},{11,12},{12,11},... | collective-permute-start | bytes 417800 | tf_op jit(solution)/shard_map/ppermute | solution.py:604
  64.5 0.0 collective-permute-done.6.rows_one
  64.5 2.9 %collective-permute-done.7.rows_two = f32[272,128]{1,0:T(8,128)S(1)} collective-permute-done((f32[272,128]{1,0:T(8,128)}, f32[272,128]{1,0:T(8,128)S(1)}, u32[]{:S(2)}, u32[]{:S(2)}) %collective-permute-start.7) | collective-permute-done | bytes 139296 | tf_op jit(solution)/shard_map/ppermute | solution.py:604
  67.4 0.6 copy-done.4
  68.1 5.2 %last_transport.1 = f32[4,32,8,128]{3,2,1,0:T(8,128)} custom-call(f32[1024,128]{1,0:T(8,128)} %get-tuple-element.66.tracers, f32[32,6,8,128]{3,2,1,0:T(8,128)} %get-tuple-element.67.face, f32[4,8,128]{2,1,0:T(8,128)} %get-tuple-element.68.side_face, f32[2,8,128]{2,1,0:T(8,128)} %get-tuple-element.69.own_one, f32[2,8,128]{2,1,0:T(8,128)} %get-tuple-element.70.own_two, ...), custom_call_target="tpu_custom_call" | custom-call | tf_op jit(solution)/shard_map/last_transport/pallas_call | solution.py:737
  (10 shorter events, 0.0 us)
Async XLA Ops:
  0.6 6.4 %copy-start = (bf16[12,32,8,128]{3,2,1,0:T(8,128)(2,1)S(1)}, bf16[12,32,8,128]{3,2,1,0:T(8,128)(2,1)}, u32[]{:S(2)}) copy-start(bf16[12,32,8,128]{3,2,1,0:T(8,128)(2,1)} %param.16) | copy-start | bytes 2359300
  3.8 6.1 %collective-permute-start = (f32[3,8,128]{2,1,0:T(8,128)}, f32[3,8,128]{2,1,0:T(8,128)S(1)}, u32[]{:S(2)}, u32[]{:S(2)}) collective-permute-start(f32[3,8,128]{2,1,0:T(8,128)} %get-tuple-element.39.own_one), channel_id=1, source_target_pairs={{0,8},{8,0},{16,24},{24,16},{1,9},{9,1},{17,25},{25,17},{2,10},{10... | collective-permute-start | bytes 36872 | tf_op jit(solution)/shard_map/ppermute | solution.py:604
  5.8 4.1 %collective-permute-start.1 = (f32[3,8,128]{2,1,0:T(8,128)}, f32[3,8,128]{2,1,0:T(8,128)S(1)}, u32[]{:S(2)}, u32[]{:S(2)}) collective-permute-start(f32[3,8,128]{2,1,0:T(8,128)} %get-tuple-element.40.own_two), channel_id=1, source_target_pairs={{0,24},{8,16},{16,8},{24,0},{1,25},{9,17},{17,9},{25,1},{2,26},{10... | collective-permute-start | bytes 36872 | tf_op jit(solution)/shard_map/ppermute | solution.py:604
  9.9 0.6 copy-start.5
  9.9 0.6 copy-start.6
  11.9 4.8 %collective-permute-start.2 = (f32[400,128]{1,0:T(8,128)}, f32[400,128]{1,0:T(8,128)S(1)}, u32[]{:S(2)}, u32[]{:S(2)}) collective-permute-start(f32[400,128]{1,0:T(8,128)} %get-tuple-element.54), channel_id=1, source_target_pairs={{0,1},{1,0},{2,3},{3,2},{4,5},{5,4},{6,7},{7,6},{8,9},{9,8},{10,11... | collective-permute-start | bytes 614408 | tf_op jit(solution)/shard_map/ppermute | solution.py:604
  13.6 7.3 %collective-permute-start.3 = (f32[400,128]{1,0:T(8,128)}, f32[400,128]{1,0:T(8,128)S(1)}, u32[]{:S(2)}, u32[]{:S(2)}) collective-permute-start(f32[400,128]{1,0:T(8,128)} %get-tuple-element.55), channel_id=1, source_target_pairs={{1,2},{2,1},{3,4},{4,3},{5,6},{6,5},{9,10},{10,9},{11,12},{12,11},... | collective-permute-start | bytes 614408 | tf_op jit(solution)/shard_map/ppermute | solution.py:604
  16.7 4.2 %copy-start.1 = (f32[400,128]{1,0:T(8,128)}, f32[400,128]{1,0:T(8,128)S(1)}, u32[]{:S(2)}) copy-start(f32[400,128]{1,0:T(8,128)S(1)} %collective-permute-done.2.rows_one) | copy-start | bytes 614404
  20.9 0.7 copy-start.2
  53.5 2.8 %collective-permute-start.4 = (f32[2,8,128]{2,1,0:T(8,128)}, f32[2,8,128]{2,1,0:T(8,128)S(1)}, u32[]{:S(2)}, u32[]{:S(2)}) collective-permute-start(f32[2,8,128]{2,1,0:T(8,128)} %get-tuple-element.69.own_one), channel_id=1, source_target_pairs={{0,8},{8,0},{16,24},{24,16},{1,9},{9,1},{17,25},{25,17},{2,10},{10... | collective-permute-start | bytes 24584 | tf_op jit(solution)/shard_map/ppermute | solution.py:604
  54.3 3.6 %collective-permute-start.5 = (f32[2,8,128]{2,1,0:T(8,128)}, f32[2,8,128]{2,1,0:T(8,128)S(1)}, u32[]{:S(2)}, u32[]{:S(2)}) collective-permute-start(f32[2,8,128]{2,1,0:T(8,128)} %get-tuple-element.70.own_two), channel_id=1, source_target_pairs={{0,24},{8,16},{16,8},{24,0},{1,25},{9,17},{17,9},{25,1},{2,26},{10... | collective-permute-start | bytes 24584 | tf_op jit(solution)/shard_map/ppermute | solution.py:604
  56.3 1.7 %copy-start.7 = (f32[2,8,128]{2,1,0:T(8,128)}, f32[2,8,128]{2,1,0:T(8,128)S(1)}, u32[]{:S(2)}) copy-start(f32[2,8,128]{2,1,0:T(8,128)S(1)} %collective-permute-done.4.cols_one) | copy-start | bytes 24580
  57.9 0.6 copy-start.8
  59.9 4.6 %collective-permute-start.6 = (f32[272,128]{1,0:T(8,128)}, f32[272,128]{1,0:T(8,128)S(1)}, u32[]{:S(2)}, u32[]{:S(2)}) collective-permute-start(f32[272,128]{1,0:T(8,128)} %get-tuple-element.73), channel_id=1, source_target_pairs={{0,1},{1,0},{2,3},{3,2},{4,5},{5,4},{6,7},{7,6},{8,9},{9,8},{10,11... | collective-permute-start | bytes 417800 | tf_op jit(solution)/shard_map/ppermute | solution.py:604
  60.0 7.4 %collective-permute-start.7 = (f32[272,128]{1,0:T(8,128)}, f32[272,128]{1,0:T(8,128)S(1)}, u32[]{:S(2)}, u32[]{:S(2)}) collective-permute-start(f32[272,128]{1,0:T(8,128)} %get-tuple-element.74), channel_id=1, source_target_pairs={{1,2},{2,1},{3,4},{4,3},{5,6},{6,5},{9,10},{10,9},{11,12},{12,11},... | collective-permute-start | bytes 417800 | tf_op jit(solution)/shard_map/ppermute | solution.py:604
  64.5 2.9 %copy-start.3 = (f32[272,128]{1,0:T(8,128)}, f32[272,128]{1,0:T(8,128)S(1)}, u32[]{:S(2)}) copy-start(f32[272,128]{1,0:T(8,128)S(1)} %collective-permute-done.6.rows_one) | copy-start | bytes 417796
  67.4 0.7 copy-start.4

commit v4 on v3

--- a/solution.py
+++ b/solution.py
@@ -75,10 +75,10 @@
 
 def pack_sides(tile, slot, packs):
     head, tail = packs
-    lane = lane_id()
-    here = (lane >= RIM * slot) & (lane < RIM * slot + RIM)
-    head = jnp.where(here, pltpu.roll(tile, RIM * slot, 1), head)
-    tail = jnp.where(here, pltpu.roll(tile, lax.rem(RIM * slot + RIM, COLS), 1), tail)
+    own = lane_id() // RIM
+    moved = pltpu.roll(tile, RIM * slot, 1)
+    head = jnp.where(own == slot, moved, head)
+    tail = jnp.where(own == lax.rem(slot + SLOTS - 1, SLOTS), moved, tail)
     return head, tail
 
 
@@ -123,6 +123,7 @@
 
     packs = each_level(levels, step, ((zero, zero),) * count, 8)
     for tile, (head, tail) in enumerate(packs):
+        tail = pltpu.roll(tail, RIM, 1)
         one_ref[tile] = jnp.where(even, tail, head)
         two_ref[tile] = jnp.where(even, head, tail)
 
@@ -140,9 +141,12 @@
         at += tiles
 
 
+def corner_rows(packed):
+    return pl.cdiv(2 * RIM * packed, ROWS) * ROWS
+
+
 def row_payload(fields, levels):
-    rows = RIM * fields * levels + 2 * RIM * packed_tiles(fields, levels)
-    return -(-rows // 16) * 16
+    return RIM * fields * levels + corner_rows(packed_tiles(fields, levels))
 
 
 def pack_kernel(levels, flags, tracers, winds, one, two, one_rows, two_rows):
@@ -163,27 +167,20 @@
     return jnp.where(even, one, two), jnp.where(even, two, one)
 
 
-def corner_kernel(one_in, two_in, flags, cols_one, cols_two, one, two, near, far, sems):
+def corner_kernel(one_in, two_in, flags, cols_one, cols_two, one, two):
     del one_in, two_in
-    near[...] = jnp.zeros(near.shape, jnp.float32)
-    far[...] = jnp.zeros(far.shape, jnp.float32)
     lon_even, lat_even = flags[LON_EVEN] > 0, flags[LAT_EVEN] > 0
     count = cols_one.shape[0]
+    base = one.shape[0] - corner_rows(count)
     for tile in range(count):
         for side, block in enumerate(in_order(lon_even, cols_one[tile], cols_two[tile])):
-            at = RIM * (side * count + tile)
+            at = base + RIM * (side * count + tile)
             head, tail = block[0:RIM], block[ROWS - RIM : ROWS]
-            near[at : at + RIM, :] = jnp.where(lat_even, tail, head)
-            far[at : at + RIM, :] = jnp.where(lat_even, head, tail)
-    base = one.shape[0] - near.shape[0]
-    copies = [
-        pltpu.make_async_copy(block, whole.at[pl.ds(base, near.shape[0])], sems.at[k])
-        for k, (block, whole) in enumerate(((near, one), (far, two)))
-    ]
-    for copy in copies:
-        copy.start()
-    for copy in copies:
-        copy.wait()
+            one[at : at + RIM, :] = jnp.where(lat_even, tail, head)
+            two[at : at + RIM, :] = jnp.where(lat_even, head, tail)
+    for at in range(base + 2 * RIM * count, one.shape[0], RIM):
+        one[at : at + RIM, :] = jnp.zeros((RIM, COLS), jnp.float32)
+        two[at : at + RIM, :] = jnp.zeros((RIM, COLS), jnp.float32)
 
 
 def unpack_rows(even, rows_one, rows_two, rim_ref, corner_ref, tiles, packed):
@@ -595,6 +592,14 @@
     return jax.ShapeDtypeStruct(shape, f32)
 
 
+def held(*shape, dtype=f32):
+    return pltpu.VMEM(shape, dtype)
+
+
+def near(*arrays):
+    return [pltpu.with_memory_space_constraint(x, pltpu.VMEM) for x in arrays]
+
+
 def swap_pairs(one, two, axis, ring):
     count = lax.axis_size(axis)
     near = [(i, i ^ 1) for i in range(count)]
@@ -604,19 +609,15 @@
     return lax.ppermute(one, axis, near), lax.ppermute(two, axis, far)
 
 
-def exchange_rows(one, two, flags, cols):
-    any_space = pl.BlockSpec(memory_space=pl.ANY)
-    spare = -(-2 * RIM * cols[0].shape[0] // 16) * 16
-    one, two = pl.pallas_call(
+def add_corners(one, two, flags, cols):
+    return pl.pallas_call(
         corner_kernel,
-        in_specs=[any_space] * 2 + [smem] + [vmem] * 2,
-        out_specs=[any_space] * 2,
-        out_shape=[tiles_like(*one.shape)] * 2,
+        in_specs=[vmem] * 2 + [smem] + [vmem] * 2,
+        out_specs=[vmem] * 2,
+        out_shape=[held(*one.shape)] * 2,
         input_output_aliases={0: 0, 1: 1},
-        scratch_shapes=[pltpu.VMEM((spare, COLS), f32)] * 2 + [pltpu.SemaphoreType.DMA((2,))],
         name="add_corners",
-    )(one, two, flags, *cols)
-    return swap_pairs(one, two, "lat", False)
+    )(*near(one, two), flags, *near(*cols))
 
 
 def body(
@@ -646,7 +647,7 @@
         raise ValueError("unsupported sizes")
 
     flat = (tracers.reshape(-1, COLS), winds.reshape(-1, COLS))
-    columns = tiles_like(packed_tiles(fields, levels), ROWS, COLS)
+    columns = held(packed_tiles(fields, levels), ROWS, COLS)
     lat, lats = lax.axis_index("lat"), lax.axis_size("lat")
     flags = [lat < lats - 1, lat > 0, lat % 2 == 0, lax.axis_index("lon") % 2 == 0]
     flags = jnp.stack(flags).astype(jnp.int32)
@@ -654,11 +655,14 @@
         functools.partial(pack_kernel, levels),
         in_specs=[smem] + [vmem] * 2,
         out_specs=[vmem] * 4,
-        out_shape=[columns] * 2 + [tiles_like(row_payload(fields, levels), COLS)] * 2,
+        out_shape=[columns] * 2 + [held(row_payload(fields, levels), COLS)] * 2,
         name="pack",
     )(flags, *flat)
     own = (one, two)
     cols = swap_pairs(one, two, "lon", True)
+
+    rows = add_corners(rows_one, rows_two, flags, cols)
+    rows, gases, sun_index = lax.optimization_barrier((rows, gases, sun_index))
 
     groups = bands // ROWS
     bf16 = jnp.bfloat16
@@ -667,15 +671,15 @@
         in_specs=[vmem, smem, vmem, smem] + [vmem] * 7,
         out_specs=[vmem] * 9,
         out_shape=[
-            jax.ShapeDtypeStruct((ROWS * hid, w_first.shape[0] * ROWS), bf16),
-            tiles_like(hid, COLS),
-            jax.ShapeDtypeStruct((hid, hid), bf16),
-            tiles_like(hid, COLS),
-            jax.ShapeDtypeStruct((bands, hid + 16), bf16),
-            tiles_like(groups, ROWS, COLS),
-            tiles_like(ROWS, ROWS, COLS),
-            tiles_like(ROWS, ROWS, COLS),
-            tiles_like(ROWS, COLS),
+            held(ROWS * hid, w_first.shape[0] * ROWS, dtype=bf16),
+            held(hid, COLS),
+            held(hid, hid, dtype=bf16),
+            held(hid, COLS),
+            held(bands, hid + 16, dtype=bf16),
+            held(groups, ROWS, COLS),
+            held(ROWS, ROWS, COLS),
+            held(ROWS, ROWS, COLS),
+            held(ROWS, COLS),
         ],
         scratch_shapes=[
             pltpu.VMEM((COLS, COLS), f32),
@@ -696,21 +700,17 @@
         b_third.reshape(1, -1),
     )
     gas_rows = gases.transpose(1, 0, 2, 3).reshape(levels, gas * ROWS, COLS)
-    cols, prepared, gas_rows = lax.optimization_barrier((cols, prepared, gas_rows))
-    rows = exchange_rows(rows_one, rows_two, flags, cols)
+    rows = swap_pairs(*rows, "lat", False)
 
     packed = packed_tiles(fields, levels)
     state, heating, one, two, rows_one, rows_two, face, side_face = pl.pallas_call(
         first_kernel,
         in_specs=[vmem] * 8 + [smem] + [vmem] * 10,
         out_specs=[vmem] * 8,
-        out_shape=[
-            tiles_like(ntr * levels * ROWS, COLS),
-            tiles_like(levels, ROWS, COLS),
-        ]
-        + [tiles_like(packed_tiles(ntr, levels), ROWS, COLS)] * 2
-        + [tiles_like(row_payload(ntr, levels), COLS)] * 2
-        + [tiles_like(levels, 6, ROWS, COLS), tiles_like(4, ROWS, COLS)],
+        out_shape=[held(ntr * levels * ROWS, COLS), tiles_like(levels, ROWS, COLS)]
+        + [held(packed_tiles(ntr, levels), ROWS, COLS)] * 2
+        + [held(row_payload(ntr, levels), COLS)] * 2
+        + [held(levels, 6, ROWS, COLS), held(4, ROWS, COLS)],
         scratch_shapes=[
             pltpu.VMEM((fields * levels * ROWS, COLS), f32),
             pltpu.VMEM((2 * packed, ROWS, COLS), f32),
@@ -728,12 +728,13 @@
             pltpu.VMEM((groups, ROWS, COLS), f32),
             pltpu.VMEM((ROWS, levels + 1, ROWS, COLS), f32),
         ],
+        compiler_params=pltpu.CompilerParams(vmem_limit_bytes=28 << 20),
         name="transport_radiation",
-    )(tracers, winds, *own, *cols, *rows, flags, gas_rows, *prepared)
+    )(*near(tracers, winds, *own, *cols, *rows), flags, *near(gas_rows, *prepared))
 
     own = (one, two)
     cols = swap_pairs(one, two, "lon", True)
-    rows = exchange_rows(rows_one, rows_two, flags, cols)
+    rows = swap_pairs(*add_corners(rows_one, rows_two, flags, cols), "lat", False)
     final = pl.pallas_call(
         last_kernel,
         in_specs=[vmem] * 9 + [smem],
@@ -744,8 +745,9 @@
             pltpu.VMEM((2 * packed_tiles(ntr, levels), ROWS, COLS), f32),
         ]
         + [pltpu.VMEM((packed_tiles(ntr, levels), ROWS, COLS), f32)] * 3,
+        compiler_params=pltpu.CompilerParams(vmem_limit_bytes=8 << 20),
         name="last_transport",
-    )(state, face, side_face, *own, *cols, *rows, flags)
+    )(*near(state, face, side_face, *own, *cols, *rows), flags)
     return final, heating
 
 

time: 73.7 us -> 66.1 us (0.90)
  Pallas kernels: 44.2 us -> 38.5 us
  local copies, waits for them, and re-layouts: 3.59 us -> 1.5 us
    pallas_call x1, Pallas kernels: 31.9 us -> 30 us  [body(): pl.pallas_call(first_kernel, in_specs=[vmem] * 8 + [smem] + [vmem] * 10,...]
    pallas_call x2, Pallas kernels: 2.71 us -> 1.35 us  [add_corners(): pl.pallas_call(corner_kernel, in_specs=[vmem] * 2 + [smem] + [vmem] * 2,...]
    unnamed x18 -> x10, local copies, waits for them, and re-layouts: 2.54 us -> 1.37 us
    reshape x1, local copies, waits for them, and re-layouts: 1.05 us -> 0.14 us  [body(): gas_rows = gases.transpose(1, 0, 2, 3).reshape(levels, gas * ROWS, COLS)]
    pallas_call x1, Pallas kernels: 5.23 us -> 4.34 us  [body(): pl.pallas_call(last_kernel, in_specs=[vmem] * 9 + [smem], out_specs=vmem,...]
    pallas_call x1, Pallas kernels: 2.56 us -> 1.73 us  [body(): pl.pallas_call(functools.partial(pack_kernel, levels), in_specs=[smem] +...]
  transfers between devices with their start and end apart: 8 -> 8, of which waited for: 4 -> 5; matrix products, arithmetic and copies ran while one was open for 1% -> 0% of each run, Pallas kernels for 2% -> 2%
where the time goes in v4:
time: 66.1 us; the launch traced here: 65.8 us
  Pallas kernels  38.5 us (58%)
  starting transfers between devices  15.5 us (23%)
  waiting for transfers between devices  8.82 us (13%)
  local copies, waits for them, and re-layouts  1.5 us (2%)
  between operations  0.77 us (1%)
  other arithmetic  0.67 us (1%)
    pallas_call x1, Pallas kernels, body(): pl.pallas_call(first_kernel, in_specs=[vmem] * 8 + [smem] + [vmem] * 10,...  30 us
    ppermute x8, starting transfers between devices, swap_pairs(): return (lax.ppermute(one, axis, near), lax.ppermute(two, axis, far))  15.5 us
    ppermute x8, waiting for transfers between devices, swap_pairs(): return (lax.ppermute(one, axis, near), lax.ppermute(two, axis, far))  8.82 us
    pallas_call x1, Pallas kernels, body(): pl.pallas_call(last_kernel, in_specs=[vmem] * 9 + [smem], out_specs=vmem,...  4.34 us
    pallas_call x1, Pallas kernels, body(): pl.pallas_call(functools.partial(pack_kernel, levels), in_specs=[smem] +...  1.73 us
    unnamed x10, local copies, waits for them, and re-layouts  1.37 us
    pallas_call x2, Pallas kernels, add_corners(): pl.pallas_call(corner_kernel, in_specs=[vmem] * 2 + [smem] + [vmem] * 2,...  1.35 us
  transfers between devices with their start and end apart: 8, of which 5 were waited for; matrix products, arithmetic and copies ran while one was open for 0% of the time, Pallas kernels for 2%

profile of v4, /device:TPU:1, one launch (start us, length us, event | category | flops | bytes accessed | tf_op | source)
XLA Modules:
  0.0 65.8 jit_solution(15395791970483868802)
XLA Ops:
  0.6 0.0 copy-start
  0.7 0.7 %add_convert_fusion.flags = s32[4]{0:T(128)} fusion(pred[1]{0:T(512)(128)(4,1)} %bitcast.3, pred[1]{0:T(512)(128)(4,1)} %bitcast.2, pred[1]{0:T(512)(128)(4,1)} %bitcast.1, pred[1]{0:T(512)(128)(4,1)} %bitcast), kind=kLoop, calls=%fused_computation.1 | loop fusion | flops 16 | bytes 20 | tf_op jit(solution)/shard_map/convert_element_type | solution.py:653
  1.3 1.7 %pack.1 = (f32[3,8,128]{2,1,0:T(8,128)S(1)}, f32[3,8,128]{2,1,0:T(8,128)S(1)}, f32[400,128]{1,0:T(8,128)S(1)}, f32[400,128]{1,0:T(8,128)S(1)}) custom-call(s32[4]{0:T(128)} %add_convert_fusion.flags, f32[1024,128]{1,0:T(8,128)} %bitcast.16, f32[512,128]{1,0:T(8,128)} %bitcast.17), custom_call_target="tpu_custom_call" | custom-call | tf_op jit(solution)/shard_map/pack/pallas_call | solution.py:654
  3.1 2.0 %collective-permute-start = (f32[3,8,128]{2,1,0:T(8,128)S(1)}, f32[3,8,128]{2,1,0:T(8,128)S(1)}, u32[]{:S(2)}, u32[]{:S(2)}) collective-permute-start(f32[3,8,128]{2,1,0:T(8,128)S(1)} %get-tuple-element.31.own_one), channel_id=1, source_target_pairs={{0,8},{8,0},{16,24},{24,16},{1,9},{9,1},{17,25},{25,17},{2,10},{10... | collective-permute-start | bytes 36872 | tf_op jit(solution)/shard_map/ppermute | solution.py:609
  5.1 1.2 %collective-permute-start.1 = (f32[3,8,128]{2,1,0:T(8,128)S(1)}, f32[3,8,128]{2,1,0:T(8,128)S(1)}, u32[]{:S(2)}, u32[]{:S(2)}) collective-permute-start(f32[3,8,128]{2,1,0:T(8,128)S(1)} %get-tuple-element.32.own_two), channel_id=1, source_target_pairs={{0,24},{8,16},{16,8},{24,0},{1,25},{9,17},{17,9},{25,1},{2,26},{10... | collective-permute-start | bytes 36872 | tf_op jit(solution)/shard_map/ppermute | solution.py:609
  6.3 0.0 collective-permute-done.cols_one
  6.3 2.3 %collective-permute-done.1.cols_two = f32[3,8,128]{2,1,0:T(8,128)S(1)} collective-permute-done((f32[3,8,128]{2,1,0:T(8,128)S(1)}, f32[3,8,128]{2,1,0:T(8,128)S(1)}, u32[]{:S(2)}, u32[]{:S(2)}) %collective-permute-start.1) | collective-permute-done | bytes 12320 | tf_op jit(solution)/shard_map/ppermute | solution.py:609
  8.7 0.7 %add_corners.2 = (f32[400,128]{1,0:T(8,128)S(1)}, f32[400,128]{1,0:T(8,128)S(1)}) custom-call(f32[400,128]{1,0:T(8,128)S(1)} %get-tuple-element.33.one_in, f32[400,128]{1,0:T(8,128)S(1)} %get-tuple-element.34.two_in, s32[4]{0:T(128)} %add_convert_fusion.flags, ...), custom_call_target="tpu_custom_call", output_to_operand_aliasing={{0}: (0, {}), {1}: (1, {})} | custom-call | tf_op jit(solution)/shard_map/add_corners/pallas_call | solution.py:613
  9.3 2.1 %collective-permute-start.2 = (f32[400,128]{1,0:T(8,128)S(1)}, f32[400,128]{1,0:T(8,128)S(1)}, u32[]{:S(2)}, u32[]{:S(2)}) collective-permute-start(f32[400,128]{1,0:T(8,128)S(1)} %get-tuple-element.37), channel_id=1, source_target_pairs={{0,1},{1,0},{2,3},{3,2},{4,5},{5,4},{6,7},{7,6},{8,9},{9,8},{10,11... | collective-permute-start | bytes 614408 | tf_op jit(solution)/shard_map/ppermute | solution.py:609
  11.4 3.1 %collective-permute-start.3 = (f32[400,128]{1,0:T(8,128)S(1)}, f32[400,128]{1,0:T(8,128)S(1)}, u32[]{:S(2)}, u32[]{:S(2)}) collective-permute-start(f32[400,128]{1,0:T(8,128)S(1)} %get-tuple-element.38), channel_id=1, source_target_pairs={{1,2},{2,1},{3,4},{4,3},{5,6},{6,5},{9,10},{10,9},{11,12},{12,11},... | collective-permute-start | bytes 614408 | tf_op jit(solution)/shard_map/ppermute | solution.py:609
  14.5 1.1 %prepare.1 = (bf16[512,128]{1,0:T(8,128)(2,1)S(1)}, f32[64,128]{1,0:T(8,128)S(1)}, bf16[64,64]{1,0:T(8,128)(2,1)S(1)}, f32[64,128]{1,0:T(8,128)S(1)}, bf16[224,8...) custom-call(s32[8,128]{1,0:T(8,128)} %index, ...), custom_call_target="tpu_custom_call" | custom-call | tf_op jit(solution)/shard_map/prepare/pallas_call | solution.py:669
  15.6 0.0 copy-done
  15.6 0.0 copy-start.1
  15.6 0.0 copy-start.2
  15.6 0.1 copy_bitcast_fusion.gases
  15.8 0.0 collective-permute-done.2.rows_one
  15.8 2.7 %collective-permute-done.3.rows_two = f32[400,128]{1,0:T(8,128)S(1)} collective-permute-done((f32[400,128]{1,0:T(8,128)S(1)}, f32[400,128]{1,0:T(8,128)S(1)}, u32[]{:S(2)}, u32[]{:S(2)}) %collective-permute-start.3) | collective-permute-done | bytes 204832 | tf_op jit(solution)/shard_map/ppermute | solution.py:609
  18.5 0.0 copy-done.1
  18.5 0.0 copy-done.2
  18.5 0.7 %copy-done.3 = s32[4]{0:T(128)S(1)} copy-done((s32[4]{0:T(128)S(1)}, s32[4]{0:T(128)}, u32[]{:S(2)}) %copy-start.3) | copy-done | bytes 40
  19.1 30.0 %transport_radiation.1 = (f32[1024,128]{1,0:T(8,128)S(1)}, f32[32,8,128]{2,1,0:T(8,128)}, f32[2,8,128]{2,1,0:T(8,128)S(1)}, f32[2,8,128]{2,1,0:T(8,128)S(1)}, f3...) custom-call(f32[4,32,8,128]{3,2,1,0:T(8,128)S(1)} %copy-done.1, ...), custom_call_target="tpu_custom_call" | custom-call | tf_op jit(solution)/shard_map/transport_radiation/pallas_call | solution.py:706
  49.1 0.0 collective-permute-start.4
  49.1 2.4 %collective-permute-start.5 = (f32[2,8,128]{2,1,0:T(8,128)S(1)}, f32[2,8,128]{2,1,0:T(8,128)S(1)}, u32[]{:S(2)}, u32[]{:S(2)}) collective-permute-start(f32[2,8,128]{2,1,0:T(8,128)S(1)} %get-tuple-element.54.own_two), channel_id=1, source_target_pairs={{0,24},{8,16},{16,8},{24,0},{1,25},{9,17},{17,9},{25,1},{2,26},{10... | collective-permute-start | bytes 24584 | tf_op jit(solution)/shard_map/ppermute | solution.py:609
  51.5 0.1 collective-permute-done.4.cols_one
  51.6 1.0 %collective-permute-done.5.cols_two = f32[2,8,128]{2,1,0:T(8,128)S(1)} collective-permute-done((f32[2,8,128]{2,1,0:T(8,128)S(1)}, f32[2,8,128]{2,1,0:T(8,128)S(1)}, u32[]{:S(2)}, u32[]{:S(2)}) %collective-permute-start.5) | collective-permute-done | bytes 8224 | tf_op jit(solution)/shard_map/ppermute | solution.py:609
  52.7 0.7 %add_corners.3 = (f32[264,128]{1,0:T(8,128)S(1)}, f32[264,128]{1,0:T(8,128)S(1)}) custom-call(f32[264,128]{1,0:T(8,128)S(1)} %get-tuple-element.55.one_in, f32[264,128]{1,0:T(8,128)S(1)} %get-tuple-element.56.two_in, s32[4]{0:T(128)} %add_convert_fusion.flags, ...), custom_call_target="tpu_custom_call", output_to_operand_aliasing={{0}: (0, {}), {1}: (1, {})} | custom-call | tf_op jit(solution)/shard_map/add_corners/pallas_call | solution.py:613
  53.3 0.1 collective-permute-start.6
  53.4 4.7 %collective-permute-start.7 = (f32[264,128]{1,0:T(8,128)S(1)}, f32[264,128]{1,0:T(8,128)S(1)}, u32[]{:S(2)}, u32[]{:S(2)}) collective-permute-start(f32[264,128]{1,0:T(8,128)S(1)} %get-tuple-element.58), channel_id=1, source_target_pairs={{1,2},{2,1},{3,4},{4,3},{5,6},{6,5},{9,10},{10,9},{11,12},{12,11},... | collective-permute-start | bytes 405512 | tf_op jit(solution)/shard_map/ppermute | solution.py:609
  58.1 0.0 collective-permute-done.6.rows_one
  58.1 2.7 %collective-permute-done.7.rows_two = f32[264,128]{1,0:T(8,128)S(1)} collective-permute-done((f32[264,128]{1,0:T(8,128)S(1)}, f32[264,128]{1,0:T(8,128)S(1)}, u32[]{:S(2)}, u32[]{:S(2)}) %collective-permute-start.7) | collective-permute-done | bytes 135200 | tf_op jit(solution)/shard_map/ppermute | solution.py:609
  60.8 0.7 %copy-done.4 = s32[4]{0:T(128)S(1)} copy-done((s32[4]{0:T(128)S(1)}, s32[4]{0:T(128)}, u32[]{:S(2)}) %copy-start.4) | copy-done | bytes 40
  61.4 4.3 %last_transport.1 = f32[4,32,8,128]{3,2,1,0:T(8,128)} custom-call(f32[1024,128]{1,0:T(8,128)S(1)} %get-tuple-element.50.tracers, f32[32,6,8,128]{3,2,1,0:T(8,128)S(1)} %get-tuple-element.51.face, f32[4,8,128]{2,1,0:T(8,128)S(1)} %get-tuple-element.52.side_face, f32[2,8,128]{2,1,0:T(8,128)S(1)} %get-tuple-element.53.own_one, ...), custom_call_target="tpu_custom_call" | custom-call | tf_op jit(solution)/shard_map/last_transport/pallas_call | solution.py:738
  (2 shorter events, 0.0 us)
Async XLA Ops:
  0.6 15.0 %copy-start = (bf16[12,32,8,128]{3,2,1,0:T(8,128)(2,1)S(1)}, bf16[12,32,8,128]{3,2,1,0:T(8,128)(2,1)}, u32[]{:S(2)}) copy-start(bf16[12,32,8,128]{3,2,1,0:T(8,128)(2,1)} %param.16) | copy-start | bytes 2359300
  3.1 3.2 %collective-permute-start = (f32[3,8,128]{2,1,0:T(8,128)S(1)}, f32[3,8,128]{2,1,0:T(8,128)S(1)}, u32[]{:S(2)}, u32[]{:S(2)}) collective-permute-start(f32[3,8,128]{2,1,0:T(8,128)S(1)} %get-tuple-element.31.own_one), channel_id=1, source_target_pairs={{0,8},{8,0},{16,24},{24,16},{1,9},{9,1},{17,25},{25,17},{2,10},{10... | collective-permute-start | bytes 36872 | tf_op jit(solution)/shard_map/ppermute | solution.py:609
  5.1 3.6 %collective-permute-start.1 = (f32[3,8,128]{2,1,0:T(8,128)S(1)}, f32[3,8,128]{2,1,0:T(8,128)S(1)}, u32[]{:S(2)}, u32[]{:S(2)}) collective-permute-start(f32[3,8,128]{2,1,0:T(8,128)S(1)} %get-tuple-element.32.own_two), channel_id=1, source_target_pairs={{0,24},{8,16},{16,8},{24,0},{1,25},{9,17},{17,9},{25,1},{2,26},{10... | collective-permute-start | bytes 36872 | tf_op jit(solution)/shard_map/ppermute | solution.py:609
  9.3 6.4 %collective-permute-start.2 = (f32[400,128]{1,0:T(8,128)S(1)}, f32[400,128]{1,0:T(8,128)S(1)}, u32[]{:S(2)}, u32[]{:S(2)}) collective-permute-start(f32[400,128]{1,0:T(8,128)S(1)} %get-tuple-element.37), channel_id=1, source_target_pairs={{0,1},{1,0},{2,3},{3,2},{4,5},{5,4},{6,7},{7,6},{8,9},{9,8},{10,11... | collective-permute-start | bytes 614408 | tf_op jit(solution)/shard_map/ppermute | solution.py:609
  11.4 7.1 %collective-permute-start.3 = (f32[400,128]{1,0:T(8,128)S(1)}, f32[400,128]{1,0:T(8,128)S(1)}, u32[]{:S(2)}, u32[]{:S(2)}) collective-permute-start(f32[400,128]{1,0:T(8,128)S(1)} %get-tuple-element.38), channel_id=1, source_target_pairs={{1,2},{2,1},{3,4},{4,3},{5,6},{6,5},{9,10},{10,9},{11,12},{12,11},... | collective-permute-start | bytes 614408 | tf_op jit(solution)/shard_map/ppermute | solution.py:609
  15.6 2.9 %copy-start.1 = (f32[4,32,8,128]{3,2,1,0:T(8,128)S(1)}, f32[4,32,8,128]{3,2,1,0:T(8,128)}, u32[]{:S(2)}) copy-start(f32[4,32,8,128]{3,2,1,0:T(8,128)} %tracers.1) | copy-start | bytes 1572868
  15.6 2.8 %copy-start.2 = (f32[2,32,8,128]{3,2,1,0:T(8,128)S(1)}, f32[2,32,8,128]{3,2,1,0:T(8,128)}, u32[]{:S(2)}) copy-start(f32[2,32,8,128]{3,2,1,0:T(8,128)} %winds.1) | copy-start | bytes 786436
  18.5 0.7 %copy-start.3 = (s32[4]{0:T(128)S(1)}, s32[4]{0:T(128)}, u32[]{:S(2)}) copy-start(s32[4]{0:T(128)} %add_convert_fusion.flags) | copy-start | bytes 52
  49.1 2.5 %collective-permute-start.4 = (f32[2,8,128]{2,1,0:T(8,128)S(1)}, f32[2,8,128]{2,1,0:T(8,128)S(1)}, u32[]{:S(2)}, u32[]{:S(2)}) collective-permute-start(f32[2,8,128]{2,1,0:T(8,128)S(1)} %get-tuple-element.53.own_one), channel_id=1, source_target_pairs={{0,8},{8,0},{16,24},{24,16},{1,9},{9,1},{17,25},{25,17},{2,10},{10... | collective-permute-start | bytes 24584 | tf_op jit(solution)/shard_map/ppermute | solution.py:609
  49.1 3.5 %collective-permute-start.5 = (f32[2,8,128]{2,1,0:T(8,128)S(1)}, f32[2,8,128]{2,1,0:T(8,128)S(1)}, u32[]{:S(2)}, u32[]{:S(2)}) collective-permute-start(f32[2,8,128]{2,1,0:T(8,128)S(1)} %get-tuple-element.54.own_two), channel_id=1, source_target_pairs={{0,24},{8,16},{16,8},{24,0},{1,25},{9,17},{17,9},{25,1},{2,26},{10... | collective-permute-start | bytes 24584 | tf_op jit(solution)/shard_map/ppermute | solution.py:609
  53.3 4.7 %collective-permute-start.6 = (f32[264,128]{1,0:T(8,128)S(1)}, f32[264,128]{1,0:T(8,128)S(1)}, u32[]{:S(2)}, u32[]{:S(2)}) collective-permute-start(f32[264,128]{1,0:T(8,128)S(1)} %get-tuple-element.57), channel_id=1, source_target_pairs={{0,1},{1,0},{2,3},{3,2},{4,5},{5,4},{6,7},{7,6},{8,9},{9,8},{10,11... | collective-permute-start | bytes 405512 | tf_op jit(solution)/shard_map/ppermute | solution.py:609
  53.4 7.3 %collective-permute-start.7 = (f32[264,128]{1,0:T(8,128)S(1)}, f32[264,128]{1,0:T(8,128)S(1)}, u32[]{:S(2)}, u32[]{:S(2)}) collective-permute-start(f32[264,128]{1,0:T(8,128)S(1)} %get-tuple-element.58), channel_id=1, source_target_pairs={{1,2},{2,1},{3,4},{4,3},{5,6},{6,5},{9,10},{10,9},{11,12},{12,11},... | collective-permute-start | bytes 405512 | tf_op jit(solution)/shard_map/ppermute | solution.py:609
  60.8 0.7 %copy-start.4 = (s32[4]{0:T(128)S(1)}, s32[4]{0:T(128)}, u32[]{:S(2)}) copy-start(s32[4]{0:T(128)} %add_convert_fusion.flags) | copy-start | bytes 52

commit v5 on v4

--- a/solution.py
+++ b/solution.py
@@ -19,6 +19,10 @@
 RIM = 2
 SLOTS = COLS // RIM
 HAS_AFTER, HAS_BEFORE, LAT_EVEN, LON_EVEN = range(4)
+
+
+def choose(flag, one, two):
+    return jnp.where(jnp.broadcast_to(flag, one.shape) > 0.0, one, two)
 
 
 def lane_id():
@@ -87,8 +91,8 @@
 
 
 def kept_rows(flags):
-    after = (row_id() == 0) & (flags[HAS_AFTER] > 0)
-    before = (row_id() == ROWS - 1) & (flags[HAS_BEFORE] > 0)
+    after = (row_id() == 0) & (flags[HAS_AFTER] > 0.0)
+    before = (row_id() == ROWS - 1) & (flags[HAS_BEFORE] > 0.0)
     return jnp.where(after | before, 1.0, 0.0)
 
 
@@ -124,8 +128,8 @@
     packs = each_level(levels, step, ((zero, zero),) * count, 8)
     for tile, (head, tail) in enumerate(packs):
         tail = pltpu.roll(tail, RIM, 1)
-        one_ref[tile] = jnp.where(even, tail, head)
-        two_ref[tile] = jnp.where(even, head, tail)
+        one_ref[tile] = choose(even, tail, head)
+        two_ref[tile] = choose(even, head, tail)
 
 
 def pack_rows(sources, even, one, two):
@@ -136,8 +140,8 @@
         for row in range(RIM):
             head = ref[pl.ds(row, tiles, stride=ROWS), :]
             tail = ref[pl.ds(ROWS - RIM + row, tiles, stride=ROWS), :]
-            one[pl.ds(row * total + at, tiles), :] = jnp.where(even, tail, head)
-            two[pl.ds(row * total + at, tiles), :] = jnp.where(even, head, tail)
+            one[pl.ds(row * total + at, tiles), :] = choose(even, tail, head)
+            two[pl.ds(row * total + at, tiles), :] = choose(even, head, tail)
         at += tiles
 
 
@@ -159,25 +163,25 @@
                     pl.ds(pl.multiple_of(base + level * ROWS, ROWS), ROWS), :
                 ]
             )
-    pack_rows((tracers, winds), flags[LAT_EVEN] > 0, one_rows, two_rows)
-    pack_fields(sources, levels, flags[LON_EVEN] > 0, one, two)
+    pack_rows((tracers, winds), flags[LAT_EVEN, 0:1], one_rows, two_rows)
+    pack_fields(sources, levels, flags[LON_EVEN, 0:1], one, two)
 
 
 def in_order(even, one, two):
-    return jnp.where(even, one, two), jnp.where(even, two, one)
+    return choose(even, one, two), choose(even, two, one)
 
 
 def corner_kernel(one_in, two_in, flags, cols_one, cols_two, one, two):
     del one_in, two_in
-    lon_even, lat_even = flags[LON_EVEN] > 0, flags[LAT_EVEN] > 0
+    lon_even, lat_even = flags[LON_EVEN, 0:1], flags[LAT_EVEN, 0:1]
     count = cols_one.shape[0]
     base = one.shape[0] - corner_rows(count)
     for tile in range(count):
         for side, block in enumerate(in_order(lon_even, cols_one[tile], cols_two[tile])):
             at = base + RIM * (side * count + tile)
             head, tail = block[0:RIM], block[ROWS - RIM : ROWS]
-            one[at : at + RIM, :] = jnp.where(lat_even, tail, head)
-            two[at : at + RIM, :] = jnp.where(lat_even, head, tail)
+            one[at : at + RIM, :] = choose(lat_even, tail, head)
+            two[at : at + RIM, :] = choose(lat_even, head, tail)
     for at in range(base + 2 * RIM * count, one.shape[0], RIM):
         one[at : at + RIM, :] = jnp.zeros((RIM, COLS), jnp.float32)
         two[at : at + RIM, :] = jnp.zeros((RIM, COLS), jnp.float32)
@@ -280,7 +284,7 @@
     packed = packed_tiles(fields, levels)
     groups = lsolar.shape[0]
     hid = b1.shape[0]
-    lon_even, lat_even = flags[LON_EVEN] > 0, flags[LAT_EVEN] > 0
+    lon_even, lat_even = flags[LON_EVEN, 0:1], flags[LAT_EVEN, 0:1]
     unpack_rows(lat_even, rows_one, rows_two, rim_ref, corner_ref, fields * levels, packed)
     keep = kept_rows(flags)
     sides = [
@@ -477,7 +481,7 @@
 ):
     ntr, levels = out.shape[0], out.shape[1]
     packed = packed_tiles(ntr, levels)
-    lon_even, lat_even = flags[LON_EVEN] > 0, flags[LAT_EVEN] > 0
+    lon_even, lat_even = flags[LON_EVEN, 0:1], flags[LAT_EVEN, 0:1]
     unpack_rows(lat_even, rows_one, rows_two, rim_ref, corner_ref, ntr * levels, packed)
     keep = kept_rows(flags)
     of_sides = [side_face[k] for k in range(4)]
@@ -612,12 +616,12 @@
 def add_corners(one, two, flags, cols):
     return pl.pallas_call(
         corner_kernel,
-        in_specs=[vmem] * 2 + [smem] + [vmem] * 2,
+        in_specs=[vmem] * 5,
         out_specs=[vmem] * 2,
         out_shape=[held(*one.shape)] * 2,
         input_output_aliases={0: 0, 1: 1},
         name="add_corners",
-    )(*near(one, two), flags, *near(*cols))
+    )(*near(one, two, flags, *cols))
 
 
 def body(
@@ -650,14 +654,15 @@
     columns = held(packed_tiles(fields, levels), ROWS, COLS)
     lat, lats = lax.axis_index("lat"), lax.axis_size("lat")
     flags = [lat < lats - 1, lat > 0, lat % 2 == 0, lax.axis_index("lon") % 2 == 0]
-    flags = jnp.stack(flags).astype(jnp.int32)
+    flags = jnp.stack(flags).astype(f32)[:, None, None]
+    flags = jnp.broadcast_to(flags, (4, ROWS, COLS))
     one, two, rows_one, rows_two = pl.pallas_call(
         functools.partial(pack_kernel, levels),
-        in_specs=[smem] + [vmem] * 2,
+        in_specs=[vmem] * 3,
         out_specs=[vmem] * 4,
         out_shape=[columns] * 2 + [held(row_payload(fields, levels), COLS)] * 2,
         name="pack",
-    )(flags, *flat)
+    )(*near(flags), *flat)
     own = (one, two)
     cols = swap_pairs(one, two, "lon", True)
 
@@ -705,7 +710,7 @@
     packed = packed_tiles(fields, levels)
     state, heating, one, two, rows_one, rows_two, face, side_face = pl.pallas_call(
         first_kernel,
-        in_specs=[vmem] * 8 + [smem] + [vmem] * 10,
+        in_specs=[vmem] * 19,
         out_specs=[vmem] * 8,
         out_shape=[held(ntr * levels * ROWS, COLS), tiles_like(levels, ROWS, COLS)]
         + [held(packed_tiles(ntr, levels), ROWS, COLS)] * 2
@@ -730,14 +735,14 @@
         ],
         compiler_params=pltpu.CompilerParams(vmem_limit_bytes=28 << 20),
         name="transport_radiation",
-    )(*near(tracers, winds, *own, *cols, *rows), flags, *near(gas_rows, *prepared))
+    )(*near(tracers, winds, *own, *cols, *rows, flags, gas_rows, *prepared))
 
     own = (one, two)
     cols = swap_pairs(one, two, "lon", True)
     rows = swap_pairs(*add_corners(rows_one, rows_two, flags, cols), "lat", False)
     final = pl.pallas_call(
         last_kernel,
-        in_specs=[vmem] * 9 + [smem],
+        in_specs=[vmem] * 10,
         out_specs=vmem,
         out_shape=tiles_like(ntr, levels, ROWS, COLS),
         scratch_shapes=[
@@ -747,7 +752,7 @@
         + [pltpu.VMEM((packed_tiles(ntr, levels), ROWS, COLS), f32)] * 3,
         compiler_params=pltpu.CompilerParams(vmem_limit_bytes=8 << 20),
         name="last_transport",
-    )(*near(state, face, side_face, *own, *cols, *rows), flags)
+    )(*near(state, face, side_face, *own, *cols, *rows, flags))
     return final, heating
 
 

time: 66.1 us -> 61.7 us (0.933)
  Pallas kernels: 38.5 us -> 36.1 us
  local copies, waits for them, and re-layouts: 1.5 us -> 0.23 us
    pallas_call x5, Pallas kernels: 37.4 us -> 35 us  [the longest x1 29.4 us: body(): pl.pallas_call(first_kernel, in_specs=[vmem] * 19, out_specs=[vmem] * 8,...]
    unnamed x10 -> x6, local copies, waits for them, and re-layouts: 1.37 us -> 0.02 us
where the time goes in v5:
time: 61.7 us; the launch traced here: 61.5 us
  Pallas kernels  36.1 us (59%)
  starting transfers between devices  15.5 us (25%)
  waiting for transfers between devices  8.82 us (14%)
  between operations  0.75 us (1%)
    pallas_call x1, Pallas kernels, body(): pl.pallas_call(first_kernel, in_specs=[vmem] * 19, out_specs=[vmem] * 8,...  29.4 us
    ppermute x8, starting transfers between devices, swap_pairs(): return (lax.ppermute(one, axis, near), lax.ppermute(two, axis, far))  15.5 us
    ppermute x8, waiting for transfers between devices, swap_pairs(): return (lax.ppermute(one, axis, near), lax.ppermute(two, axis, far))  8.82 us
    pallas_call x1, Pallas kernels, body(): pl.pallas_call(last_kernel, in_specs=[vmem] * 10, out_specs=vmem, out_sha...  3.81 us
    pallas_call x1, Pallas kernels, body(): pl.pallas_call(functools.partial(pack_kernel, levels), in_specs=[vmem] *...  1.76 us
  transfers between devices with their start and end apart: 8, of which 5 were waited for; matrix products, arithmetic and copies ran while one was open for 0% of the time, Pallas kernels for 2%

profile of v5, /device:TPU:1, one launch (start us, length us, event | category | flops | bytes accessed | tf_op | source)
XLA Modules:
  0.0 61.5 jit_solution(5431848542848925183)
XLA Ops:
  0.6 0.0 copy-start
  0.7 0.1 add_convert_fusion
  0.7 0.1 broadcast_in_dim.2.flags
  0.8 1.8 %pack.1 = (f32[3,8,128]{2,1,0:T(8,128)S(1)}, f32[3,8,128]{2,1,0:T(8,128)S(1)}, f32[400,128]{1,0:T(8,128)S(1)}, f32[400,128]{1,0:T(8,128)S(1)}) custom-call(f32[4,8,128]{2,1,0:T(8,128)S(1)} %broadcast_in_dim.2.flags, f32[1024,128]{1,0:T(8,128)} %bitcast.16, f32[512,128]{1,0:T(8,128)} %bitcast.17), custom_call_target="tpu_custom_call" | custom-call | tf_op jit(solution)/shard_map/pack/pallas_call | solution.py:659
  2.6 2.0 %collective-permute-start = (f32[3,8,128]{2,1,0:T(8,128)S(1)}, f32[3,8,128]{2,1,0:T(8,128)S(1)}, u32[]{:S(2)}, u32[]{:S(2)}) collective-permute-start(f32[3,8,128]{2,1,0:T(8,128)S(1)} %get-tuple-element.31.own_one), channel_id=1, source_target_pairs={{0,8},{8,0},{16,24},{24,16},{1,9},{9,1},{17,25},{25,17},{2,10},{10... | collective-permute-start | bytes 36872 | tf_op jit(solution)/shard_map/ppermute | solution.py:613
  4.6 1.2 %collective-permute-start.1 = (f32[3,8,128]{2,1,0:T(8,128)S(1)}, f32[3,8,128]{2,1,0:T(8,128)S(1)}, u32[]{:S(2)}, u32[]{:S(2)}) collective-permute-start(f32[3,8,128]{2,1,0:T(8,128)S(1)} %get-tuple-element.32.own_two), channel_id=1, source_target_pairs={{0,24},{8,16},{16,8},{24,0},{1,25},{9,17},{17,9},{25,1},{2,26},{10... | collective-permute-start | bytes 36872 | tf_op jit(solution)/shard_map/ppermute | solution.py:613
  5.8 0.0 collective-permute-done.cols_one
  5.8 2.3 %collective-permute-done.1.cols_two = f32[3,8,128]{2,1,0:T(8,128)S(1)} collective-permute-done((f32[3,8,128]{2,1,0:T(8,128)S(1)}, f32[3,8,128]{2,1,0:T(8,128)S(1)}, u32[]{:S(2)}, u32[]{:S(2)}) %collective-permute-start.1) | collective-permute-done | bytes 12320 | tf_op jit(solution)/shard_map/ppermute | solution.py:613
  8.2 2.1 %collective-permute-start.2 = (f32[400,128]{1,0:T(8,128)S(1)}, f32[400,128]{1,0:T(8,128)S(1)}, u32[]{:S(2)}, u32[]{:S(2)}) collective-permute-start(f32[400,128]{1,0:T(8,128)S(1)} %get-tuple-element.37), channel_id=1, source_target_pairs={{0,1},{1,0},{2,3},{3,2},{4,5},{5,4},{6,7},{7,6},{8,9},{9,8},{10,11... | collective-permute-start | bytes 614408 | tf_op jit(solution)/shard_map/ppermute | solution.py:613
  10.2 3.1 %collective-permute-start.3 = (f32[400,128]{1,0:T(8,128)S(1)}, f32[400,128]{1,0:T(8,128)S(1)}, u32[]{:S(2)}, u32[]{:S(2)}) collective-permute-start(f32[400,128]{1,0:T(8,128)S(1)} %get-tuple-element.38), channel_id=1, source_target_pairs={{1,2},{2,1},{3,4},{4,3},{5,6},{6,5},{9,10},{10,9},{11,12},{12,11},... | collective-permute-start | bytes 614408 | tf_op jit(solution)/shard_map/ppermute | solution.py:613
  13.4 1.1 %prepare.1 = (bf16[512,128]{1,0:T(8,128)(2,1)S(1)}, f32[64,128]{1,0:T(8,128)S(1)}, bf16[64,64]{1,0:T(8,128)(2,1)S(1)}, f32[64,128]{1,0:T(8,128)S(1)}, bf16[224,8...) custom-call(s32[8,128]{1,0:T(8,128)} %index, ...), custom_call_target="tpu_custom_call" | custom-call | tf_op jit(solution)/shard_map/prepare/pallas_call | solution.py:674
  14.4 0.0 copy-done
  14.5 0.0 copy-start.1
  14.5 0.0 copy-start.2
  14.5 0.1 copy_bitcast_fusion.gases
  14.6 0.0 collective-permute-done.2.rows_one
  14.6 2.7 %collective-permute-done.3.rows_two = f32[400,128]{1,0:T(8,128)S(1)} collective-permute-done((f32[400,128]{1,0:T(8,128)S(1)}, f32[400,128]{1,0:T(8,128)S(1)}, u32[]{:S(2)}, u32[]{:S(2)}) %collective-permute-start.3) | collective-permute-done | bytes 204832 | tf_op jit(solution)/shard_map/ppermute | solution.py:613
  17.3 0.0 copy-done.1
  17.3 0.0 copy-done.2
  17.3 29.4 %transport_radiation.1 = (f32[1024,128]{1,0:T(8,128)S(1)}, f32[32,8,128]{2,1,0:T(8,128)}, f32[2,8,128]{2,1,0:T(8,128)S(1)}, f32[2,8,128]{2,1,0:T(8,128)S(1)}, f3...) custom-call(f32[4,32,8,128]{3,2,1,0:T(8,128)S(1)} %copy-done.1, ...), custom_call_target="tpu_custom_call" | custom-call | tf_op jit(solution)/shard_map/transport_radiation/pallas_call | solution.py:711
  46.8 0.0 collective-permute-start.4
  46.8 2.4 %collective-permute-start.5 = (f32[2,8,128]{2,1,0:T(8,128)S(1)}, f32[2,8,128]{2,1,0:T(8,128)S(1)}, u32[]{:S(2)}, u32[]{:S(2)}) collective-permute-start(f32[2,8,128]{2,1,0:T(8,128)S(1)} %get-tuple-element.54.own_two), channel_id=1, source_target_pairs={{0,24},{8,16},{16,8},{24,0},{1,25},{9,17},{17,9},{25,1},{2,26},{10... | collective-permute-start | bytes 24584 | tf_op jit(solution)/shard_map/ppermute | solution.py:613
  49.2 0.1 collective-permute-done.4.cols_one
  49.3 1.0 %collective-permute-done.5.cols_two = f32[2,8,128]{2,1,0:T(8,128)S(1)} collective-permute-done((f32[2,8,128]{2,1,0:T(8,128)S(1)}, f32[2,8,128]{2,1,0:T(8,128)S(1)}, u32[]{:S(2)}, u32[]{:S(2)}) %collective-permute-start.5) | collective-permute-done | bytes 8224 | tf_op jit(solution)/shard_map/ppermute | solution.py:613
  50.3 0.0 collective-permute-start.6
  50.3 4.7 %collective-permute-start.7 = (f32[264,128]{1,0:T(8,128)S(1)}, f32[264,128]{1,0:T(8,128)S(1)}, u32[]{:S(2)}, u32[]{:S(2)}) collective-permute-start(f32[264,128]{1,0:T(8,128)S(1)} %get-tuple-element.58), channel_id=1, source_target_pairs={{1,2},{2,1},{3,4},{4,3},{5,6},{6,5},{9,10},{10,9},{11,12},{12,11},... | collective-permute-start | bytes 405512 | tf_op jit(solution)/shard_map/ppermute | solution.py:613
  55.0 0.0 collective-permute-done.6.rows_one
  55.0 2.7 %collective-permute-done.7.rows_two = f32[264,128]{1,0:T(8,128)S(1)} collective-permute-done((f32[264,128]{1,0:T(8,128)S(1)}, f32[264,128]{1,0:T(8,128)S(1)}, u32[]{:S(2)}, u32[]{:S(2)}) %collective-permute-start.7) | collective-permute-done | bytes 135200 | tf_op jit(solution)/shard_map/ppermute | solution.py:613
  57.6 3.8 %last_transport.1 = f32[4,32,8,128]{3,2,1,0:T(8,128)} custom-call(f32[1024,128]{1,0:T(8,128)S(1)} %get-tuple-element.50.tracers, f32[32,6,8,128]{3,2,1,0:T(8,128)S(1)} %get-tuple-element.51.face, f32[4,8,128]{2,1,0:T(8,128)S(1)} %get-tuple-element.52.side_face, f32[2,8,128]{2,1,0:T(8,128)S(1)} %get-tuple-element.53.own_one, ...), custom_call_target="tpu_custom_call" | custom-call | tf_op jit(solution)/shard_map/last_transport/pallas_call | solution.py:743
  (2 shorter events, 0.0 us)
Async XLA Ops:
  0.6 13.8 %copy-start = (bf16[12,32,8,128]{3,2,1,0:T(8,128)(2,1)S(1)}, bf16[12,32,8,128]{3,2,1,0:T(8,128)(2,1)}, u32[]{:S(2)}) copy-start(bf16[12,32,8,128]{3,2,1,0:T(8,128)(2,1)} %param.16) | copy-start | bytes 2359300
  2.6 3.2 %collective-permute-start = (f32[3,8,128]{2,1,0:T(8,128)S(1)}, f32[3,8,128]{2,1,0:T(8,128)S(1)}, u32[]{:S(2)}, u32[]{:S(2)}) collective-permute-start(f32[3,8,128]{2,1,0:T(8,128)S(1)} %get-tuple-element.31.own_one), channel_id=1, source_target_pairs={{0,8},{8,0},{16,24},{24,16},{1,9},{9,1},{17,25},{25,17},{2,10},{10... | collective-permute-start | bytes 36872 | tf_op jit(solution)/shard_map/ppermute | solution.py:613
  4.6 3.6 %collective-permute-start.1 = (f32[3,8,128]{2,1,0:T(8,128)S(1)}, f32[3,8,128]{2,1,0:T(8,128)S(1)}, u32[]{:S(2)}, u32[]{:S(2)}) collective-permute-start(f32[3,8,128]{2,1,0:T(8,128)S(1)} %get-tuple-element.32.own_two), channel_id=1, source_target_pairs={{0,24},{8,16},{16,8},{24,0},{1,25},{9,17},{17,9},{25,1},{2,26},{10... | collective-permute-start | bytes 36872 | tf_op jit(solution)/shard_map/ppermute | solution.py:613
  8.2 6.4 %collective-permute-start.2 = (f32[400,128]{1,0:T(8,128)S(1)}, f32[400,128]{1,0:T(8,128)S(1)}, u32[]{:S(2)}, u32[]{:S(2)}) collective-permute-start(f32[400,128]{1,0:T(8,128)S(1)} %get-tuple-element.37), channel_id=1, source_target_pairs={{0,1},{1,0},{2,3},{3,2},{4,5},{5,4},{6,7},{7,6},{8,9},{9,8},{10,11... | collective-permute-start | bytes 614408 | tf_op jit(solution)/shard_map/ppermute | solution.py:613
  10.2 7.1 %collective-permute-start.3 = (f32[400,128]{1,0:T(8,128)S(1)}, f32[400,128]{1,0:T(8,128)S(1)}, u32[]{:S(2)}, u32[]{:S(2)}) collective-permute-start(f32[400,128]{1,0:T(8,128)S(1)} %get-tuple-element.38), channel_id=1, source_target_pairs={{1,2},{2,1},{3,4},{4,3},{5,6},{6,5},{9,10},{10,9},{11,12},{12,11},... | collective-permute-start | bytes 614408 | tf_op jit(solution)/shard_map/ppermute | solution.py:613
  14.5 2.9 %copy-start.1 = (f32[4,32,8,128]{3,2,1,0:T(8,128)S(1)}, f32[4,32,8,128]{3,2,1,0:T(8,128)}, u32[]{:S(2)}) copy-start(f32[4,32,8,128]{3,2,1,0:T(8,128)} %tracers.1) | copy-start | bytes 1572868
  14.5 2.8 %copy-start.2 = (f32[2,32,8,128]{3,2,1,0:T(8,128)S(1)}, f32[2,32,8,128]{3,2,1,0:T(8,128)}, u32[]{:S(2)}) copy-start(f32[2,32,8,128]{3,2,1,0:T(8,128)} %winds.1) | copy-start | bytes 786436
  46.8 2.5 %collective-permute-start.4 = (f32[2,8,128]{2,1,0:T(8,128)S(1)}, f32[2,8,128]{2,1,0:T(8,128)S(1)}, u32[]{:S(2)}, u32[]{:S(2)}) collective-permute-start(f32[2,8,128]{2,1,0:T(8,128)S(1)} %get-tuple-element.53.own_one), channel_id=1, source_target_pairs={{0,8},{8,0},{16,24},{24,16},{1,9},{9,1},{17,25},{25,17},{2,10},{10... | collective-permute-start | bytes 24584 | tf_op jit(solution)/shard_map/ppermute | solution.py:613
  46.8 3.5 %collective-permute-start.5 = (f32[2,8,128]{2,1,0:T(8,128)S(1)}, f32[2,8,128]{2,1,0:T(8,128)S(1)}, u32[]{:S(2)}, u32[]{:S(2)}) collective-permute-start(f32[2,8,128]{2,1,0:T(8,128)S(1)} %get-tuple-element.54.own_two), channel_id=1, source_target_pairs={{0,24},{8,16},{16,8},{24,0},{1,25},{9,17},{17,9},{25,1},{2,26},{10... | collective-permute-start | bytes 24584 | tf_op jit(solution)/shard_map/ppermute | solution.py:613
  50.3 4.7 %collective-permute-start.6 = (f32[264,128]{1,0:T(8,128)S(1)}, f32[264,128]{1,0:T(8,128)S(1)}, u32[]{:S(2)}, u32[]{:S(2)}) collective-permute-start(f32[264,128]{1,0:T(8,128)S(1)} %get-tuple-element.57), channel_id=1, source_target_pairs={{0,1},{1,0},{2,3},{3,2},{4,5},{5,4},{6,7},{7,6},{8,9},{9,8},{10,11... | collective-permute-start | bytes 405512 | tf_op jit(solution)/shard_map/ppermute | solution.py:613
  50.3 7.3 %collective-permute-start.7 = (f32[264,128]{1,0:T(8,128)S(1)}, f32[264,128]{1,0:T(8,128)S(1)}, u32[]{:S(2)}, u32[]{:S(2)}) collective-permute-start(f32[264,128]{1,0:T(8,128)S(1)} %get-tuple-element.58), channel_id=1, source_target_pairs={{1,2},{2,1},{3,4},{4,3},{5,6},{6,5},{9,10},{10,9},{11,12},{12,11},... | collective-permute-start | bytes 405512 | tf_op jit(solution)/shard_map/ppermute | solution.py:613
